TPU v7x, 256 devices: a whole 4x4x8 slice. The times are simulated.
256 devices in a mesh: gx: 32 (over z, y), gy: 8 (over x, core).
Axes of the slice: x: 4, y: 4, z: 8, core: 2. Of those that a mesh axis runs over, the one named last changes fastest.
Arguments:
- populations: float32 [19, 256, 512, 128], P(None, 'gx', 'gy'), may hold values from 0.5 to 2
- solid_flags: int32 [256, 512, 128], P('gx', 'gy'), may hold values 0 or 1
- point_cells: int32 [3, 4608], replicated, may hold values from 0 to 511, as said below
- point_turbine: int32 [4608], replicated, may hold values from 0 to 23, as said below
- blade_speed: float32 [3, 4608], replicated, may hold values from -0.3 to 0.3
- chord: float32 [4608], replicated, may hold values from 0.3 to 3
- turbine_gain: float32 [24], replicated, may hold values from 0.5 to 2
Outputs:
- read: float32 [19, 256, 512, 128], P(None, 'gx', 'gy')
- point_force: float32 [3, 4608], replicated
Inputs may be any that keep to these rules, and one draw needn't show every extreme that they name: `point_cells`: row 0 and row 1 are a point's streamwise and spanwise cell, row 2 its height, which lies in [4, 124]; all points of one turbine share the streamwise cell. `point_turbine`: each turbine has exactly 192 points.
All inputs are finite; a program needn't handle non-finite values. No bound on the sum of `solid_flags` on one device may be relied on, other than what follows from the above.
Results may differ from a plain program's by a relative error of at most 0.00007.
Values sent between devices are 32-bit elements; how exact they have to be, the bound alone decides.
No kernel may reach another device: no remote copies, remote signals or barrier semaphores. Data moves between devices by JAX's collectives and lax.ppermute only.
A program may use at most 128 MiB of HBM per device.

v0:
```python
import functools

import jax
import jax.numpy as jnp
from jax import lax
from jax.experimental import pallas as pl
from jax.experimental.pallas import tpu as pltpu
from jax.sharding import PartitionSpec as P


SMEAR = 3
RELAX = 0.8
SCALE = 1.5
CHUNK = 256
LANES = 128
DIRS = [
    (0, 0, 0),
    (1, 0, 0),
    (-1, 0, 0),
    (0, 1, 0),
    (0, -1, 0),
    (0, 0, 1),
    (0, 0, -1),
    (1, 1, 0),
    (-1, -1, 0),
    (1, -1, 0),
    (-1, 1, 0),
    (1, 0, 1),
    (-1, 0, -1),
    (1, 0, -1),
    (-1, 0, 1),
    (0, 1, 1),
    (0, -1, -1),
    (0, 1, -1),
    (0, -1, 1),
]
OPP = [0, 2, 1, 4, 3, 6, 5, 8, 7, 10, 9, 12, 11, 14, 13, 16, 15, 18, 17]
EAST = [i for i in range(19) if DIRS[i][0] == 1]
WEST = [i for i in range(19) if DIRS[i][0] == -1]
NORTH = [i for i in range(19) if DIRS[i][1] == 1]
SOUTH = [i for i in range(19) if DIRS[i][1] == -1]
CX, CY = 8, 64
F32, BF16 = jnp.float32, jnp.bfloat16
FORCE_FLOPS = 40_000_000
STEP_FLOPS = 60_000_000
HBM = pl.BlockSpec(memory_space=pltpu.HBM)
VMEM = pl.BlockSpec(memory_space=pltpu.VMEM)
NT = (((1,), (1,)), ((), ()))
NN = (((1,), (0,)), ((), ()))


def dot(a, b, dims=NN):
    return lax.dot_general(a, b, dims, preferred_element_type=F32)


def split3(v):
    high = v.astype(BF16)
    rest = v - high.astype(F32)
    mid = rest.astype(BF16)
    low = (rest - mid.astype(F32)).astype(BF16)
    return high, mid, low


def moments(g):
    s = [None] * 19
    d = [None] * 19
    for k in range(1, 19, 2):
        s[k] = g[k] + g[k + 1]
        d[k] = g[k] - g[k + 1]
    w1, w2 = 1.0 / 18.0, 1.0 / 36.0
    rho = (
        g[0] * (1.0 / 3.0)
        + (s[1] + s[3] + s[5]) * w1
        + ((s[7] + s[9]) + (s[11] + s[13]) + (s[15] + s[17])) * w2
    )
    mx = d[1] * w1 + ((d[7] + d[9]) + (d[11] + d[13])) * w2
    my = d[3] * w1 + ((d[7] - d[9]) + (d[15] + d[17])) * w2
    mz = d[5] * w1 + ((d[11] - d[13]) + (d[15] - d[17])) * w2
    return rho, (mx, my, mz)


def along(c, v):
    total = None
    for comp, part in zip(c, v):
        if comp == 0:
            continue
        if total is None:
            total = part if comp > 0 else -part
        else:
            total = total + part if comp > 0 else total - part
    return total


class Collision:
    def __init__(self, rho, mom, force):
        inv = 1.0 / rho
        amp = 1.0 - 0.5 / RELAX
        vel = [(m + 0.5 * f) * inv for m, f in zip(mom, force)]
        usq = vel[0] * vel[0] + vel[1] * vel[1] + vel[2] * vel[2]
        uf = vel[0] * force[0] + vel[1] * force[1] + vel[2] * force[2]
        heavy = rho * (1.0 / RELAX)
        self.base = heavy - 1.5 * heavy * usq - 3.0 * amp * uf
        self.vel = vel
        rho3, rho45 = 3.0 * heavy, 4.5 * heavy
        self.odd_vec = [rho3 * u + (3.0 * amp) * f for u, f in zip(vel, force)]
        self.even_vec = [rho45 * u + (9.0 * amp) * f for u, f in zip(vel, force)]

    def terms(self, k):
        if k == 0:
            return self.base, None
        c = DIRS[k]
        return self.base + along(c, self.vel) * along(c, self.even_vec), along(c, self.odd_vec)

    def one(self, k):
        first = k if k % 2 == 1 else k - 1
        even, odd = self.terms(first)
        return even + odd if first == k else even - odd


KEEP = 1.0 - 1.0 / RELAX


def sample_kernel(
    gain_hbm, pops_hbm, flags_hbm, cells_hbm, turb_hbm, chord_hbm, blade_hbm,
    sibling, across, east, west, pops,
    vh, vm, vl, sel, fld, m128, r128, dense, got_ref,
    gain, flags, cells, turb, chord, blade, sems, in_sems,
):
    small = [
        pltpu.make_async_copy(src, dst, in_sems.at[k])
        for k, (src, dst) in enumerate(
            (
                (cells_hbm, cells),
                (turb_hbm, turb.at[0]),
                (chord_hbm, chord.at[0]),
                (blade_hbm, blade),
                (gain_hbm, gain),
                (flags_hbm, flags),
            )
        )
    ]
    for copy in small:
        copy.start()
    for x in range(CX):
        pltpu.make_async_copy(pops_hbm.at[:, x], pops.at[:, x], sems.at[x]).start()
    points = cells.shape[1]
    tiles = points // LANES
    start_x, start_y = lax.axis_index("gx") * CX, lax.axis_index("gy") * CY
    even = lax.axis_index("gy") % 2 == 0
    for copy in small[:5]:
        copy.wait()
    px = cells[0:1, :] - start_x
    py = cells[1:2, :] - start_y
    own = (px >= 0) & (px < CX) & (py >= 0) & (py < CY)
    own = jnp.where(own, 1.0, 0.0)
    m128[...] = jnp.zeros_like(m128)
    for j in range(tiles):
        m128[j : j + 1, :] = own[:, j * LANES : (j + 1) * LANES]
    mask = m128[...]
    maskb = mask.astype(BF16)
    rows = lax.broadcasted_iota(jnp.int32, (LANES, LANES), 0)
    cols = lax.broadcasted_iota(jnp.int32, (LANES, LANES), 1)
    before = jnp.where(rows < cols, 1.0, 0.0).astype(BF16)
    above = jnp.where(rows > cols, 1.0, 0.0).astype(BF16)
    inside = dot(maskb, before)
    ahead = jnp.sum(dot(above, maskb), axis=1, keepdims=True)
    r128[...] = jnp.where(mask > 0.0, inside + ahead, -1.0)
    count = jnp.sum(mask).astype(jnp.int32)

    fld[0:1, :] = px.astype(F32)
    fld[1:2, :] = py.astype(F32)
    fld[2:3, :] = cells[2:3, :].astype(F32)
    fld[3:4, :] = turb[...].astype(F32)
    ch = split3(chord[...])
    bl = split3(blade[...])
    for k in range(3):
        fld[4 + k : 5 + k, :] = ch[k].astype(F32)
        fld[7 + 3 * k : 10 + 3 * k, :] = bl[k].astype(F32)
    dense[...] = jnp.zeros_like(dense)
    spots = lax.broadcasted_iota(jnp.int32, (CHUNK, LANES), 0).astype(F32)

    def choose(turn):
        base = (turn * CHUNK).astype(F32) if not isinstance(turn, int) else 0.0
        for j in range(tiles):
            hit = r128[j : j + 1, :] - base == spots
            sel[:, j * LANES : (j + 1) * LANES] = jnp.where(hit, 1.0, 0.0).astype(BF16)
        got_ref[...] = dot(fld[...].astype(BF16), sel[...], NT)

    @pl.when(count > 0)
    def _():
        choose(0)

    small[5].wait()

    def plane(x, carry):
        pltpu.make_async_copy(pops_hbm.at[:, x], pops.at[:, x], sems.at[x]).wait()
        for yb in range(CY // 16):
            g = [pops[i, x, yb * 16 : yb * 16 + 16, :] for i in range(19)]
            rho, mom = moments(g)
            for c in range(3):
                at = pl.multiple_of(c * CX * CY + x * CY + yb * 16, 16)
                high, mid, low = split3(mom[c] / rho)
                vh[pl.ds(at, 16), :] = high
                vm[pl.ds(at, 16), :] = mid
                vl[pl.ds(at, 16), :] = low
        return carry

    lax.fori_loop(0, CX, plane, 0)

    def pack(ids, g, flag):
        rho, mom = moments(g)
        solid = flag != 0
        held = [jnp.where(solid, g[OPP[i]], g[i]) for i in ids]
        return held + [rho, *mom, flag.astype(F32)]

    for ids, x, out in ((EAST, CX - 1, east), (WEST, 0, west)):
        for yb in range(CY // 8):
            at = slice(yb * 8, yb * 8 + 8)
            parts = pack(ids, [pops[i, x, at, :] for i in range(19)], flags[x, at, :])
            for k, part in enumerate(parts):
                out[k, at, :] = part
    up = pack(NORTH, [pops[i, :, CY - 1, :] for i in range(19)], flags[:, CY - 1, :])
    down = pack(SOUTH, [pops[i, :, 0, :] for i in range(19)], flags[:, 0, :])
    for k, (a, b) in enumerate(zip(up, down)):
        sibling[112 + 8 * k : 120 + 8 * k, :] = jnp.where(even, a, b)
        across[112 + 8 * k : 120 + 8 * k, :] = jnp.where(even, b, a)

    levels = lax.broadcasted_iota(jnp.int32, (LANES, CHUNK), 0).astype(F32)
    cell_ids = lax.broadcasted_iota(jnp.int32, (CX * CY, CHUNK), 0).astype(F32)

    def chunk(turn, carry):
        @pl.when(turn > 0)
        def _():
            choose(turn)

        got = got_ref[...]
        cell = got[0:1] * CY + got[1:2]
        onez = jnp.where(levels == got[2:3], 1.0, 0.0).astype(BF16)
        factor = jnp.zeros((1, CHUNK), F32)
        for t in range(gain.shape[0]):
            factor = jnp.where(got[3:4] == t, gain[t], factor)
        factor = factor * (got[4:5] + got[5:6] + got[6:7])
        rel = []
        for c in range(3):
            at = slice(c * CX * CY, (c + 1) * CX * CY)
            lines = dot(vh[at, :], onez) + dot(vm[at, :], onez) + dot(vl[at, :], onez)
            sampled = jnp.sum(jnp.where(cell_ids == cell, lines, 0.0), axis=0, keepdims=True)
            speed = got[7 + c : 8 + c] + got[10 + c : 11 + c] + got[13 + c : 14 + c]
            rel.append(sampled - speed)
        size = jnp.sqrt(rel[0] * rel[0] + rel[1] * rel[1] + rel[2] * rel[2] + 0.0001)
        size = -(factor * size)
        pieces = [split3(size * r) for r in rel]
        stack = [pieces[c][k].astype(F32) for k in range(3) for c in range(3)]
        stack = jnp.concatenate(stack + [jnp.zeros((7, CHUNK), F32)], axis=0).astype(BF16)
        spread = dot(stack, sel[...])
        dense[...] += spread[0:3] + spread[3:6] + spread[6:9]
        return carry

    lax.fori_loop(0, (count + CHUNK - 1) // CHUNK, chunk, 0)
    for c in range(3):
        for j in range(tiles):
            sibling[c * tiles + j : c * tiles + j + 1, :] = dense[
                c : c + 1, j * LANES : (j + 1) * LANES
            ]
    sibling[3 * tiles : 112, :] = jnp.zeros((112 - 3 * tiles, LANES), F32)
    across[0:112, :] = sibling[0:112, :]


def known(a, b):
    return jnp.where(a != 0.0, a, b)


def join_kernel(own, beside, beyond, out):
    even = lax.axis_index("gy") % 2 == 0
    out[0:112, :] = known(own[0:112, :], known(beside[0:112, :], beyond[0:112, :]))
    at = 112
    for x, first, second in ((CX - 1, 7, 9), (0, 10, 8)):
        for ids, wanted, south in ((NORTH, first, True), (SOUTH, second, False)):
            for k in [ids.index(wanted), 5, 6, 7, 8, 9]:
                row = slice(112 + 8 * k + x, 113 + 8 * k + x)
                a, b = beside[row, :], beyond[row, :]
                out[at : at + 1, :] = jnp.where(even, b, a) if south else jnp.where(even, a, b)
                at += 1


def finish_kernel(mine, other, out):
    whole = known(mine[...], other[...])
    tiles = out.shape[1] // LANES
    for c in range(3):
        for j in range(tiles):
            row = c * tiles + j
            out[c : c + 1, j * LANES : (j + 1) * LANES] = whole[row : row + 1, :]


FY = 72


def force_kernel(cells, points_in, out, sel, fld, m128, r128, *, total_x, total_y):
    points = cells.shape[1]
    tiles = points // LANES

    def wrapped(v, total):
        v = jnp.where(v < -(total // 2), v + total, v)
        return jnp.where(v >= total // 2, v - total, v)

    px = wrapped(cells[0:1, :] - lax.axis_index("gx") * CX, total_x)
    py = wrapped(cells[1:2, :] - lax.axis_index("gy") * CY, total_y)
    reach = SMEAR + 1
    near = (px >= -reach) & (px < CX + reach) & (py >= -reach) & (py < CY + reach)
    near = jnp.where(near, 1.0, 0.0)
    m128[...] = jnp.zeros_like(m128)
    for j in range(tiles):
        m128[j : j + 1, :] = near[:, j * LANES : (j + 1) * LANES]
    mask = m128[...]
    maskb = mask.astype(BF16)
    rows = lax.broadcasted_iota(jnp.int32, (LANES, LANES), 0)
    cols = lax.broadcasted_iota(jnp.int32, (LANES, LANES), 1)
    before = jnp.where(rows < cols, 1.0, 0.0).astype(BF16)
    above = jnp.where(rows > cols, 1.0, 0.0).astype(BF16)
    inside = dot(maskb, before)
    ahead = jnp.sum(dot(above, maskb), axis=1, keepdims=True)
    r128[...] = jnp.where(mask > 0.0, inside + ahead, -1.0)
    count = jnp.sum(mask).astype(jnp.int32)

    fld[0:1, :] = px.astype(F32)
    fld[1:2, :] = py.astype(F32)
    fld[2:3, :] = cells[2:3, :].astype(F32)
    pieces = split3(points_in[0:112, :])
    for k in range(3):
        piece = pieces[k].astype(F32)
        for c in range(3):
            for j in range(tiles):
                fld[3 + 3 * k + c : 4 + 3 * k + c, j * LANES : (j + 1) * LANES] = piece[
                    c * tiles + j : c * tiles + j + 1, :
                ]
    fld[12:16, :] = jnp.zeros((4, points), F32)
    out[...] = jnp.zeros_like(out)
    spots = lax.broadcasted_iota(jnp.int32, (CHUNK, LANES), 0).astype(F32)

    def kernel_value(cell, point):
        dist = cell - point
        return jnp.where(
            jnp.abs(dist) <= SMEAR, jnp.exp(-((dist / SCALE) * (dist / SCALE))), 0.0
        )

    def iota(size):
        return lax.broadcasted_iota(jnp.int32, (size, CHUNK), 0).astype(F32)

    def chunk(turn, carry):
        base = (turn * CHUNK).astype(F32)
        for j in range(tiles):
            hit = r128[j : j + 1, :] - base == spots
            sel[:, j * LANES : (j + 1) * LANES] = jnp.where(hit, 1.0, 0.0).astype(BF16)
        got = dot(fld[...].astype(BF16), sel[...], NT)
        kx = kernel_value(iota(16) - 1.0, got[0:1])
        ky = kernel_value(iota(FY) - 1.0, got[1:2])
        kz = kernel_value(iota(LANES), got[2:3])
        left = jnp.concatenate(
            [(got[3 + c : 4 + c] + got[6 + c : 7 + c] + got[9 + c : 10 + c]) * ky for c in range(3)],
            axis=0,
        )
        left_high = left.astype(BF16)
        left_low = (left - left_high.astype(F32)).astype(BF16)
        for x in range(CX + 2):
            right = kx[x : x + 1] * kz
            right_high = right.astype(BF16)
            right_low = (right - right_high.astype(F32)).astype(BF16)
            field = dot(left_high, right_high, NT) + (
                dot(left_high, right_low, NT) + dot(left_low, right_high, NT)
            )
            for c in range(3):
                out[c, x, :, :] += field[c * FY : (c + 1) * FY]
        return carry

    lax.fori_loop(0, (count + CHUNK - 1) // CHUNK, chunk, 0)


OY = 8


def step_kernel(
    pops, flags, force, from_west, from_east, beside, beyond, west_pts, east_pts,
    out_hbm, out, out_sems,
):
    lane = lax.broadcasted_iota(jnp.int32, (8, LANES), 1)
    not_first, not_last = lane > 0, lane < LANES - 1
    first, last = lane == 0, lane == LANES - 1

    def put(i, x, row, val):
        cx, cy, cz = DIRS[i]
        dst = out.at[i, x + 1 + cx, pl.ds(OY + row + cy, val.shape[0]), :]
        if cz == 0:
            dst[...] = val
        elif cz == 1:
            pltpu.store(dst, pltpu.roll(val, 1, 1), mask=not_first[: val.shape[0]])
        else:
            pltpu.store(dst, pltpu.roll(val, LANES - 1, 1), mask=not_last[: val.shape[0]])

    for ids, x, src in ((EAST, -1, from_west), (WEST, CX, from_east)):
        for yb in range(CY // 8):
            at = slice(yb * 8, yb * 8 + 8)
            frc = [force[c, x + 1, yb * 8 + 1 : yb * 8 + 9, :] for c in range(3)]
            rho, mom, solid = src[5, at, :], [src[6 + c, at, :] for c in range(3)], src[9, at, :] != 0.0
            hit = Collision(rho, mom, frc)
            for k, i in enumerate(ids):
                held = src[k, at, :]
                put(i, x, yb * 8, jnp.where(solid, held, KEEP * held + hit.one(i)))
    even = lax.axis_index("gy") % 2 == 0
    for ids, y in ((NORTH, -1), (SOUTH, CY)):
        part = []
        for k in range(10):
            a, b = beside[112 + 8 * k : 120 + 8 * k, :], beyond[112 + 8 * k : 120 + 8 * k, :]
            part.append(jnp.where(even, b, a) if y < 0 else jnp.where(even, a, b))
        frc = [force[c, 1 : CX + 1, y + 1, :] for c in range(3)]
        hit = Collision(part[5], part[6:9], frc)
        solid = part[9] != 0.0
        for k, i in enumerate(ids):
            val = jnp.where(solid, part[k], KEEP * part[k] + hit.one(i))
            cx, cy, cz = DIRS[i]
            if cz != 0:
                val = pltpu.roll(val, 1 if cz == 1 else LANES - 1, 1)
            for x in range(CX):
                dst = out.at[i, x + 1 + cx, OY + y + cy : OY + y + cy + 1, :]
                if cz == 0:
                    dst[...] = val[x : x + 1]
                else:
                    keep = (not_first if cz == 1 else not_last)[0:1]
                    pltpu.store(dst, val[x : x + 1], mask=keep)
    for src, at, i, x, y in (
        (west_pts, 112, 7, -1, -1),
        (west_pts, 118, 9, -1, CY),
        (east_pts, 124, 10, CX, -1),
        (east_pts, 130, 8, CX, CY),
    ):
        held, rho = src[at : at + 1, :], src[at + 1 : at + 2, :]
        mom = [src[at + 2 + c : at + 3 + c, :] for c in range(3)]
        solid = src[at + 5 : at + 6, :] != 0.0
        frc = [force[c, x + 1, y + 1 : y + 2, :] for c in range(3)]
        hit = Collision(rho, mom, frc)
        put(i, x, y, jnp.where(solid, held, KEEP * held + hit.one(i)))

    def send(x):
        return pltpu.make_async_copy(
            out.at[:, x + 1, OY : OY + CY, :], out_hbm.at[:, x], out_sems.at[x]
        )

    def plane(x, carry):
        for yb in range(CY // 8):
            at = slice(yb * 8, yb * 8 + 8)
            g = [pops[i, x, at, :] for i in range(19)]
            solid = flags[x, at, :] != 0
            rho, mom = moments(g)
            frc = [force[c, x + 1, yb * 8 + 1 : yb * 8 + 9, :] for c in range(3)]
            hit = Collision(rho, mom, frc)
            put(0, x, yb * 8, jnp.where(solid, g[0], KEEP * g[0] + hit.base))
            for k in range(1, 19, 2):
                even, odd = hit.terms(k)
                ahead = jnp.where(solid, g[k + 1], KEEP * g[k] + (even + odd))
                back = jnp.where(solid, g[k], KEEP * g[k + 1] + (even - odd))
                put(k, x, yb * 8, ahead)
                put(k + 1, x, yb * 8, back)
                if DIRS[k][2] != 0:
                    up, down = (k, k + 1) if DIRS[k][2] == 1 else (k + 1, k)
                    rising, falling = (ahead, back) if up == k else (back, ahead)
                    rows = pl.ds(OY + yb * 8, 8)
                    pltpu.store(out.at[up, x + 1, rows, :], falling, mask=first)
                    pltpu.store(out.at[down, x + 1, rows, :], rising, mask=last)

        @pl.when(x > 0)
        def _():
            send(x - 1).start()

        return carry

    lax.fori_loop(0, CX, plane, 0)
    send(CX - 1).start()
    for x in range(CX):
        send(x).wait()


def from_behind(block, axis, distance):
    count = lax.axis_size(axis)
    return lax.ppermute(block, axis, [((i - distance) % count, i) for i in range(count)])


def exchanged(block, source):
    count_x, count_y = lax.axis_size("gx"), lax.axis_size("gy")
    pairs = []
    for x in range(count_x):
        for y in range(count_y):
            from_x, from_y = source(x, y)
            pairs.append(((from_x % count_x) * count_y + from_y % count_y, x * count_y + y))
    return lax.ppermute(block, ("gx", "gy"), pairs)


def swapped(block):
    return exchanged(block, lambda x, y: (x, y ^ 1))


def fetched(block, first, second):
    return exchanged(
        block, lambda x, y: (x + (second if y % 2 else first)[0], y + (second if y % 2 else first)[1])
    )


def cost(flops):
    return pl.CostEstimate(flops=flops, bytes_accessed=0, transcendentals=0)


def local(populations, solid_flags, point_cells, point_turbine, blade_speed, chord, turbine_gain):
    points = point_cells.shape[1]
    total_x = CX * lax.axis_size("gx")
    total_y = CY * lax.axis_size("gy")
    sds = jax.ShapeDtypeStruct
    params = pltpu.CompilerParams(vmem_limit_bytes=40 * 1024 * 1024)
    light = pltpu.CompilerParams(vmem_limit_bytes=4 * 1024 * 1024)
    compact = [
        pltpu.VMEM((CHUNK, points), BF16),
        pltpu.VMEM((16, points), F32),
        pltpu.VMEM((LANES, LANES), F32),
        pltpu.VMEM((LANES, LANES), F32),
    ]
    sibling, across, east, west, held_pops = pl.pallas_call(
        sample_kernel,
        out_shape=(
            sds((192, LANES), F32),
            sds((192, LANES), F32),
            sds((10, CY, LANES), F32),
            sds((10, CY, LANES), F32),
            sds(populations.shape, F32),
        ),
        in_specs=[HBM] * 7,
        out_specs=(VMEM,) * 5,
        scratch_shapes=[
            *[pltpu.VMEM((3 * CX * CY, LANES), BF16)] * 3,
            *compact,
            pltpu.VMEM((3, points), F32),
            pltpu.VMEM((16, CHUNK), F32),
            pltpu.SMEM(turbine_gain.shape, F32),
            pltpu.VMEM(solid_flags.shape, jnp.int32),
            pltpu.VMEM((3, points), jnp.int32),
            pltpu.VMEM((1, points), jnp.int32),
            pltpu.VMEM((1, points), F32),
            pltpu.VMEM((3, points), F32),
            pltpu.SemaphoreType.DMA((CX,)),
            pltpu.SemaphoreType.DMA((6,)),
        ],
        compiler_params=params,
        name="sample",
    )(
        *[
            pltpu.with_memory_space_constraint(arg, pltpu.HBM)
            for arg in (
                turbine_gain, populations, solid_flags, point_cells, point_turbine, chord,
                blade_speed,
            )
        ]
    )
    beside = swapped(sibling)
    beyond = exchanged(across, lambda x, y: (x, y + 1 if y % 2 else y - 1))
    from_west = from_behind(east, "gx", 1)
    from_east = from_behind(west, "gx", -1)
    joined = pl.pallas_call(
        join_kernel,
        out_shape=sds((136, LANES), F32),
        in_specs=[VMEM] * 3,
        out_specs=VMEM,
        compiler_params=light,
        name="join",
    )(sibling, beside, beyond)
    west_pts = from_behind(joined, "gx", 1)
    east_pts = from_behind(joined, "gx", -1)
    near = known(joined[:112], known(west_pts[:112], east_pts[:112]))
    force = pl.pallas_call(
        functools.partial(force_kernel, total_x=total_x, total_y=total_y),
        out_shape=sds((3, CX + 2, FY, LANES), F32),
        in_specs=[VMEM, VMEM],
        out_specs=VMEM,
        scratch_shapes=compact,
        compiler_params=params,
        cost_estimate=cost(FORCE_FLOPS),
        name="force",
    )(point_cells, near)
    read = pl.pallas_call(
        step_kernel,
        out_shape=sds(populations.shape, F32),
        in_specs=[VMEM] * 9,
        out_specs=HBM,
        scratch_shapes=[
            pltpu.VMEM((19, CX + 2, CY + 16, LANES), F32),
            pltpu.SemaphoreType.DMA((CX,)),
        ],
        compiler_params=params,
        cost_estimate=cost(STEP_FLOPS),
        name="step",
    )(
        held_pops, solid_flags, force, from_west, from_east, beside, beyond, west_pts, east_pts,
    )
    have = known(near, swapped(near))
    got = fetched(have, (3, 0), (-3, 0))
    have = known(have, got)
    have = known(have, swapped(have))
    got = fetched(have, (7, 0), (4, 4))
    have = known(have, got)
    have = known(have, swapped(have))
    got = fetched(have, (8, 0), (20, 4))
    have = known(have, got)
    point_force = pl.pallas_call(
        finish_kernel,
        out_shape=sds((3, points), F32),
        in_specs=[VMEM] * 2,
        out_specs=VMEM,
        compiler_params=light,
        name="finish",
    )(have, swapped(have))
    return read, point_force


def solution(mesh):
    in_specs = (P(None, "gx", "gy", None), P("gx", "gy", None), P(), P(), P(), P(), P())
    out_specs = (P(None, "gx", "gy", None), P())
    return jax.shard_map(local, mesh=mesh, in_specs=in_specs, out_specs=out_specs, check_vma=False)
```

profile of v0, /device:TPU:1, one launch (start us, length us, event | category | flops | bytes accessed | tf_op | source)
XLA Modules:
  0.0 63.4 jit_solution(15799373529435997977)
XLA Ops:
  0.7 5.8 %sample.1 = (f32[192,128]{1,0:T(8,128)S(1)}, f32[192,128]{1,0:T(8,128)S(1)}, f32[10,64,128]{2,1,0:T(8,128)S(1)}, f32[10,64,128]{2,1,0:T(8,128)S(1)}, f32[19,8,64,128]{3,2,1,0:T(8,128)S(1)}) custom-call(f32[24]{0:T(128)} %gain_hbm.1, f32[19,8,64,128]{3,2,1,0:T(8,128)} %pops_hbm.1, s32[8,64,128]{2,1,0:T(8,128)} %flags.1, s32[3,4608]{1,0:T(4,128)} %cells.1, ...), custom_call_target="tpu_custom_call" | custom-call | tf_op jit(solution)/shard_map/sample/pallas_call | solution.py:523
  6.5 3.3 %collective-permute-start = (f32[192,128]{1,0:T(8,128)S(1)}, f32[192,128]{1,0:T(8,128)S(1)}, u32[]{:S(2)}, u32[]{:S(2)}) collective-permute-start(f32[192,128]{1,0:T(8,128)S(1)} %get-tuple-element.8.own), channel_id=1, source_target_pairs={{1,0},{0,1},{3,2},{2,3},{5,4},{4,5},{7,6},{6,7},{9,8},{8,9},{11,10... | collective-permute-start | bytes 294920 | tf_op jit(solution)/shard_map/ppermute | solution.py:493
  9.8 0.9 %collective-permute-done.beside = f32[192,128]{1,0:T(8,128)S(1)} collective-permute-done((f32[192,128]{1,0:T(8,128)S(1)}, f32[192,128]{1,0:T(8,128)S(1)}, u32[]{:S(2)}, u32[]{:S(2)}) %collective-permute-start) | collective-permute-done | bytes 98336 | tf_op jit(solution)/shard_map/ppermute | solution.py:493
  10.7 3.4 %collective-permute-done.1.beyond = f32[192,128]{1,0:T(8,128)S(1)} collective-permute-done((f32[192,128]{1,0:T(8,128)S(1)}, f32[192,128]{1,0:T(8,128)S(1)}, u32[]{:S(2)}, u32[]{:S(2)}) %collective-permute-start.1) | collective-permute-done | bytes 98336 | tf_op jit(solution)/shard_map/ppermute | solution.py:493
  14.2 3.9 %collective-permute-start.3 = (f32[136,128]{1,0:T(8,128)S(1)}, f32[136,128]{1,0:T(8,128)S(1)}, u32[]{:S(2)}, u32[]{:S(2)}) collective-permute-start(f32[136,128]{1,0:T(8,128)S(1)} %join.1), channel_id=1, source_target_pairs={{8,0},{16,8},{24,16},{32,24},{40,32},{48,40},{56,48},{64,56},{72,6... | collective-permute-start | bytes 208904 | tf_op jit(solution)/shard_map/ppermute | solution.py:483
  18.1 1.4 %collective-permute-done.3.east_pts = f32[136,128]{1,0:T(8,128)S(1)} collective-permute-done((f32[136,128]{1,0:T(8,128)S(1)}, f32[136,128]{1,0:T(8,128)S(1)}, u32[]{:S(2)}, u32[]{:S(2)}) %collective-permute-start.3) | collective-permute-done | bytes 69664 | tf_op jit(solution)/shard_map/ppermute | solution.py:483
  19.4 5.1 %collective-permute-done.2.west_pts = f32[136,128]{1,0:T(8,128)S(1)} collective-permute-done((f32[136,128]{1,0:T(8,128)S(1)}, f32[136,128]{1,0:T(8,128)S(1)}, u32[]{:S(2)}, u32[]{:S(2)}) %collective-permute-start.2) | collective-permute-done | bytes 69664 | tf_op jit(solution)/shard_map/ppermute | solution.py:483
  24.6 4.9 %collective-permute-start.6 = (f32[112,128]{1,0:T(8,128)S(1)}, f32[112,128]{1,0:T(8,128)S(1)}, u32[]{:S(2)}, u32[]{:S(2)}) collective-permute-start(f32[112,128]{1,0:T(8,128)S(1)} %compare_select_fusion.7.points_in), channel_id=1, source_target_pairs={{1,0},{0,1},{3,2},{2,3},{5,4},{4,5},{7,6},{6,7},{9,8},{8,9},{11,10... | collective-permute-start | bytes 172040 | tf_op jit(solution)/shard_map/ppermute | solution.py:493
  29.4 0.9 %collective-permute-done.6 = f32[112,128]{1,0:T(8,128)S(1)} collective-permute-done((f32[112,128]{1,0:T(8,128)S(1)}, f32[112,128]{1,0:T(8,128)S(1)}, u32[]{:S(2)}, u32[]{:S(2)}) %collective-permute-start.6) | collective-permute-done | bytes 57376 | tf_op jit(solution)/shard_map/ppermute | solution.py:493
  30.4 5.1 %collective-permute-done.7 = f32[112,128]{1,0:T(8,128)S(1)} collective-permute-done((f32[112,128]{1,0:T(8,128)S(1)}, f32[112,128]{1,0:T(8,128)S(1)}, u32[]{:S(2)}, u32[]{:S(2)}) %collective-permute-start.7) | collective-permute-done | bytes 57376 | tf_op jit(solution)/shard_map/ppermute | solution.py:493
  35.5 0.7 %collective-permute-start.8 = (f32[112,128]{1,0:T(8,128)S(1)}, f32[112,128]{1,0:T(8,128)S(1)}, u32[]{:S(2)}, u32[]{:S(2)}) collective-permute-start(f32[112,128]{1,0:T(8,128)S(1)} %compare_select_fusion.4), channel_id=1, source_target_pairs={{1,0},{0,1},{3,2},{2,3},{5,4},{4,5},{7,6},{6,7},{9,8},{8,9},{11,10... | collective-permute-start | bytes 172040 | tf_op jit(solution)/shard_map/ppermute | solution.py:493
  36.2 0.9 %collective-permute-done.8 = f32[112,128]{1,0:T(8,128)S(1)} collective-permute-done((f32[112,128]{1,0:T(8,128)S(1)}, f32[112,128]{1,0:T(8,128)S(1)}, u32[]{:S(2)}, u32[]{:S(2)}) %collective-permute-start.8) | collective-permute-done | bytes 57376 | tf_op jit(solution)/shard_map/ppermute | solution.py:493
  37.2 5.8 %collective-permute-done.9 = f32[112,128]{1,0:T(8,128)S(1)} collective-permute-done((f32[112,128]{1,0:T(8,128)S(1)}, f32[112,128]{1,0:T(8,128)S(1)}, u32[]{:S(2)}, u32[]{:S(2)}) %collective-permute-start.9) | collective-permute-done | bytes 57376 | tf_op jit(solution)/shard_map/ppermute | solution.py:493
  43.0 0.9 %collective-permute-start.10 = (f32[112,128]{1,0:T(8,128)S(1)}, f32[112,128]{1,0:T(8,128)S(1)}, u32[]{:S(2)}, u32[]{:S(2)}) collective-permute-start(f32[112,128]{1,0:T(8,128)S(1)} %compare_select_fusion.2), channel_id=1, source_target_pairs={{1,0},{0,1},{3,2},{2,3},{5,4},{4,5},{7,6},{6,7},{9,8},{8,9},{11,10... | collective-permute-start | bytes 172040 | tf_op jit(solution)/shard_map/ppermute | solution.py:493
  43.9 0.9 %collective-permute-done.10 = f32[112,128]{1,0:T(8,128)S(1)} collective-permute-done((f32[112,128]{1,0:T(8,128)S(1)}, f32[112,128]{1,0:T(8,128)S(1)}, u32[]{:S(2)}, u32[]{:S(2)}) %collective-permute-start.10) | collective-permute-done | bytes 57376 | tf_op jit(solution)/shard_map/ppermute | solution.py:493
  44.8 0.0 collective-permute-start.11
  44.9 1.0 %collective-permute-start.4 = (f32[10,64,128]{2,1,0:T(8,128)S(1)}, f32[10,64,128]{2,1,0:T(8,128)S(1)}, u32[]{:S(2)}, u32[]{:S(2)}) collective-permute-start(f32[10,64,128]{2,1,0:T(8,128)S(1)} %get-tuple-element.10), channel_id=1, source_target_pairs={{248,0},{0,8},{8,16},{16,24},{24,32},{32,40},{40,48},{48,56},{56,6... | collective-permute-start | bytes 983048 | tf_op jit(solution)/shard_map/ppermute | solution.py:483
  45.9 3.9 %collective-permute-start.5 = (f32[10,64,128]{2,1,0:T(8,128)S(1)}, f32[10,64,128]{2,1,0:T(8,128)S(1)}, u32[]{:S(2)}, u32[]{:S(2)}) collective-permute-start(f32[10,64,128]{2,1,0:T(8,128)S(1)} %get-tuple-element.11), channel_id=1, source_target_pairs={{8,0},{16,8},{24,16},{32,24},{40,32},{48,40},{56,48},{64,56},{72,6... | collective-permute-start | bytes 983048 | tf_op jit(solution)/shard_map/ppermute | solution.py:483
  49.8 3.6 %collective-permute-done.11 = f32[112,128]{1,0:T(8,128)S(1)} collective-permute-done((f32[112,128]{1,0:T(8,128)S(1)}, f32[112,128]{1,0:T(8,128)S(1)}, u32[]{:S(2)}, u32[]{:S(2)}) %collective-permute-start.11) | collective-permute-done | bytes 57376 | tf_op jit(solution)/shard_map/ppermute | solution.py:493
  53.3 0.1 collective-permute-start.12
  53.4 3.6 %force.1 = f32[3,10,72,128]{3,2,1,0:T(8,128)S(1)} custom-call(s32[3,4608]{1,0:T(4,128)S(1)} %copy-done.1, f32[112,128]{1,0:T(8,128)S(1)} %compare_select_fusion.7.points_in), custom_call_target="tpu_custom_call" | custom-call | flops 40000000 | tf_op jit(solution)/shard_map/force/pallas_call | solution.py:574
  57.1 1.4 %collective-permute-done.4.from_west = f32[10,64,128]{2,1,0:T(8,128)S(1)} collective-permute-done((f32[10,64,128]{2,1,0:T(8,128)S(1)}, f32[10,64,128]{2,1,0:T(8,128)S(1)}, u32[]{:S(2)}, u32[]{:S(2)}) %collective-permute-start.4) | collective-permute-done | bytes 327712 | tf_op jit(solution)/shard_map/ppermute | solution.py:483
  58.5 4.2 %step.1 = f32[19,8,64,128]{3,2,1,0:T(8,128)} custom-call(f32[19,8,64,128]{3,2,1,0:T(8,128)S(1)} %get-tuple-element.7.pops, s32[8,64,128]{2,1,0:T(8,128)S(1)} %copy-done, f32[3,10,72,128]{3,2,1,0:T(8,128)S(1)} %force.1, f32[10,64,128]{2,1,0:T(8,128)S(1)} %collective-permute-done.4.from_west, f32[10,64,128]{2,1,0:T(8,128)S(1)} %collective-permute-done.5.from_east, ...), custom_call_target="tpu_custom_call" | custom-call | flops 60000000 | tf_op jit(solution)/shard_map/step/pallas_call | solution.py:584
  62.7 0.7 %finish.1 = f32[3,4608]{1,0:T(4,128)} custom-call(f32[112,128]{1,0:T(8,128)S(1)} %compare_select_fusion.mine, f32[112,128]{1,0:T(8,128)S(1)} %collective-permute-done.12.other), custom_call_target="tpu_custom_call" | custom-call | tf_op jit(solution)/shard_map/finish/pallas_call | solution.py:608
  (18 shorter events, 0.2 us)
Async XLA Ops:
  0.6 57.9 %copy-start = (s32[8,64,128]{2,1,0:T(8,128)S(1)}, s32[8,64,128]{2,1,0:T(8,128)}, u32[]{:S(2)}) copy-start(s32[8,64,128]{2,1,0:T(8,128)} %flags.1) | copy-start | bytes 786436
  0.6 52.8 %copy-start.1 = (s32[3,4608]{1,0:T(4,128)S(1)}, s32[3,4608]{1,0:T(4,128)}, u32[]{:S(2)}) copy-start(s32[3,4608]{1,0:T(4,128)} %cells.1) | copy-start | bytes 165892
  6.5 4.2 %collective-permute-start = (f32[192,128]{1,0:T(8,128)S(1)}, f32[192,128]{1,0:T(8,128)S(1)}, u32[]{:S(2)}, u32[]{:S(2)}) collective-permute-start(f32[192,128]{1,0:T(8,128)S(1)} %get-tuple-element.8.own), channel_id=1, source_target_pairs={{1,0},{0,1},{3,2},{2,3},{5,4},{4,5},{7,6},{6,7},{9,8},{8,9},{11,10... | collective-permute-start | bytes 294920 | tf_op jit(solution)/shard_map/ppermute | solution.py:493
  9.8 4.3 %collective-permute-start.1 = (f32[192,128]{1,0:T(8,128)S(1)}, f32[192,128]{1,0:T(8,128)S(1)}, u32[]{:S(2)}, u32[]{:S(2)}) collective-permute-start(f32[192,128]{1,0:T(8,128)S(1)} %get-tuple-element.9), channel_id=1, source_target_pairs={{7,0},{2,1},{1,2},{4,3},{3,4},{6,5},{5,6},{0,7},{15,8},{10,9},{9,1... | collective-permute-start | bytes 294920 | tf_op jit(solution)/shard_map/ppermute | solution.py:493
  14.2 5.3 %collective-permute-start.3 = (f32[136,128]{1,0:T(8,128)S(1)}, f32[136,128]{1,0:T(8,128)S(1)}, u32[]{:S(2)}, u32[]{:S(2)}) collective-permute-start(f32[136,128]{1,0:T(8,128)S(1)} %join.1), channel_id=1, source_target_pairs={{8,0},{16,8},{24,16},{32,24},{40,32},{48,40},{56,48},{64,56},{72,6... | collective-permute-start | bytes 208904 | tf_op jit(solution)/shard_map/ppermute | solution.py:483
  18.1 6.5 %collective-permute-start.2 = (f32[136,128]{1,0:T(8,128)S(1)}, f32[136,128]{1,0:T(8,128)S(1)}, u32[]{:S(2)}, u32[]{:S(2)}) collective-permute-start(f32[136,128]{1,0:T(8,128)S(1)} %join.1), channel_id=1, source_target_pairs={{248,0},{0,8},{8,16},{16,24},{24,32},{32,40},{40,48},{48,56},{56,6... | collective-permute-start | bytes 208904 | tf_op jit(solution)/shard_map/ppermute | solution.py:483
  24.6 5.7 %collective-permute-start.6 = (f32[112,128]{1,0:T(8,128)S(1)}, f32[112,128]{1,0:T(8,128)S(1)}, u32[]{:S(2)}, u32[]{:S(2)}) collective-permute-start(f32[112,128]{1,0:T(8,128)S(1)} %compare_select_fusion.7.points_in), channel_id=1, source_target_pairs={{1,0},{0,1},{3,2},{2,3},{5,4},{4,5},{7,6},{6,7},{9,8},{8,9},{11,10... | collective-permute-start | bytes 172040 | tf_op jit(solution)/shard_map/ppermute | solution.py:493
  30.3 5.2 %collective-permute-start.7 = (f32[112,128]{1,0:T(8,128)S(1)}, f32[112,128]{1,0:T(8,128)S(1)}, u32[]{:S(2)}, u32[]{:S(2)}) collective-permute-start(f32[112,128]{1,0:T(8,128)S(1)} %compare_select_fusion.5), channel_id=1, source_target_pairs={{24,0},{233,1},{26,2},{235,3},{28,4},{237,5},{30,6},{239,7},{32,8}... | collective-permute-start | bytes 172040 | tf_op jit(solution)/shard_map/ppermute | solution.py:493
  35.5 1.6 %collective-permute-start.8 = (f32[112,128]{1,0:T(8,128)S(1)}, f32[112,128]{1,0:T(8,128)S(1)}, u32[]{:S(2)}, u32[]{:S(2)}) collective-permute-start(f32[112,128]{1,0:T(8,128)S(1)} %compare_select_fusion.4), channel_id=1, source_target_pairs={{1,0},{0,1},{3,2},{2,3},{5,4},{4,5},{7,6},{6,7},{9,8},{8,9},{11,10... | collective-permute-start | bytes 172040 | tf_op jit(solution)/shard_map/ppermute | solution.py:493
  37.1 5.9 %collective-permute-start.9 = (f32[112,128]{1,0:T(8,128)S(1)}, f32[112,128]{1,0:T(8,128)S(1)}, u32[]{:S(2)}, u32[]{:S(2)}) collective-permute-start(f32[112,128]{1,0:T(8,128)S(1)} %compare_select_fusion.3), channel_id=1, source_target_pairs={{56,0},{37,1},{58,2},{39,3},{60,4},{33,5},{62,6},{35,7},{64,8},{45... | collective-permute-start | bytes 172040 | tf_op jit(solution)/shard_map/ppermute | solution.py:493
  43.0 1.8 %collective-permute-start.10 = (f32[112,128]{1,0:T(8,128)S(1)}, f32[112,128]{1,0:T(8,128)S(1)}, u32[]{:S(2)}, u32[]{:S(2)}) collective-permute-start(f32[112,128]{1,0:T(8,128)S(1)} %compare_select_fusion.2), channel_id=1, source_target_pairs={{1,0},{0,1},{3,2},{2,3},{5,4},{4,5},{7,6},{6,7},{9,8},{8,9},{11,10... | collective-permute-start | bytes 172040 | tf_op jit(solution)/shard_map/ppermute | solution.py:493
  44.8 8.5 %collective-permute-start.11 = (f32[112,128]{1,0:T(8,128)S(1)}, f32[112,128]{1,0:T(8,128)S(1)}, u32[]{:S(2)}, u32[]{:S(2)}) collective-permute-start(f32[112,128]{1,0:T(8,128)S(1)} %compare_select_fusion.1), channel_id=1, source_target_pairs={{64,0},{165,1},{66,2},{167,3},{68,4},{161,5},{70,6},{163,7},{72,8}... | collective-permute-start | bytes 172040 | tf_op jit(solution)/shard_map/ppermute | solution.py:493
  44.9 13.6 %collective-permute-start.4 = (f32[10,64,128]{2,1,0:T(8,128)S(1)}, f32[10,64,128]{2,1,0:T(8,128)S(1)}, u32[]{:S(2)}, u32[]{:S(2)}) collective-permute-start(f32[10,64,128]{2,1,0:T(8,128)S(1)} %get-tuple-element.10), channel_id=1, source_target_pairs={{248,0},{0,8},{8,16},{16,24},{24,32},{32,40},{40,48},{48,56},{56,6... | collective-permute-start | bytes 983048 | tf_op jit(solution)/shard_map/ppermute | solution.py:483
  45.9 12.7 %collective-permute-start.5 = (f32[10,64,128]{2,1,0:T(8,128)S(1)}, f32[10,64,128]{2,1,0:T(8,128)S(1)}, u32[]{:S(2)}, u32[]{:S(2)}) collective-permute-start(f32[10,64,128]{2,1,0:T(8,128)S(1)} %get-tuple-element.11), channel_id=1, source_target_pairs={{8,0},{16,8},{24,16},{32,24},{40,32},{48,40},{56,48},{64,56},{72,6... | collective-permute-start | bytes 983048 | tf_op jit(solution)/shard_map/ppermute | solution.py:483
  53.3 9.4 %collective-permute-start.12 = (f32[112,128]{1,0:T(8,128)S(1)}, f32[112,128]{1,0:T(8,128)S(1)}, u32[]{:S(2)}, u32[]{:S(2)}) collective-permute-start(f32[112,128]{1,0:T(8,128)S(1)} %compare_select_fusion.mine), channel_id=1, source_target_pairs={{1,0},{0,1},{3,2},{2,3},{5,4},{4,5},{7,6},{6,7},{9,8},{8,9},{11,10... | collective-permute-start | bytes 172040 | tf_op jit(solution)/shard_map/ppermute | solution.py:493
where the time goes:
time: 63.4 us
  waiting for transfers between devices  29.4 us (46%)
  starting transfers between devices  18.8 us (30%)
  Pallas kernels  14.3 us (23%)
  between operations  0.74 us (1%)
    ppermute x9, waiting for transfers between devices, exchanged(): return lax.ppermute(block, ('gx', 'gy'), pairs)  21.5 us
    ppermute x9, starting transfers between devices, exchanged(): return lax.ppermute(block, ('gx', 'gy'), pairs)  10 us
    ppermute x4, starting transfers between devices, from_behind(): lax.ppermute(block, axis, [((i - distance) % count, i) for i in range(cou...  8.76 us
    ppermute x4, waiting for transfers between devices, from_behind(): lax.ppermute(block, axis, [((i - distance) % count, i) for i in range(cou...  7.9 us
    pallas_call x1, Pallas kernels, local(): pl.pallas_call(sample_kernel, out_shape=(sds((192, LANES), F32), sds((192...  5.85 us
    pallas_call x1, Pallas kernels, local(): pl.pallas_call(step_kernel, out_shape=sds(populations.shape, F32), in_spe...  4.16 us
    pallas_call x1, Pallas kernels, local(): pl.pallas_call(functools.partial(force_kernel, total_x=total_x, total_y=t...  3.64 us
  transfers between devices with their start and end apart: 13, of which 11 were waited for; matrix products, arithmetic and copies ran while one was open for 0% of the time, Pallas kernels for 12%

commit v1 on v0

--- a/solution.py
+++ b/solution.py
@@ -379,16 +379,16 @@
 
 
 def step_kernel(
-    pops, flags, force, from_west, from_east, beside, beyond, west_pts, east_pts,
-    out_hbm, out, out_sems,
+    pops, flags, force, from_west, from_east, beside, beyond, west_pts, east_pts, *rest, low, high
 ):
+    out_hbm, out, out_sems = rest[-3:]
     lane = lax.broadcasted_iota(jnp.int32, (8, LANES), 1)
     not_first, not_last = lane > 0, lane < LANES - 1
     first, last = lane == 0, lane == LANES - 1
 
     def put(i, x, row, val):
         cx, cy, cz = DIRS[i]
-        dst = out.at[i, x + 1 + cx, pl.ds(OY + row + cy, val.shape[0]), :]
+        dst = out.at[i, x - low + 1 + cx, pl.ds(OY + row + cy, val.shape[0]), :]
         if cz == 0:
             dst[...] = val
         elif cz == 1:
@@ -396,15 +396,27 @@
         else:
             pltpu.store(dst, pltpu.roll(val, LANES - 1, 1), mask=not_last[: val.shape[0]])
 
-    for ids, x, src in ((EAST, -1, from_west), (WEST, CX, from_east)):
+    def inside(x):
+        return low <= x < high
+
+    def force_at(x, yb):
+        return [force[c, x + 1, yb * 8 + 1 : yb * 8 + 9, :] for c in range(3)]
+
+    for ids, x, src in ((EAST, low - 1, from_west), (WEST, high, from_east)):
         for yb in range(CY // 8):
             at = slice(yb * 8, yb * 8 + 8)
-            frc = [force[c, x + 1, yb * 8 + 1 : yb * 8 + 9, :] for c in range(3)]
-            rho, mom, solid = src[5, at, :], [src[6 + c, at, :] for c in range(3)], src[9, at, :] != 0.0
-            hit = Collision(rho, mom, frc)
-            for k, i in enumerate(ids):
-                held = src[k, at, :]
-                put(i, x, yb * 8, jnp.where(solid, held, KEEP * held + hit.one(i)))
+            if 0 <= x < CX:
+                g = [pops[i, x, at, :] for i in range(19)]
+                rho, mom = moments(g)
+                solid = flags[x, at, :] != 0
+                held = [jnp.where(solid, g[OPP[i]], g[i]) for i in ids]
+            else:
+                rho, mom = src[5, at, :], [src[6 + c, at, :] for c in range(3)]
+                solid = src[9, at, :] != 0.0
+                held = [src[k, at, :] for k in range(5)]
+            hit = Collision(rho, mom, force_at(x, yb))
+            for val, i in zip(held, ids):
+                put(i, x, yb * 8, jnp.where(solid, val, KEEP * val + hit.one(i)))
     even = lax.axis_index("gy") % 2 == 0
     for ids, y in ((NORTH, -1), (SOUTH, CY)):
         part = []
@@ -420,7 +432,9 @@
             if cz != 0:
                 val = pltpu.roll(val, 1 if cz == 1 else LANES - 1, 1)
             for x in range(CX):
-                dst = out.at[i, x + 1 + cx, OY + y + cy : OY + y + cy + 1, :]
+                if not inside(x + cx):
+                    continue
+                dst = out.at[i, x - low + 1 + cx, OY + y + cy : OY + y + cy + 1, :]
                 if cz == 0:
                     dst[...] = val[x : x + 1]
                 else:
@@ -432,6 +446,8 @@
         (east_pts, 124, 10, CX, -1),
         (east_pts, 130, 8, CX, CY),
     ):
+        if not inside(x + DIRS[i][0]):
+            continue
         held, rho = src[at : at + 1, :], src[at + 1 : at + 2, :]
         mom = [src[at + 2 + c : at + 3 + c, :] for c in range(3)]
         solid = src[at + 5 : at + 6, :] != 0.0
@@ -441,7 +457,7 @@
 
     def send(x):
         return pltpu.make_async_copy(
-            out.at[:, x + 1, OY : OY + CY, :], out_hbm.at[:, x], out_sems.at[x]
+            out.at[:, x - low + 1, OY : OY + CY, :], out_hbm.at[:, x], out_sems.at[x]
         )
 
     def plane(x, carry):
@@ -450,8 +466,7 @@
             g = [pops[i, x, at, :] for i in range(19)]
             solid = flags[x, at, :] != 0
             rho, mom = moments(g)
-            frc = [force[c, x + 1, yb * 8 + 1 : yb * 8 + 9, :] for c in range(3)]
-            hit = Collision(rho, mom, frc)
+            hit = Collision(rho, mom, force_at(x, yb))
             put(0, x, yb * 8, jnp.where(solid, g[0], KEEP * g[0] + hit.base))
             for k in range(1, 19, 2):
                 even, odd = hit.terms(k)
@@ -463,18 +478,18 @@
                     up, down = (k, k + 1) if DIRS[k][2] == 1 else (k + 1, k)
                     rising, falling = (ahead, back) if up == k else (back, ahead)
                     rows = pl.ds(OY + yb * 8, 8)
-                    pltpu.store(out.at[up, x + 1, rows, :], falling, mask=first)
-                    pltpu.store(out.at[down, x + 1, rows, :], rising, mask=last)
-
-        @pl.when(x > 0)
+                    pltpu.store(out.at[up, x - low + 1, rows, :], falling, mask=first)
+                    pltpu.store(out.at[down, x - low + 1, rows, :], rising, mask=last)
+
+        @pl.when(x > low)
         def _():
             send(x - 1).start()
 
         return carry
 
-    lax.fori_loop(0, CX, plane, 0)
-    send(CX - 1).start()
-    for x in range(CX):
+    lax.fori_loop(low, high, plane, 0)
+    send(high - 1).start()
+    for x in range(low, high):
         send(x).wait()
 
 
@@ -581,21 +596,25 @@
         cost_estimate=cost(FORCE_FLOPS),
         name="force",
     )(point_cells, near)
-    read = pl.pallas_call(
-        step_kernel,
-        out_shape=sds(populations.shape, F32),
-        in_specs=[VMEM] * 9,
-        out_specs=HBM,
-        scratch_shapes=[
-            pltpu.VMEM((19, CX + 2, CY + 16, LANES), F32),
-            pltpu.SemaphoreType.DMA((CX,)),
-        ],
-        compiler_params=params,
-        cost_estimate=cost(STEP_FLOPS),
-        name="step",
-    )(
+    step_args = (
         held_pops, solid_flags, force, from_west, from_east, beside, beyond, west_pts, east_pts,
     )
+    read = None
+    for low, high in ((0, CX // 2), (CX // 2, CX)):
+        extra = () if read is None else (read,)
+        read = pl.pallas_call(
+            functools.partial(step_kernel, low=low, high=high),
+            out_shape=sds(populations.shape, F32),
+            in_specs=[VMEM] * 9 + [HBM] * len(extra),
+            out_specs=HBM,
+            scratch_shapes=[
+                pltpu.VMEM((19, high - low + 2, CY + 16, LANES), F32),
+                pltpu.SemaphoreType.DMA((CX,)),
+            ],
+            input_output_aliases={9: 0} if extra else {},
+            compiler_params=params,
+            cost_estimate=cost(STEP_FLOPS),
+        )(*step_args, *extra)
     have = known(near, swapped(near))
     got = fetched(have, (3, 0), (-3, 0))
     have = known(have, got)

time: 63.4 us -> 65.1 us (1.027)
  Pallas kernels: 14.3 us -> 15.9 us
    pallas_call x1 -> x2, Pallas kernels: 4.16 us -> 5.77 us  [local(): pl.pallas_call(functools.partial(step_kernel, low=low, high=high), out_sh...]
  transfers between devices with their start and end apart: 13 -> 13, of which waited for: 11 -> 11; matrix products, arithmetic and copies ran while one was open for 0% -> 0% of each run, Pallas kernels for 12% -> 14%
where the time goes in v1:
time: 65.1 us; the launch traced here: 65 us
  waiting for transfers between devices  29.4 us (45%)
  starting transfers between devices  18.8 us (29%)
  Pallas kernels  15.9 us (24%)
  between operations  0.75 us (1%)
    ppermute x9, waiting for transfers between devices, exchanged(): return lax.ppermute(block, ('gx', 'gy'), pairs)  21.5 us
    ppermute x9, starting transfers between devices, exchanged(): return lax.ppermute(block, ('gx', 'gy'), pairs)  10 us
    ppermute x4, starting transfers between devices, from_behind(): lax.ppermute(block, axis, [((i - distance) % count, i) for i in range(cou...  8.76 us
    ppermute x4, waiting for transfers between devices, from_behind(): lax.ppermute(block, axis, [((i - distance) % count, i) for i in range(cou...  7.91 us
    pallas_call x1, Pallas kernels, local(): pl.pallas_call(sample_kernel, out_shape=(sds((192, LANES), F32), sds((192...  5.85 us
    pallas_call x2, Pallas kernels, local(): pl.pallas_call(functools.partial(step_kernel, low=low, high=high), out_sh...  5.77 us
    pallas_call x1, Pallas kernels, local(): pl.pallas_call(functools.partial(force_kernel, total_x=total_x, total_y=t...  3.64 us
  transfers between devices with their start and end apart: 13, of which 11 were waited for; matrix products, arithmetic and copies ran while one was open for 0% of the time, Pallas kernels for 14%

profile of v1, /device:TPU:1, one launch (start us, length us, event | category | flops | bytes accessed | tf_op | source)
XLA Modules:
  0.0 65.0 jit_solution(17077905105114087061)
XLA Ops:
  0.7 5.8 %sample.1 = (f32[192,128]{1,0:T(8,128)S(1)}, f32[192,128]{1,0:T(8,128)S(1)}, f32[10,64,128]{2,1,0:T(8,128)S(1)}, f32[10,64,128]{2,1,0:T(8,128)S(1)}, f32[19,8,64,128]{3,2,1,0:T(8,128)S(1)}) custom-call(f32[24]{0:T(128)} %gain_hbm.1, f32[19,8,64,128]{3,2,1,0:T(8,128)} %pops_hbm.1, s32[8,64,128]{2,1,0:T(8,128)} %flags.3, s32[3,4608]{1,0:T(4,128)} %cells.1, ...), custom_call_target="tpu_custom_call" | custom-call | tf_op jit(solution)/shard_map/sample/pallas_call | solution.py:538
  6.5 3.3 %collective-permute-start = (f32[192,128]{1,0:T(8,128)S(1)}, f32[192,128]{1,0:T(8,128)S(1)}, u32[]{:S(2)}, u32[]{:S(2)}) collective-permute-start(f32[192,128]{1,0:T(8,128)S(1)} %get-tuple-element.8.own), channel_id=1, source_target_pairs={{1,0},{0,1},{3,2},{2,3},{5,4},{4,5},{7,6},{6,7},{9,8},{8,9},{11,10... | collective-permute-start | bytes 294920 | tf_op jit(solution)/shard_map/ppermute | solution.py:508
  9.8 0.9 %collective-permute-done.beside = f32[192,128]{1,0:T(8,128)S(1)} collective-permute-done((f32[192,128]{1,0:T(8,128)S(1)}, f32[192,128]{1,0:T(8,128)S(1)}, u32[]{:S(2)}, u32[]{:S(2)}) %collective-permute-start) | collective-permute-done | bytes 98336 | tf_op jit(solution)/shard_map/ppermute | solution.py:508
  10.7 3.4 %collective-permute-done.1.beyond = f32[192,128]{1,0:T(8,128)S(1)} collective-permute-done((f32[192,128]{1,0:T(8,128)S(1)}, f32[192,128]{1,0:T(8,128)S(1)}, u32[]{:S(2)}, u32[]{:S(2)}) %collective-permute-start.1) | collective-permute-done | bytes 98336 | tf_op jit(solution)/shard_map/ppermute | solution.py:508
  14.2 3.9 %collective-permute-start.3 = (f32[136,128]{1,0:T(8,128)S(1)}, f32[136,128]{1,0:T(8,128)S(1)}, u32[]{:S(2)}, u32[]{:S(2)}) collective-permute-start(f32[136,128]{1,0:T(8,128)S(1)} %join.1), channel_id=1, source_target_pairs={{8,0},{16,8},{24,16},{32,24},{40,32},{48,40},{56,48},{64,56},{72,6... | collective-permute-start | bytes 208904 | tf_op jit(solution)/shard_map/ppermute | solution.py:498
  18.1 1.4 %collective-permute-done.3.east_pts = f32[136,128]{1,0:T(8,128)S(1)} collective-permute-done((f32[136,128]{1,0:T(8,128)S(1)}, f32[136,128]{1,0:T(8,128)S(1)}, u32[]{:S(2)}, u32[]{:S(2)}) %collective-permute-start.3) | collective-permute-done | bytes 69664 | tf_op jit(solution)/shard_map/ppermute | solution.py:498
  19.4 5.1 %collective-permute-done.2.west_pts = f32[136,128]{1,0:T(8,128)S(1)} collective-permute-done((f32[136,128]{1,0:T(8,128)S(1)}, f32[136,128]{1,0:T(8,128)S(1)}, u32[]{:S(2)}, u32[]{:S(2)}) %collective-permute-start.2) | collective-permute-done | bytes 69664 | tf_op jit(solution)/shard_map/ppermute | solution.py:498
  24.5 4.8 %collective-permute-start.6 = (f32[112,128]{1,0:T(8,128)S(1)}, f32[112,128]{1,0:T(8,128)S(1)}, u32[]{:S(2)}, u32[]{:S(2)}) collective-permute-start(f32[112,128]{1,0:T(8,128)S(1)} %compare_select_fusion.7.points_in), channel_id=1, source_target_pairs={{1,0},{0,1},{3,2},{2,3},{5,4},{4,5},{7,6},{6,7},{9,8},{8,9},{11,10... | collective-permute-start | bytes 172040 | tf_op jit(solution)/shard_map/ppermute | solution.py:508
  29.4 0.9 %collective-permute-done.6 = f32[112,128]{1,0:T(8,128)S(1)} collective-permute-done((f32[112,128]{1,0:T(8,128)S(1)}, f32[112,128]{1,0:T(8,128)S(1)}, u32[]{:S(2)}, u32[]{:S(2)}) %collective-permute-start.6) | collective-permute-done | bytes 57376 | tf_op jit(solution)/shard_map/ppermute | solution.py:508
  30.3 5.1 %collective-permute-done.7 = f32[112,128]{1,0:T(8,128)S(1)} collective-permute-done((f32[112,128]{1,0:T(8,128)S(1)}, f32[112,128]{1,0:T(8,128)S(1)}, u32[]{:S(2)}, u32[]{:S(2)}) %collective-permute-start.7) | collective-permute-done | bytes 57376 | tf_op jit(solution)/shard_map/ppermute | solution.py:508
  35.5 0.7 %collective-permute-start.8 = (f32[112,128]{1,0:T(8,128)S(1)}, f32[112,128]{1,0:T(8,128)S(1)}, u32[]{:S(2)}, u32[]{:S(2)}) collective-permute-start(f32[112,128]{1,0:T(8,128)S(1)} %compare_select_fusion.4), channel_id=1, source_target_pairs={{1,0},{0,1},{3,2},{2,3},{5,4},{4,5},{7,6},{6,7},{9,8},{8,9},{11,10... | collective-permute-start | bytes 172040 | tf_op jit(solution)/shard_map/ppermute | solution.py:508
  36.2 0.9 %collective-permute-done.8 = f32[112,128]{1,0:T(8,128)S(1)} collective-permute-done((f32[112,128]{1,0:T(8,128)S(1)}, f32[112,128]{1,0:T(8,128)S(1)}, u32[]{:S(2)}, u32[]{:S(2)}) %collective-permute-start.8) | collective-permute-done | bytes 57376 | tf_op jit(solution)/shard_map/ppermute | solution.py:508
  37.2 5.8 %collective-permute-done.9 = f32[112,128]{1,0:T(8,128)S(1)} collective-permute-done((f32[112,128]{1,0:T(8,128)S(1)}, f32[112,128]{1,0:T(8,128)S(1)}, u32[]{:S(2)}, u32[]{:S(2)}) %collective-permute-start.9) | collective-permute-done | bytes 57376 | tf_op jit(solution)/shard_map/ppermute | solution.py:508
  43.0 1.0 %collective-permute-start.10 = (f32[112,128]{1,0:T(8,128)S(1)}, f32[112,128]{1,0:T(8,128)S(1)}, u32[]{:S(2)}, u32[]{:S(2)}) collective-permute-start(f32[112,128]{1,0:T(8,128)S(1)} %compare_select_fusion.2), channel_id=1, source_target_pairs={{1,0},{0,1},{3,2},{2,3},{5,4},{4,5},{7,6},{6,7},{9,8},{8,9},{11,10... | collective-permute-start | bytes 172040 | tf_op jit(solution)/shard_map/ppermute | solution.py:508
  43.9 0.9 %collective-permute-done.10 = f32[112,128]{1,0:T(8,128)S(1)} collective-permute-done((f32[112,128]{1,0:T(8,128)S(1)}, f32[112,128]{1,0:T(8,128)S(1)}, u32[]{:S(2)}, u32[]{:S(2)}) %collective-permute-start.10) | collective-permute-done | bytes 57376 | tf_op jit(solution)/shard_map/ppermute | solution.py:508
  44.9 1.0 %collective-permute-start.4 = (f32[10,64,128]{2,1,0:T(8,128)S(1)}, f32[10,64,128]{2,1,0:T(8,128)S(1)}, u32[]{:S(2)}, u32[]{:S(2)}) collective-permute-start(f32[10,64,128]{2,1,0:T(8,128)S(1)} %get-tuple-element.10), channel_id=1, source_target_pairs={{248,0},{0,8},{8,16},{16,24},{24,32},{32,40},{40,48},{48,56},{56,6... | collective-permute-start | bytes 983048 | tf_op jit(solution)/shard_map/ppermute | solution.py:498
  45.9 3.9 %collective-permute-start.5 = (f32[10,64,128]{2,1,0:T(8,128)S(1)}, f32[10,64,128]{2,1,0:T(8,128)S(1)}, u32[]{:S(2)}, u32[]{:S(2)}) collective-permute-start(f32[10,64,128]{2,1,0:T(8,128)S(1)} %get-tuple-element.11), channel_id=1, source_target_pairs={{8,0},{16,8},{24,16},{32,24},{40,32},{48,40},{56,48},{64,56},{72,6... | collective-permute-start | bytes 983048 | tf_op jit(solution)/shard_map/ppermute | solution.py:498
  49.7 3.6 %collective-permute-done.11 = f32[112,128]{1,0:T(8,128)S(1)} collective-permute-done((f32[112,128]{1,0:T(8,128)S(1)}, f32[112,128]{1,0:T(8,128)S(1)}, u32[]{:S(2)}, u32[]{:S(2)}) %collective-permute-start.11) | collective-permute-done | bytes 57376 | tf_op jit(solution)/shard_map/ppermute | solution.py:508
  53.3 0.1 collective-permute-start.12
  53.4 3.6 %force.1 = f32[3,10,72,128]{3,2,1,0:T(8,128)S(1)} custom-call(s32[3,4608]{1,0:T(4,128)S(1)} %copy-done.1, f32[112,128]{1,0:T(8,128)S(1)} %compare_select_fusion.7.points_in), custom_call_target="tpu_custom_call" | custom-call | flops 40000000 | tf_op jit(solution)/shard_map/force/pallas_call | solution.py:589
  57.1 1.4 %collective-permute-done.4.from_west = f32[10,64,128]{2,1,0:T(8,128)S(1)} collective-permute-done((f32[10,64,128]{2,1,0:T(8,128)S(1)}, f32[10,64,128]{2,1,0:T(8,128)S(1)}, u32[]{:S(2)}, u32[]{:S(2)}) %collective-permute-start.4) | collective-permute-done | bytes 327712 | tf_op jit(solution)/shard_map/ppermute | solution.py:498
  58.5 2.9 %shard_map.86.rest_0_ = f32[19,8,64,128]{3,2,1,0:T(8,128)} custom-call(f32[19,8,64,128]{3,2,1,0:T(8,128)S(1)} %get-tuple-element.7.pops, s32[8,64,128]{2,1,0:T(8,128)S(1)} %copy-done, f32[3,10,72,128]{3,2,1,0:T(8,128)S(1)} %force.1, f32[10,64,128]{2,1,0:T(8,128)S(1)} %collective-permute-done.4.from_west, ...), custom_call_target="tpu_custom_call" | custom-call | flops 60000000 | tf_op jit(solution)/shard_map/pallas_call | solution.py:605
  61.4 2.9 %shard_map.87 = f32[19,8,64,128]{3,2,1,0:T(8,128)} custom-call(f32[19,8,64,128]{3,2,1,0:T(8,128)S(1)} %get-tuple-element.7.pops, s32[8,64,128]{2,1,0:T(8,128)S(1)} %copy-done, f32[3,10,72,128]{3,2,1,0:T(8,128)S(1)} %force.1, f32[10,64,128]{2,1,0:T(8,128)S(1)} %collective-permute-done.4.from_west, ...), custom_call_target="tpu_custom_call", output_to_operand_aliasing={{}: (9, {})} | custom-call | flops 60000000 | tf_op jit(solution)/shard_map/pallas_call | solution.py:605
  64.3 0.7 %finish.1 = f32[3,4608]{1,0:T(4,128)} custom-call(f32[112,128]{1,0:T(8,128)S(1)} %compare_select_fusion.mine, f32[112,128]{1,0:T(8,128)S(1)} %collective-permute-done.12.other), custom_call_target="tpu_custom_call" | custom-call | tf_op jit(solution)/shard_map/finish/pallas_call | solution.py:627
  (19 shorter events, 0.2 us)
Async XLA Ops:
  0.6 57.9 %copy-start = (s32[8,64,128]{2,1,0:T(8,128)S(1)}, s32[8,64,128]{2,1,0:T(8,128)}, u32[]{:S(2)}) copy-start(s32[8,64,128]{2,1,0:T(8,128)} %flags.3) | copy-start | bytes 786436
  0.6 52.8 %copy-start.1 = (s32[3,4608]{1,0:T(4,128)S(1)}, s32[3,4608]{1,0:T(4,128)}, u32[]{:S(2)}) copy-start(s32[3,4608]{1,0:T(4,128)} %cells.1) | copy-start | bytes 165892
  6.5 4.2 %collective-permute-start = (f32[192,128]{1,0:T(8,128)S(1)}, f32[192,128]{1,0:T(8,128)S(1)}, u32[]{:S(2)}, u32[]{:S(2)}) collective-permute-start(f32[192,128]{1,0:T(8,128)S(1)} %get-tuple-element.8.own), channel_id=1, source_target_pairs={{1,0},{0,1},{3,2},{2,3},{5,4},{4,5},{7,6},{6,7},{9,8},{8,9},{11,10... | collective-permute-start | bytes 294920 | tf_op jit(solution)/shard_map/ppermute | solution.py:508
  9.8 4.3 %collective-permute-start.1 = (f32[192,128]{1,0:T(8,128)S(1)}, f32[192,128]{1,0:T(8,128)S(1)}, u32[]{:S(2)}, u32[]{:S(2)}) collective-permute-start(f32[192,128]{1,0:T(8,128)S(1)} %get-tuple-element.9), channel_id=1, source_target_pairs={{7,0},{2,1},{1,2},{4,3},{3,4},{6,5},{5,6},{0,7},{15,8},{10,9},{9,1... | collective-permute-start | bytes 294920 | tf_op jit(solution)/shard_map/ppermute | solution.py:508
  14.2 5.3 %collective-permute-start.3 = (f32[136,128]{1,0:T(8,128)S(1)}, f32[136,128]{1,0:T(8,128)S(1)}, u32[]{:S(2)}, u32[]{:S(2)}) collective-permute-start(f32[136,128]{1,0:T(8,128)S(1)} %join.1), channel_id=1, source_target_pairs={{8,0},{16,8},{24,16},{32,24},{40,32},{48,40},{56,48},{64,56},{72,6... | collective-permute-start | bytes 208904 | tf_op jit(solution)/shard_map/ppermute | solution.py:498
  18.1 6.5 %collective-permute-start.2 = (f32[136,128]{1,0:T(8,128)S(1)}, f32[136,128]{1,0:T(8,128)S(1)}, u32[]{:S(2)}, u32[]{:S(2)}) collective-permute-start(f32[136,128]{1,0:T(8,128)S(1)} %join.1), channel_id=1, source_target_pairs={{248,0},{0,8},{8,16},{16,24},{24,32},{32,40},{40,48},{48,56},{56,6... | collective-permute-start | bytes 208904 | tf_op jit(solution)/shard_map/ppermute | solution.py:498
  24.5 5.7 %collective-permute-start.6 = (f32[112,128]{1,0:T(8,128)S(1)}, f32[112,128]{1,0:T(8,128)S(1)}, u32[]{:S(2)}, u32[]{:S(2)}) collective-permute-start(f32[112,128]{1,0:T(8,128)S(1)} %compare_select_fusion.7.points_in), channel_id=1, source_target_pairs={{1,0},{0,1},{3,2},{2,3},{5,4},{4,5},{7,6},{6,7},{9,8},{8,9},{11,10... | collective-permute-start | bytes 172040 | tf_op jit(solution)/shard_map/ppermute | solution.py:508
  30.3 5.2 %collective-permute-start.7 = (f32[112,128]{1,0:T(8,128)S(1)}, f32[112,128]{1,0:T(8,128)S(1)}, u32[]{:S(2)}, u32[]{:S(2)}) collective-permute-start(f32[112,128]{1,0:T(8,128)S(1)} %compare_select_fusion.5), channel_id=1, source_target_pairs={{24,0},{233,1},{26,2},{235,3},{28,4},{237,5},{30,6},{239,7},{32,8}... | collective-permute-start | bytes 172040 | tf_op jit(solution)/shard_map/ppermute | solution.py:508
  35.5 1.6 %collective-permute-start.8 = (f32[112,128]{1,0:T(8,128)S(1)}, f32[112,128]{1,0:T(8,128)S(1)}, u32[]{:S(2)}, u32[]{:S(2)}) collective-permute-start(f32[112,128]{1,0:T(8,128)S(1)} %compare_select_fusion.4), channel_id=1, source_target_pairs={{1,0},{0,1},{3,2},{2,3},{5,4},{4,5},{7,6},{6,7},{9,8},{8,9},{11,10... | collective-permute-start | bytes 172040 | tf_op jit(solution)/shard_map/ppermute | solution.py:508
  37.1 5.9 %collective-permute-start.9 = (f32[112,128]{1,0:T(8,128)S(1)}, f32[112,128]{1,0:T(8,128)S(1)}, u32[]{:S(2)}, u32[]{:S(2)}) collective-permute-start(f32[112,128]{1,0:T(8,128)S(1)} %compare_select_fusion.3), channel_id=1, source_target_pairs={{56,0},{37,1},{58,2},{39,3},{60,4},{33,5},{62,6},{35,7},{64,8},{45... | collective-permute-start | bytes 172040 | tf_op jit(solution)/shard_map/ppermute | solution.py:508
  43.0 1.8 %collective-permute-start.10 = (f32[112,128]{1,0:T(8,128)S(1)}, f32[112,128]{1,0:T(8,128)S(1)}, u32[]{:S(2)}, u32[]{:S(2)}) collective-permute-start(f32[112,128]{1,0:T(8,128)S(1)} %compare_select_fusion.2), channel_id=1, source_target_pairs={{1,0},{0,1},{3,2},{2,3},{5,4},{4,5},{7,6},{6,7},{9,8},{8,9},{11,10... | collective-permute-start | bytes 172040 | tf_op jit(solution)/shard_map/ppermute | solution.py:508
  44.8 8.5 %collective-permute-start.11 = (f32[112,128]{1,0:T(8,128)S(1)}, f32[112,128]{1,0:T(8,128)S(1)}, u32[]{:S(2)}, u32[]{:S(2)}) collective-permute-start(f32[112,128]{1,0:T(8,128)S(1)} %compare_select_fusion.1), channel_id=1, source_target_pairs={{64,0},{165,1},{66,2},{167,3},{68,4},{161,5},{70,6},{163,7},{72,8}... | collective-permute-start | bytes 172040 | tf_op jit(solution)/shard_map/ppermute | solution.py:508
  44.9 13.6 %collective-permute-start.4 = (f32[10,64,128]{2,1,0:T(8,128)S(1)}, f32[10,64,128]{2,1,0:T(8,128)S(1)}, u32[]{:S(2)}, u32[]{:S(2)}) collective-permute-start(f32[10,64,128]{2,1,0:T(8,128)S(1)} %get-tuple-element.10), channel_id=1, source_target_pairs={{248,0},{0,8},{8,16},{16,24},{24,32},{32,40},{40,48},{48,56},{56,6... | collective-permute-start | bytes 983048 | tf_op jit(solution)/shard_map/ppermute | solution.py:498
  45.9 12.7 %collective-permute-start.5 = (f32[10,64,128]{2,1,0:T(8,128)S(1)}, f32[10,64,128]{2,1,0:T(8,128)S(1)}, u32[]{:S(2)}, u32[]{:S(2)}) collective-permute-start(f32[10,64,128]{2,1,0:T(8,128)S(1)} %get-tuple-element.11), channel_id=1, source_target_pairs={{8,0},{16,8},{24,16},{32,24},{40,32},{48,40},{56,48},{64,56},{72,6... | collective-permute-start | bytes 983048 | tf_op jit(solution)/shard_map/ppermute | solution.py:498
  53.3 11.0 %collective-permute-start.12 = (f32[112,128]{1,0:T(8,128)S(1)}, f32[112,128]{1,0:T(8,128)S(1)}, u32[]{:S(2)}, u32[]{:S(2)}) collective-permute-start(f32[112,128]{1,0:T(8,128)S(1)} %compare_select_fusion.mine), channel_id=1, source_target_pairs={{1,0},{0,1},{3,2},{2,3},{5,4},{4,5},{7,6},{6,7},{9,8},{8,9},{11,10... | collective-permute-start | bytes 172040 | tf_op jit(solution)/shard_map/ppermute | solution.py:508

commit v2 on v1

--- a/solution.py
+++ b/solution.py
@@ -45,6 +45,7 @@
 STEP_FLOPS = 60_000_000
 HBM = pl.BlockSpec(memory_space=pltpu.HBM)
 VMEM = pl.BlockSpec(memory_space=pltpu.VMEM)
+SMEM = pl.BlockSpec(memory_space=pltpu.SMEM)
 NT = (((1,), (1,)), ((), ()))
 NN = (((1,), (0,)), ((), ()))
 
@@ -123,7 +124,7 @@
 def sample_kernel(
     gain_hbm, pops_hbm, flags_hbm, cells_hbm, turb_hbm, chord_hbm, blade_hbm,
     sibling, across, east, west, pops,
-    vh, vm, vl, sel, fld, m128, r128, dense, got_ref,
+    vhm, vl, sel, fld, m128, r128, dense, got_ref,
     gain, flags, cells, turb, chord, blade, sems, in_sems,
 ):
     small = [
@@ -200,8 +201,8 @@
             for c in range(3):
                 at = pl.multiple_of(c * CX * CY + x * CY + yb * 16, 16)
                 high, mid, low = split3(mom[c] / rho)
-                vh[pl.ds(at, 16), :] = high
-                vm[pl.ds(at, 16), :] = mid
+                vhm[pl.ds(at, 16), 0:LANES] = high
+                vhm[pl.ds(at, 16), LANES : 2 * LANES] = mid
                 vl[pl.ds(at, 16), :] = low
         return carry
 
@@ -236,6 +237,7 @@
         got = got_ref[...]
         cell = got[0:1] * CY + got[1:2]
         onez = jnp.where(levels == got[2:3], 1.0, 0.0).astype(BF16)
+        twice = jnp.concatenate([onez, onez], axis=0)
         factor = jnp.zeros((1, CHUNK), F32)
         for t in range(gain.shape[0]):
             factor = jnp.where(got[3:4] == t, gain[t], factor)
@@ -243,7 +245,7 @@
         rel = []
         for c in range(3):
             at = slice(c * CX * CY, (c + 1) * CX * CY)
-            lines = dot(vh[at, :], onez) + dot(vm[at, :], onez) + dot(vl[at, :], onez)
+            lines = dot(vhm[at, :], twice) + dot(vl[at, :], onez)
             sampled = jnp.sum(jnp.where(cell_ids == cell, lines, 0.0), axis=0, keepdims=True)
             speed = got[7 + c : 8 + c] + got[10 + c : 11 + c] + got[13 + c : 14 + c]
             rel.append(sampled - speed)
@@ -295,7 +297,17 @@
 FY = 72
 
 
-def force_kernel(cells, points_in, out, sel, fld, m128, r128, *, total_x, total_y):
+READY = 2
+
+
+def choose_points(rank, base, sel):
+    spots = lax.broadcasted_iota(jnp.int32, (CHUNK, LANES), 0).astype(F32)
+    for j in range(sel.shape[1] // LANES):
+        hit = rank[j : j + 1, :] - base == spots
+        sel[:, j * LANES : (j + 1) * LANES] = jnp.where(hit, 1.0, 0.0).astype(BF16)
+
+
+def prep_kernel(cells, sel, spot, rank, places, count_out, m128, *, total_x, total_y):
     points = cells.shape[1]
     tiles = points // LANES
 
@@ -319,23 +331,27 @@
     above = jnp.where(rows > cols, 1.0, 0.0).astype(BF16)
     inside = dot(maskb, before)
     ahead = jnp.sum(dot(above, maskb), axis=1, keepdims=True)
-    r128[...] = jnp.where(mask > 0.0, inside + ahead, -1.0)
+    rank[...] = jnp.where(mask > 0.0, inside + ahead, -1.0)
     count = jnp.sum(mask).astype(jnp.int32)
-
-    fld[0:1, :] = px.astype(F32)
-    fld[1:2, :] = py.astype(F32)
-    fld[2:3, :] = cells[2:3, :].astype(F32)
-    pieces = split3(points_in[0:112, :])
-    for k in range(3):
-        piece = pieces[k].astype(F32)
-        for c in range(3):
-            for j in range(tiles):
-                fld[3 + 3 * k + c : 4 + 3 * k + c, j * LANES : (j + 1) * LANES] = piece[
-                    c * tiles + j : c * tiles + j + 1, :
-                ]
-    fld[12:16, :] = jnp.zeros((4, points), F32)
+    count_out[0] = count
+    places[0:1, :] = px.astype(F32)
+    places[1:2, :] = py.astype(F32)
+    places[2:3, :] = cells[2:3, :].astype(F32)
+    places[3:8, :] = jnp.zeros((5, points), F32)
+    for k in range(READY):
+
+        @pl.when(count > k * CHUNK)
+        def _():
+            chosen = sel.at[k]
+            choose_points(rank, float(k * CHUNK), chosen)
+            spot[k] = dot(places[...].astype(BF16), chosen[...], NT)
+
+
+def force_kernel(sel_in, spot_in, rank, places, count_in, points_in, out, sel, fld):
+    points = fld.shape[1]
+    tiles = points // LANES
+    count = count_in[0]
     out[...] = jnp.zeros_like(out)
-    spots = lax.broadcasted_iota(jnp.int32, (CHUNK, LANES), 0).astype(F32)
 
     def kernel_value(cell, point):
         dist = cell - point
@@ -346,33 +362,55 @@
     def iota(size):
         return lax.broadcasted_iota(jnp.int32, (size, CHUNK), 0).astype(F32)
 
-    def chunk(turn, carry):
-        base = (turn * CHUNK).astype(F32)
-        for j in range(tiles):
-            hit = r128[j : j + 1, :] - base == spots
-            sel[:, j * LANES : (j + 1) * LANES] = jnp.where(hit, 1.0, 0.0).astype(BF16)
-        got = dot(fld[...].astype(BF16), sel[...], NT)
-        kx = kernel_value(iota(16) - 1.0, got[0:1])
-        ky = kernel_value(iota(FY) - 1.0, got[1:2])
-        kz = kernel_value(iota(LANES), got[2:3])
+    def spread(chosen, spot):
+        got = dot(fld[...].astype(BF16), chosen, NT)
+        kx = kernel_value(iota(16) - 1.0, spot[0:1])
+        ky = kernel_value(iota(FY) - 1.0, spot[1:2])
+        kz = kernel_value(iota(LANES), spot[2:3])
         left = jnp.concatenate(
-            [(got[3 + c : 4 + c] + got[6 + c : 7 + c] + got[9 + c : 10 + c]) * ky for c in range(3)],
+            [(got[c : 1 + c] + got[3 + c : 4 + c] + got[6 + c : 7 + c]) * ky for c in range(3)],
             axis=0,
         )
         left_high = left.astype(BF16)
         left_low = (left - left_high.astype(F32)).astype(BF16)
-        for x in range(CX + 2):
-            right = kx[x : x + 1] * kz
+        for x in range(0, CX + 2, 2):
+            right = jnp.concatenate([kx[x : x + 1] * kz, kx[x + 1 : x + 2] * kz], axis=0)
             right_high = right.astype(BF16)
             right_low = (right - right_high.astype(F32)).astype(BF16)
             field = dot(left_high, right_high, NT) + (
                 dot(left_high, right_low, NT) + dot(left_low, right_high, NT)
             )
             for c in range(3):
-                out[c, x, :, :] += field[c * FY : (c + 1) * FY]
+                part = field[c * FY : (c + 1) * FY]
+                out[c, x, :, :] += part[:, :LANES]
+                out[c, x + 1, :, :] += part[:, LANES:]
+
+    @pl.when(count > 0)
+    def _():
+        pieces = split3(points_in[0:112, :])
+        for k in range(3):
+            piece = pieces[k].astype(F32)
+            for c in range(3):
+                for j in range(tiles):
+                    fld[3 * k + c : 1 + 3 * k + c, j * LANES : (j + 1) * LANES] = piece[
+                        c * tiles + j : c * tiles + j + 1, :
+                    ]
+        fld[9:16, :] = jnp.zeros((7, points), F32)
+
+    ready = (jnp.minimum(count, READY * CHUNK) + CHUNK - 1) // CHUNK
+
+    def chunk(turn, carry):
+        spread(sel_in[turn], spot_in[turn])
         return carry
 
-    lax.fori_loop(0, (count + CHUNK - 1) // CHUNK, chunk, 0)
+    lax.fori_loop(0, ready, chunk, 0)
+
+    def late(turn, carry):
+        choose_points(rank, (turn * CHUNK).astype(F32), sel)
+        spread(sel[...], dot(places[...].astype(BF16), sel[...], NT))
+        return carry
+
+    lax.fori_loop(READY, (count + CHUNK - 1) // CHUNK, late, 0)
 
 
 OY = 8
@@ -527,7 +565,7 @@
     total_x = CX * lax.axis_size("gx")
     total_y = CY * lax.axis_size("gy")
     sds = jax.ShapeDtypeStruct
-    params = pltpu.CompilerParams(vmem_limit_bytes=40 * 1024 * 1024)
+    params = pltpu.CompilerParams(vmem_limit_bytes=24 * 1024 * 1024)
     light = pltpu.CompilerParams(vmem_limit_bytes=4 * 1024 * 1024)
     compact = [
         pltpu.VMEM((CHUNK, points), BF16),
@@ -547,7 +585,8 @@
         in_specs=[HBM] * 7,
         out_specs=(VMEM,) * 5,
         scratch_shapes=[
-            *[pltpu.VMEM((3 * CX * CY, LANES), BF16)] * 3,
+            pltpu.VMEM((3 * CX * CY, 2 * LANES), BF16),
+            pltpu.VMEM((3 * CX * CY, LANES), BF16),
             *compact,
             pltpu.VMEM((3, points), F32),
             pltpu.VMEM((16, CHUNK), F32),
@@ -586,16 +625,32 @@
     west_pts = from_behind(joined, "gx", 1)
     east_pts = from_behind(joined, "gx", -1)
     near = known(joined[:112], known(west_pts[:112], east_pts[:112]))
+    prepared = pl.pallas_call(
+        functools.partial(prep_kernel, total_x=total_x, total_y=total_y),
+        out_shape=(
+            sds((READY, CHUNK, points), BF16),
+            sds((READY, 8, CHUNK), F32),
+            sds((LANES, LANES), F32),
+            sds((8, points), F32),
+            sds((1,), jnp.int32),
+        ),
+        in_specs=[VMEM],
+        out_specs=(VMEM, VMEM, VMEM, VMEM, SMEM),
+        scratch_shapes=[pltpu.VMEM((LANES, LANES), F32)],
+        compiler_params=params,
+        cost_estimate=cost(FORCE_FLOPS),
+        name="prep",
+    )(point_cells)
     force = pl.pallas_call(
-        functools.partial(force_kernel, total_x=total_x, total_y=total_y),
+        force_kernel,
         out_shape=sds((3, CX + 2, FY, LANES), F32),
-        in_specs=[VMEM, VMEM],
+        in_specs=[VMEM, VMEM, VMEM, VMEM, SMEM, VMEM],
         out_specs=VMEM,
-        scratch_shapes=compact,
+        scratch_shapes=[pltpu.VMEM((CHUNK, points), BF16), pltpu.VMEM((16, points), F32)],
         compiler_params=params,
         cost_estimate=cost(FORCE_FLOPS),
         name="force",
-    )(point_cells, near)
+    )(*prepared, near)
     step_args = (
         held_pops, solid_flags, force, from_west, from_east, beside, beyond, west_pts, east_pts,
     )
@@ -615,7 +670,8 @@
             compiler_params=params,
             cost_estimate=cost(STEP_FLOPS),
         )(*step_args, *extra)
-    have = known(near, swapped(near))
+    got = swapped(near)
+    have = known(near, got)
     got = fetched(have, (3, 0), (-3, 0))
     have = known(have, got)
     have = known(have, swapped(have))

time: 65.1 us -> 65.1 us (level)
  waiting for transfers between devices: 29.4 us -> 28.1 us
  Pallas kernels: 15.9 us -> 16.9 us
    ppermute x4, waiting for transfers between devices: 7.91 us -> 6.6 us  [from_behind(): lax.ppermute(block, axis, [((i - distance) % count, i) for i in range(cou...]
    pallas_call x1 -> x2, Pallas kernels: 3.64 us -> 4.94 us  [the longest x1 3.23 us: local(): pl.pallas_call(force_kernel, out_shape=sds((3, CX + 2, FY, LANES), F32),...]
  transfers between devices with their start and end apart: 13 -> 13, of which waited for: 11 -> 11; matrix products, arithmetic and copies ran while one was open for 0% -> 0% of each run, Pallas kernels for 14% -> 17%
where the time goes in v2:
time: 65.1 us; the launch traced here: 64.6 us
  waiting for transfers between devices  28.1 us (43%)
  starting transfers between devices  18.8 us (29%)
  Pallas kernels  16.9 us (26%)
  between operations  0.76 us (1%)
    ppermute x9, waiting for transfers between devices, exchanged(): return lax.ppermute(block, ('gx', 'gy'), pairs)  21.5 us
    ppermute x9, starting transfers between devices, exchanged(): return lax.ppermute(block, ('gx', 'gy'), pairs)  9.71 us
    ppermute x4, starting transfers between devices, from_behind(): lax.ppermute(block, axis, [((i - distance) % count, i) for i in range(cou...  9.09 us
    ppermute x4, waiting for transfers between devices, from_behind(): lax.ppermute(block, axis, [((i - distance) % count, i) for i in range(cou...  6.6 us
    pallas_call x2, Pallas kernels, local(): pl.pallas_call(functools.partial(step_kernel, low=low, high=high), out_sh...  5.77 us
    pallas_call x1, Pallas kernels, local(): pl.pallas_call(sample_kernel, out_shape=(sds((192, LANES), F32), sds((192...  5.51 us
    pallas_call x1, Pallas kernels, local(): pl.pallas_call(force_kernel, out_shape=sds((3, CX + 2, FY, LANES), F32),...  3.23 us
    pallas_call x1, Pallas kernels, local(): pl.pallas_call(functools.partial(prep_kernel, total_x=total_x, total_y=to...  1.7 us
  transfers between devices with their start and end apart: 13, of which 11 were waited for; matrix products, arithmetic and copies ran while one was open for 0% of the time, Pallas kernels for 17%

profile of v2, /device:TPU:1, one launch (start us, length us, event | category | flops | bytes accessed | tf_op | source)
XLA Modules:
  0.0 64.6 jit_solution(876077082480296016)
XLA Ops:
  0.6 5.5 %sample.1 = (f32[192,128]{1,0:T(8,128)S(1)}, f32[192,128]{1,0:T(8,128)S(1)}, f32[10,64,128]{2,1,0:T(8,128)S(1)}, f32[10,64,128]{2,1,0:T(8,128)S(1)}, f32[19,8,64,128]{3,2,1,0:T(8,128)S(1)}) custom-call(f32[24]{0:T(128)} %gain_hbm.1, f32[19,8,64,128]{3,2,1,0:T(8,128)} %pops_hbm.1, s32[8,64,128]{2,1,0:T(8,128)} %flags.3, s32[3,4608]{1,0:T(4,128)} %cells.1, ...), custom_call_target="tpu_custom_call" | custom-call | tf_op jit(solution)/shard_map/sample/pallas_call | solution.py:576
  6.2 3.3 %collective-permute-start = (f32[192,128]{1,0:T(8,128)S(1)}, f32[192,128]{1,0:T(8,128)S(1)}, u32[]{:S(2)}, u32[]{:S(2)}) collective-permute-start(f32[192,128]{1,0:T(8,128)S(1)} %get-tuple-element.18.own), channel_id=1, source_target_pairs={{1,0},{0,1},{3,2},{2,3},{5,4},{4,5},{7,6},{6,7},{9,8},{8,9},{11,10... | collective-permute-start | bytes 294920 | tf_op jit(solution)/shard_map/ppermute | solution.py:546
  9.5 0.9 %collective-permute-done.beside = f32[192,128]{1,0:T(8,128)S(1)} collective-permute-done((f32[192,128]{1,0:T(8,128)S(1)}, f32[192,128]{1,0:T(8,128)S(1)}, u32[]{:S(2)}, u32[]{:S(2)}) %collective-permute-start) | collective-permute-done | bytes 98336 | tf_op jit(solution)/shard_map/ppermute | solution.py:546
  10.4 3.4 %collective-permute-done.1.beyond = f32[192,128]{1,0:T(8,128)S(1)} collective-permute-done((f32[192,128]{1,0:T(8,128)S(1)}, f32[192,128]{1,0:T(8,128)S(1)}, u32[]{:S(2)}, u32[]{:S(2)}) %collective-permute-start.1) | collective-permute-done | bytes 98336 | tf_op jit(solution)/shard_map/ppermute | solution.py:546
  13.8 4.2 %collective-permute-start.3 = (f32[136,128]{1,0:T(8,128)S(1)}, f32[136,128]{1,0:T(8,128)S(1)}, u32[]{:S(2)}, u32[]{:S(2)}) collective-permute-start(f32[136,128]{1,0:T(8,128)S(1)} %join.1), channel_id=1, source_target_pairs={{8,0},{16,8},{24,16},{32,24},{40,32},{48,40},{56,48},{64,56},{72,6... | collective-permute-start | bytes 208904 | tf_op jit(solution)/shard_map/ppermute | solution.py:536
  18.1 1.4 %collective-permute-done.3.east_pts = f32[136,128]{1,0:T(8,128)S(1)} collective-permute-done((f32[136,128]{1,0:T(8,128)S(1)}, f32[136,128]{1,0:T(8,128)S(1)}, u32[]{:S(2)}, u32[]{:S(2)}) %collective-permute-start.3) | collective-permute-done | bytes 69664 | tf_op jit(solution)/shard_map/ppermute | solution.py:536
  19.4 5.1 %collective-permute-done.2.west_pts = f32[136,128]{1,0:T(8,128)S(1)} collective-permute-done((f32[136,128]{1,0:T(8,128)S(1)}, f32[136,128]{1,0:T(8,128)S(1)}, u32[]{:S(2)}, u32[]{:S(2)}) %collective-permute-start.2) | collective-permute-done | bytes 69664 | tf_op jit(solution)/shard_map/ppermute | solution.py:536
  24.6 4.5 %collective-permute-start.6 = (f32[112,128]{1,0:T(8,128)S(1)}, f32[112,128]{1,0:T(8,128)S(1)}, u32[]{:S(2)}, u32[]{:S(2)}) collective-permute-start(f32[112,128]{1,0:T(8,128)S(1)} %compare_select_fusion.7.points_in), channel_id=1, source_target_pairs={{1,0},{0,1},{3,2},{2,3},{5,4},{4,5},{7,6},{6,7},{9,8},{8,9},{11,10... | collective-permute-start | bytes 172040 | tf_op jit(solution)/shard_map/ppermute | solution.py:546
  29.1 0.9 %collective-permute-done.6 = f32[112,128]{1,0:T(8,128)S(1)} collective-permute-done((f32[112,128]{1,0:T(8,128)S(1)}, f32[112,128]{1,0:T(8,128)S(1)}, u32[]{:S(2)}, u32[]{:S(2)}) %collective-permute-start.6) | collective-permute-done | bytes 57376 | tf_op jit(solution)/shard_map/ppermute | solution.py:546
  30.0 5.1 %collective-permute-done.7 = f32[112,128]{1,0:T(8,128)S(1)} collective-permute-done((f32[112,128]{1,0:T(8,128)S(1)}, f32[112,128]{1,0:T(8,128)S(1)}, u32[]{:S(2)}, u32[]{:S(2)}) %collective-permute-start.7) | collective-permute-done | bytes 57376 | tf_op jit(solution)/shard_map/ppermute | solution.py:546
  35.2 0.7 %collective-permute-start.8 = (f32[112,128]{1,0:T(8,128)S(1)}, f32[112,128]{1,0:T(8,128)S(1)}, u32[]{:S(2)}, u32[]{:S(2)}) collective-permute-start(f32[112,128]{1,0:T(8,128)S(1)} %compare_select_fusion.4), channel_id=1, source_target_pairs={{1,0},{0,1},{3,2},{2,3},{5,4},{4,5},{7,6},{6,7},{9,8},{8,9},{11,10... | collective-permute-start | bytes 172040 | tf_op jit(solution)/shard_map/ppermute | solution.py:546
  35.9 0.9 %collective-permute-done.8 = f32[112,128]{1,0:T(8,128)S(1)} collective-permute-done((f32[112,128]{1,0:T(8,128)S(1)}, f32[112,128]{1,0:T(8,128)S(1)}, u32[]{:S(2)}, u32[]{:S(2)}) %collective-permute-start.8) | collective-permute-done | bytes 57376 | tf_op jit(solution)/shard_map/ppermute | solution.py:546
  36.8 5.8 %collective-permute-done.9 = f32[112,128]{1,0:T(8,128)S(1)} collective-permute-done((f32[112,128]{1,0:T(8,128)S(1)}, f32[112,128]{1,0:T(8,128)S(1)}, u32[]{:S(2)}, u32[]{:S(2)}) %collective-permute-start.9) | collective-permute-done | bytes 57376 | tf_op jit(solution)/shard_map/ppermute | solution.py:546
  42.7 0.9 %collective-permute-start.10 = (f32[112,128]{1,0:T(8,128)S(1)}, f32[112,128]{1,0:T(8,128)S(1)}, u32[]{:S(2)}, u32[]{:S(2)}) collective-permute-start(f32[112,128]{1,0:T(8,128)S(1)} %compare_select_fusion.2), channel_id=1, source_target_pairs={{1,0},{0,1},{3,2},{2,3},{5,4},{4,5},{7,6},{6,7},{9,8},{8,9},{11,10... | collective-permute-start | bytes 172040 | tf_op jit(solution)/shard_map/ppermute | solution.py:546
  43.6 0.9 %collective-permute-done.10 = f32[112,128]{1,0:T(8,128)S(1)} collective-permute-done((f32[112,128]{1,0:T(8,128)S(1)}, f32[112,128]{1,0:T(8,128)S(1)}, u32[]{:S(2)}, u32[]{:S(2)}) %collective-permute-start.10) | collective-permute-done | bytes 57376 | tf_op jit(solution)/shard_map/ppermute | solution.py:546
  44.6 1.3 %collective-permute-start.4 = (f32[10,64,128]{2,1,0:T(8,128)S(1)}, f32[10,64,128]{2,1,0:T(8,128)S(1)}, u32[]{:S(2)}, u32[]{:S(2)}) collective-permute-start(f32[10,64,128]{2,1,0:T(8,128)S(1)} %get-tuple-element.20), channel_id=1, source_target_pairs={{248,0},{0,8},{8,16},{16,24},{24,32},{32,40},{40,48},{48,56},{56,6... | collective-permute-start | bytes 983048 | tf_op jit(solution)/shard_map/ppermute | solution.py:536
  45.9 3.6 %collective-permute-start.5 = (f32[10,64,128]{2,1,0:T(8,128)S(1)}, f32[10,64,128]{2,1,0:T(8,128)S(1)}, u32[]{:S(2)}, u32[]{:S(2)}) collective-permute-start(f32[10,64,128]{2,1,0:T(8,128)S(1)} %get-tuple-element.21), channel_id=1, source_target_pairs={{8,0},{16,8},{24,16},{32,24},{40,32},{48,40},{56,48},{64,56},{72,6... | collective-permute-start | bytes 983048 | tf_op jit(solution)/shard_map/ppermute | solution.py:536
  49.4 3.6 %collective-permute-done.11 = f32[112,128]{1,0:T(8,128)S(1)} collective-permute-done((f32[112,128]{1,0:T(8,128)S(1)}, f32[112,128]{1,0:T(8,128)S(1)}, u32[]{:S(2)}, u32[]{:S(2)}) %collective-permute-start.11) | collective-permute-done | bytes 57376 | tf_op jit(solution)/shard_map/ppermute | solution.py:546
  53.1 1.7 %prep.1 = (bf16[2,256,4608]{2,1,0:T(8,128)(2,1)S(1)}, f32[2,8,256]{2,1,0:T(8,128)S(1)}, f32[128,128]{1,0:T(8,128)S(1)}, f32[8,4608]{1,0:T(8,128)S(1)}, s32[1]{0:T(128)}) custom-call(s32[3,4608]{1,0:T(4,128)S(1)} %copy-done.1), custom_call_target="tpu_custom_call" | custom-call | flops 40000000 | tf_op jit(solution)/shard_map/prep/pallas_call | solution.py:628
  54.8 3.2 %force.1 = f32[3,10,72,128]{3,2,1,0:T(8,128)S(1)} custom-call(bf16[2,256,4608]{2,1,0:T(8,128)(2,1)S(1)} %get-tuple-element.13.sel_in, f32[2,8,256]{2,1,0:T(8,128)S(1)} %get-tuple-element.14.spot_in, f32[128,128]{1,0:T(8,128)S(1)} %get-tuple-element.15.rank, f32[8,4608]{1,0:T(8,128)S(1)} %get-tuple-element.16.places, s32[1]{0:T(128)} %get-tuple-element.17.count_in, ...), custom_call_target="tpu_custom_call" | custom-call | flops 40000000 | tf_op jit(solution)/shard_map/force/pallas_call | solution.py:644
  58.1 0.1 collective-permute-done.4.from_west
  58.2 2.9 %shard_map.86.rest_0_ = f32[19,8,64,128]{3,2,1,0:T(8,128)} custom-call(f32[19,8,64,128]{3,2,1,0:T(8,128)S(1)} %get-tuple-element.12.pops, s32[8,64,128]{2,1,0:T(8,128)S(1)} %copy-done, f32[3,10,72,128]{3,2,1,0:T(8,128)S(1)} %force.1, f32[10,64,128]{2,1,0:T(8,128)S(1)} %collective-permute-done.4.from_west, ...), custom_call_target="tpu_custom_call" | custom-call | flops 60000000 | tf_op jit(solution)/shard_map/pallas_call | solution.py:660
  61.1 2.9 %shard_map.87 = f32[19,8,64,128]{3,2,1,0:T(8,128)} custom-call(f32[19,8,64,128]{3,2,1,0:T(8,128)S(1)} %get-tuple-element.12.pops, s32[8,64,128]{2,1,0:T(8,128)S(1)} %copy-done, f32[3,10,72,128]{3,2,1,0:T(8,128)S(1)} %force.1, f32[10,64,128]{2,1,0:T(8,128)S(1)} %collective-permute-done.4.from_west, ...), custom_call_target="tpu_custom_call", output_to_operand_aliasing={{}: (9, {})} | custom-call | flops 60000000 | tf_op jit(solution)/shard_map/pallas_call | solution.py:660
  64.0 0.7 %finish.1 = f32[3,4608]{1,0:T(4,128)} custom-call(f32[112,128]{1,0:T(8,128)S(1)} %compare_select_fusion.mine, f32[112,128]{1,0:T(8,128)S(1)} %collective-permute-done.12.other), custom_call_target="tpu_custom_call" | custom-call | tf_op jit(solution)/shard_map/finish/pallas_call | solution.py:683
  (20 shorter events, 0.3 us)
Async XLA Ops:
  0.6 52.5 %copy-start.1 = (s32[3,4608]{1,0:T(4,128)S(1)}, s32[3,4608]{1,0:T(4,128)}, u32[]{:S(2)}) copy-start(s32[3,4608]{1,0:T(4,128)} %cells.1) | copy-start | bytes 165892
  6.2 52.0 %copy-start = (s32[8,64,128]{2,1,0:T(8,128)S(1)}, s32[8,64,128]{2,1,0:T(8,128)}, u32[]{:S(2)}) copy-start(s32[8,64,128]{2,1,0:T(8,128)} %flags.3) | copy-start | bytes 786436
  6.2 4.2 %collective-permute-start = (f32[192,128]{1,0:T(8,128)S(1)}, f32[192,128]{1,0:T(8,128)S(1)}, u32[]{:S(2)}, u32[]{:S(2)}) collective-permute-start(f32[192,128]{1,0:T(8,128)S(1)} %get-tuple-element.18.own), channel_id=1, source_target_pairs={{1,0},{0,1},{3,2},{2,3},{5,4},{4,5},{7,6},{6,7},{9,8},{8,9},{11,10... | collective-permute-start | bytes 294920 | tf_op jit(solution)/shard_map/ppermute | solution.py:546
  9.5 4.3 %collective-permute-start.1 = (f32[192,128]{1,0:T(8,128)S(1)}, f32[192,128]{1,0:T(8,128)S(1)}, u32[]{:S(2)}, u32[]{:S(2)}) collective-permute-start(f32[192,128]{1,0:T(8,128)S(1)} %get-tuple-element.19), channel_id=1, source_target_pairs={{7,0},{2,1},{1,2},{4,3},{3,4},{6,5},{5,6},{0,7},{15,8},{10,9},{9,1... | collective-permute-start | bytes 294920 | tf_op jit(solution)/shard_map/ppermute | solution.py:546
  13.8 5.6 %collective-permute-start.3 = (f32[136,128]{1,0:T(8,128)S(1)}, f32[136,128]{1,0:T(8,128)S(1)}, u32[]{:S(2)}, u32[]{:S(2)}) collective-permute-start(f32[136,128]{1,0:T(8,128)S(1)} %join.1), channel_id=1, source_target_pairs={{8,0},{16,8},{24,16},{32,24},{40,32},{48,40},{56,48},{64,56},{72,6... | collective-permute-start | bytes 208904 | tf_op jit(solution)/shard_map/ppermute | solution.py:536
  18.1 6.5 %collective-permute-start.2 = (f32[136,128]{1,0:T(8,128)S(1)}, f32[136,128]{1,0:T(8,128)S(1)}, u32[]{:S(2)}, u32[]{:S(2)}) collective-permute-start(f32[136,128]{1,0:T(8,128)S(1)} %join.1), channel_id=1, source_target_pairs={{248,0},{0,8},{8,16},{16,24},{24,32},{32,40},{40,48},{48,56},{56,6... | collective-permute-start | bytes 208904 | tf_op jit(solution)/shard_map/ppermute | solution.py:536
  24.6 5.4 %collective-permute-start.6 = (f32[112,128]{1,0:T(8,128)S(1)}, f32[112,128]{1,0:T(8,128)S(1)}, u32[]{:S(2)}, u32[]{:S(2)}) collective-permute-start(f32[112,128]{1,0:T(8,128)S(1)} %compare_select_fusion.7.points_in), channel_id=1, source_target_pairs={{1,0},{0,1},{3,2},{2,3},{5,4},{4,5},{7,6},{6,7},{9,8},{8,9},{11,10... | collective-permute-start | bytes 172040 | tf_op jit(solution)/shard_map/ppermute | solution.py:546
  30.0 5.2 %collective-permute-start.7 = (f32[112,128]{1,0:T(8,128)S(1)}, f32[112,128]{1,0:T(8,128)S(1)}, u32[]{:S(2)}, u32[]{:S(2)}) collective-permute-start(f32[112,128]{1,0:T(8,128)S(1)} %compare_select_fusion.5), channel_id=1, source_target_pairs={{24,0},{233,1},{26,2},{235,3},{28,4},{237,5},{30,6},{239,7},{32,8}... | collective-permute-start | bytes 172040 | tf_op jit(solution)/shard_map/ppermute | solution.py:546
  35.2 1.6 %collective-permute-start.8 = (f32[112,128]{1,0:T(8,128)S(1)}, f32[112,128]{1,0:T(8,128)S(1)}, u32[]{:S(2)}, u32[]{:S(2)}) collective-permute-start(f32[112,128]{1,0:T(8,128)S(1)} %compare_select_fusion.4), channel_id=1, source_target_pairs={{1,0},{0,1},{3,2},{2,3},{5,4},{4,5},{7,6},{6,7},{9,8},{8,9},{11,10... | collective-permute-start | bytes 172040 | tf_op jit(solution)/shard_map/ppermute | solution.py:546
  36.8 5.9 %collective-permute-start.9 = (f32[112,128]{1,0:T(8,128)S(1)}, f32[112,128]{1,0:T(8,128)S(1)}, u32[]{:S(2)}, u32[]{:S(2)}) collective-permute-start(f32[112,128]{1,0:T(8,128)S(1)} %compare_select_fusion.3), channel_id=1, source_target_pairs={{56,0},{37,1},{58,2},{39,3},{60,4},{33,5},{62,6},{35,7},{64,8},{45... | collective-permute-start | bytes 172040 | tf_op jit(solution)/shard_map/ppermute | solution.py:546
  42.7 1.8 %collective-permute-start.10 = (f32[112,128]{1,0:T(8,128)S(1)}, f32[112,128]{1,0:T(8,128)S(1)}, u32[]{:S(2)}, u32[]{:S(2)}) collective-permute-start(f32[112,128]{1,0:T(8,128)S(1)} %compare_select_fusion.2), channel_id=1, source_target_pairs={{1,0},{0,1},{3,2},{2,3},{5,4},{4,5},{7,6},{6,7},{9,8},{8,9},{11,10... | collective-permute-start | bytes 172040 | tf_op jit(solution)/shard_map/ppermute | solution.py:546
  44.5 8.5 %collective-permute-start.11 = (f32[112,128]{1,0:T(8,128)S(1)}, f32[112,128]{1,0:T(8,128)S(1)}, u32[]{:S(2)}, u32[]{:S(2)}) collective-permute-start(f32[112,128]{1,0:T(8,128)S(1)} %compare_select_fusion.1), channel_id=1, source_target_pairs={{64,0},{165,1},{66,2},{167,3},{68,4},{161,5},{70,6},{163,7},{72,8}... | collective-permute-start | bytes 172040 | tf_op jit(solution)/shard_map/ppermute | solution.py:546
  44.6 13.6 %collective-permute-start.4 = (f32[10,64,128]{2,1,0:T(8,128)S(1)}, f32[10,64,128]{2,1,0:T(8,128)S(1)}, u32[]{:S(2)}, u32[]{:S(2)}) collective-permute-start(f32[10,64,128]{2,1,0:T(8,128)S(1)} %get-tuple-element.20), channel_id=1, source_target_pairs={{248,0},{0,8},{8,16},{16,24},{24,32},{32,40},{40,48},{48,56},{56,6... | collective-permute-start | bytes 983048 | tf_op jit(solution)/shard_map/ppermute | solution.py:536
  45.9 12.3 %collective-permute-start.5 = (f32[10,64,128]{2,1,0:T(8,128)S(1)}, f32[10,64,128]{2,1,0:T(8,128)S(1)}, u32[]{:S(2)}, u32[]{:S(2)}) collective-permute-start(f32[10,64,128]{2,1,0:T(8,128)S(1)} %get-tuple-element.21), channel_id=1, source_target_pairs={{8,0},{16,8},{24,16},{32,24},{40,32},{48,40},{56,48},{64,56},{72,6... | collective-permute-start | bytes 983048 | tf_op jit(solution)/shard_map/ppermute | solution.py:536
  53.0 11.0 %collective-permute-start.12 = (f32[112,128]{1,0:T(8,128)S(1)}, f32[112,128]{1,0:T(8,128)S(1)}, u32[]{:S(2)}, u32[]{:S(2)}) collective-permute-start(f32[112,128]{1,0:T(8,128)S(1)} %compare_select_fusion.mine), channel_id=1, source_target_pairs={{1,0},{0,1},{3,2},{2,3},{5,4},{4,5},{7,6},{6,7},{9,8},{8,9},{11,10... | collective-permute-start | bytes 172040 | tf_op jit(solution)/shard_map/ppermute | solution.py:546

commit v3 on v2

--- a/solution.py
+++ b/solution.py
@@ -45,7 +45,6 @@
 STEP_FLOPS = 60_000_000
 HBM = pl.BlockSpec(memory_space=pltpu.HBM)
 VMEM = pl.BlockSpec(memory_space=pltpu.VMEM)
-SMEM = pl.BlockSpec(memory_space=pltpu.SMEM)
 NT = (((1,), (1,)), ((), ()))
 NN = (((1,), (0,)), ((), ()))
 
@@ -60,6 +59,10 @@
     mid = rest.astype(BF16)
     low = (rest - mid.astype(F32)).astype(BF16)
     return high, mid, low
+
+
+def picked(table, lanes):
+    return jnp.take_along_axis(table, lanes, axis=1, mode="promise_in_bounds")
 
 
 def moments(g):
@@ -124,7 +127,7 @@
 def sample_kernel(
     gain_hbm, pops_hbm, flags_hbm, cells_hbm, turb_hbm, chord_hbm, blade_hbm,
     sibling, across, east, west, pops,
-    vhm, vl, sel, fld, m128, r128, dense, got_ref,
+    vhm, vl, sel, fld, m128, r128, got_ref,
     gain, flags, cells, turb, chord, blade, sems, in_sems,
 ):
     small = [
@@ -177,7 +180,6 @@
     for k in range(3):
         fld[4 + k : 5 + k, :] = ch[k].astype(F32)
         fld[7 + 3 * k : 10 + 3 * k, :] = bl[k].astype(F32)
-    dense[...] = jnp.zeros_like(dense)
     spots = lax.broadcasted_iota(jnp.int32, (CHUNK, LANES), 0).astype(F32)
 
     def choose(turn):
@@ -251,20 +253,22 @@
             rel.append(sampled - speed)
         size = jnp.sqrt(rel[0] * rel[0] + rel[1] * rel[1] + rel[2] * rel[2] + 0.0001)
         size = -(factor * size)
-        pieces = [split3(size * r) for r in rel]
-        stack = [pieces[c][k].astype(F32) for k in range(3) for c in range(3)]
-        stack = jnp.concatenate(stack + [jnp.zeros((7, CHUNK), F32)], axis=0).astype(BF16)
-        spread = dot(stack, sel[...])
-        dense[...] += spread[0:3] + spread[3:6] + spread[6:9]
+        for c in range(3):
+            value = size * rel[c]
+            low = jnp.broadcast_to(value[:, :LANES], (8, LANES))
+            high = jnp.broadcast_to(value[:, LANES:], (8, LANES))
+            for t in range(0, tiles, 8):
+                count_rows = min(8, tiles - t)
+                order = r128[t : t + 8, :].astype(jnp.int32) - turn * CHUNK
+                inside_chunk = (order >= 0) & (order < CHUNK)
+                spot = order & (LANES - 1)
+                got_value = jnp.where(order >= LANES, picked(high, spot), picked(low, spot))
+                at = slice(c * tiles + t, c * tiles + t + count_rows)
+                sibling[at, :] = jnp.where(inside_chunk, got_value, 0.0)[:count_rows] + sibling[at, :]
         return carry
 
+    sibling[0:112, :] = jnp.zeros((112, LANES), F32)
     lax.fori_loop(0, (count + CHUNK - 1) // CHUNK, chunk, 0)
-    for c in range(3):
-        for j in range(tiles):
-            sibling[c * tiles + j : c * tiles + j + 1, :] = dense[
-                c : c + 1, j * LANES : (j + 1) * LANES
-            ]
-    sibling[3 * tiles : 112, :] = jnp.zeros((112 - 3 * tiles, LANES), F32)
     across[0:112, :] = sibling[0:112, :]
 
 
@@ -297,7 +301,7 @@
 FY = 72
 
 
-READY = 2
+READY = 4
 
 
 def choose_points(rank, base, sel):
@@ -307,7 +311,7 @@
         sel[:, j * LANES : (j + 1) * LANES] = jnp.where(hit, 1.0, 0.0).astype(BF16)
 
 
-def prep_kernel(cells, sel, spot, rank, places, count_out, m128, *, total_x, total_y):
+def prep_kernel(cells, spot, rank, places, sel, m128, *, total_x, total_y):
     points = cells.shape[1]
     tiles = points // LANES
 
@@ -333,24 +337,27 @@
     ahead = jnp.sum(dot(above, maskb), axis=1, keepdims=True)
     rank[...] = jnp.where(mask > 0.0, inside + ahead, -1.0)
     count = jnp.sum(mask).astype(jnp.int32)
-    count_out[0] = count
     places[0:1, :] = px.astype(F32)
     places[1:2, :] = py.astype(F32)
     places[2:3, :] = cells[2:3, :].astype(F32)
-    places[3:8, :] = jnp.zeros((5, points), F32)
-    for k in range(READY):
-
-        @pl.when(count > k * CHUNK)
-        def _():
-            chosen = sel.at[k]
-            choose_points(rank, float(k * CHUNK), chosen)
-            spot[k] = dot(places[...].astype(BF16), chosen[...], NT)
-
-
-def force_kernel(sel_in, spot_in, rank, places, count_in, points_in, out, sel, fld):
-    points = fld.shape[1]
-    tiles = points // LANES
-    count = count_in[0]
+    number = lax.broadcasted_iota(jnp.int32, (1, points), 1)
+    places[3:4, :] = (number // LANES).astype(F32)
+    places[4:5, :] = (number % LANES).astype(F32)
+    places[5:6, :] = jnp.ones((1, points), F32)
+    places[6:8, :] = jnp.zeros((2, points), F32)
+
+    def chunk(turn, carry):
+        choose_points(rank, (turn * CHUNK).astype(F32), sel)
+        spot[turn] = dot(places[...].astype(BF16), sel[...], NT)
+        return carry
+
+    lax.fori_loop(0, jnp.minimum((count + CHUNK - 1) // CHUNK, READY), chunk, 0)
+    spot[READY] = jnp.broadcast_to(count.astype(F32), (8, CHUNK))
+
+
+def force_kernel(spot_in, rank, places, points_in, out, sel, late):
+    tiles = places.shape[1] // LANES
+    count = jnp.max(spot_in[READY, 0:1, 0:LANES]).astype(jnp.int32)
     out[...] = jnp.zeros_like(out)
 
     def kernel_value(cell, point):
@@ -362,55 +369,57 @@
     def iota(size):
         return lax.broadcasted_iota(jnp.int32, (size, CHUNK), 0).astype(F32)
 
-    def spread(chosen, spot):
-        got = dot(fld[...].astype(BF16), chosen, NT)
+    row_ids = lax.broadcasted_iota(jnp.int32, (8, LANES), 0)
+
+    def spread(spot):
+        forces = []
+        for c in range(3):
+            halves = []
+            for h in range(0, CHUNK, LANES):
+                row = jnp.broadcast_to(spot[3:4, h : h + LANES].astype(jnp.int32), (8, LANES))
+                lane = jnp.broadcast_to(spot[4:5, h : h + LANES].astype(jnp.int32), (8, LANES))
+                total = jnp.zeros((8, LANES), F32)
+                for t in range(c * tiles // 8, ((c + 1) * tiles - 1) // 8 + 1):
+                    value = picked(points_in[8 * t : 8 * t + 8, :], lane)
+                    total = jnp.where(row_ids + (8 * t - c * tiles) == row, value, total)
+                halves.append(jnp.sum(total, axis=0, keepdims=True))
+            force = jnp.concatenate(halves, axis=1)
+            forces.append(jnp.where(spot[5:6] > 0.5, force, 0.0))
         kx = kernel_value(iota(16) - 1.0, spot[0:1])
         ky = kernel_value(iota(FY) - 1.0, spot[1:2])
         kz = kernel_value(iota(LANES), spot[2:3])
-        left = jnp.concatenate(
-            [(got[c : 1 + c] + got[3 + c : 4 + c] + got[6 + c : 7 + c]) * ky for c in range(3)],
-            axis=0,
-        )
+        left = jnp.concatenate([f * ky for f in forces], axis=0)
         left_high = left.astype(BF16)
         left_low = (left - left_high.astype(F32)).astype(BF16)
+        left_both = jnp.concatenate([left_high, left_low], axis=0)
+        lines = 3 * FY
         for x in range(0, CX + 2, 2):
             right = jnp.concatenate([kx[x : x + 1] * kz, kx[x + 1 : x + 2] * kz], axis=0)
             right_high = right.astype(BF16)
             right_low = (right - right_high.astype(F32)).astype(BF16)
-            field = dot(left_high, right_high, NT) + (
-                dot(left_high, right_low, NT) + dot(left_low, right_high, NT)
-            )
+            both = dot(left_both, right_high, NT)
+            field = both[:lines] + (dot(left_high, right_low, NT) + both[lines:])
             for c in range(3):
                 part = field[c * FY : (c + 1) * FY]
                 out[c, x, :, :] += part[:, :LANES]
                 out[c, x + 1, :, :] += part[:, LANES:]
 
-    @pl.when(count > 0)
-    def _():
-        pieces = split3(points_in[0:112, :])
-        for k in range(3):
-            piece = pieces[k].astype(F32)
-            for c in range(3):
-                for j in range(tiles):
-                    fld[3 * k + c : 1 + 3 * k + c, j * LANES : (j + 1) * LANES] = piece[
-                        c * tiles + j : c * tiles + j + 1, :
-                    ]
-        fld[9:16, :] = jnp.zeros((7, points), F32)
-
-    ready = (jnp.minimum(count, READY * CHUNK) + CHUNK - 1) // CHUNK
+    chunks = (count + CHUNK - 1) // CHUNK
 
     def chunk(turn, carry):
-        spread(sel_in[turn], spot_in[turn])
+        @pl.when(turn >= READY)
+        def _():
+            choose_points(rank, (turn * CHUNK).astype(F32), sel)
+            late[...] = dot(places[...].astype(BF16), sel[...], NT)
+
+        @pl.when(turn < READY)
+        def _():
+            late[...] = spot_in[turn]
+
+        spread(late[...])
         return carry
 
-    lax.fori_loop(0, ready, chunk, 0)
-
-    def late(turn, carry):
-        choose_points(rank, (turn * CHUNK).astype(F32), sel)
-        spread(sel[...], dot(places[...].astype(BF16), sel[...], NT))
-        return carry
-
-    lax.fori_loop(READY, (count + CHUNK - 1) // CHUNK, late, 0)
+    lax.fori_loop(0, chunks, chunk, 0)
 
 
 OY = 8
@@ -588,7 +597,6 @@
             pltpu.VMEM((3 * CX * CY, 2 * LANES), BF16),
             pltpu.VMEM((3 * CX * CY, LANES), BF16),
             *compact,
-            pltpu.VMEM((3, points), F32),
             pltpu.VMEM((16, CHUNK), F32),
             pltpu.SMEM(turbine_gain.shape, F32),
             pltpu.VMEM(solid_flags.shape, jnp.int32),
@@ -628,15 +636,13 @@
     prepared = pl.pallas_call(
         functools.partial(prep_kernel, total_x=total_x, total_y=total_y),
         out_shape=(
-            sds((READY, CHUNK, points), BF16),
-            sds((READY, 8, CHUNK), F32),
+            sds((READY + 1, 8, CHUNK), F32),
             sds((LANES, LANES), F32),
             sds((8, points), F32),
-            sds((1,), jnp.int32),
         ),
         in_specs=[VMEM],
-        out_specs=(VMEM, VMEM, VMEM, VMEM, SMEM),
-        scratch_shapes=[pltpu.VMEM((LANES, LANES), F32)],
+        out_specs=(VMEM, VMEM, VMEM),
+        scratch_shapes=[pltpu.VMEM((CHUNK, points), BF16), pltpu.VMEM((LANES, LANES), F32)],
         compiler_params=params,
         cost_estimate=cost(FORCE_FLOPS),
         name="prep",
@@ -644,9 +650,9 @@
     force = pl.pallas_call(
         force_kernel,
         out_shape=sds((3, CX + 2, FY, LANES), F32),
-        in_specs=[VMEM, VMEM, VMEM, VMEM, SMEM, VMEM],
+        in_specs=[VMEM] * 4,
         out_specs=VMEM,
-        scratch_shapes=[pltpu.VMEM((CHUNK, points), BF16), pltpu.VMEM((16, points), F32)],
+        scratch_shapes=[pltpu.VMEM((CHUNK, points), BF16), pltpu.VMEM((8, CHUNK), F32)],
         compiler_params=params,
         cost_estimate=cost(FORCE_FLOPS),
         name="force",

time: 65.1 us -> 64.2 us (0.986)
  Pallas kernels: 16.9 us -> 13.5 us
  waiting for transfers between devices: 28.1 us -> 31 us
    ppermute x4, waiting for transfers between devices: 6.6 us -> 9.51 us  [from_behind(): lax.ppermute(block, axis, [((i - distance) % count, i) for i in range(cou...]
    pallas_call x1, Pallas kernels: 3.23 us -> 0.91 us  [local(): pl.pallas_call(force_kernel, out_shape=sds((3, CX + 2, FY, LANES), F32),...]
  transfers between devices with their start and end apart: 13 -> 13, of which waited for: 11 -> 11; matrix products, arithmetic and copies ran while one was open for 0% -> 0% of each run, Pallas kernels for 17% -> 12%
where the time goes in v3:
time: 64.2 us; the launch traced here: 64.1 us
  waiting for transfers between devices  31 us (48%)
  starting transfers between devices  18.8 us (29%)
  Pallas kernels  13.5 us (21%)
  between operations  0.76 us (1%)
    ppermute x9, waiting for transfers between devices, exchanged(): return lax.ppermute(block, ('gx', 'gy'), pairs)  21.5 us
    ppermute x4, starting transfers between devices, from_behind(): lax.ppermute(block, axis, [((i - distance) % count, i) for i in range(cou...  9.62 us
    ppermute x4, waiting for transfers between devices, from_behind(): lax.ppermute(block, axis, [((i - distance) % count, i) for i in range(cou...  9.51 us
    ppermute x9, starting transfers between devices, exchanged(): return lax.ppermute(block, ('gx', 'gy'), pairs)  9.17 us
    pallas_call x2, Pallas kernels, local(): pl.pallas_call(functools.partial(step_kernel, low=low, high=high), out_sh...  5.77 us
    pallas_call x1, Pallas kernels, local(): pl.pallas_call(sample_kernel, out_shape=(sds((192, LANES), F32), sds((192...  4.97 us
  transfers between devices with their start and end apart: 13, of which 11 were waited for; matrix products, arithmetic and copies ran while one was open for 0% of the time, Pallas kernels for 12%

profile of v3, /device:TPU:1, one launch (start us, length us, event | category | flops | bytes accessed | tf_op | source)
XLA Modules:
  0.0 64.1 jit_solution(7914935464193121210)
XLA Ops:
  0.7 5.0 %sample.1 = (f32[192,128]{1,0:T(8,128)S(1)}, f32[192,128]{1,0:T(8,128)S(1)}, f32[10,64,128]{2,1,0:T(8,128)S(1)}, f32[10,64,128]{2,1,0:T(8,128)S(1)}, f32[19,8,64,128]{3,2,1,0:T(8,128)S(1)}) custom-call(f32[24]{0:T(128)} %gain_hbm.1, f32[19,8,64,128]{3,2,1,0:T(8,128)} %pops_hbm.1, s32[8,64,128]{2,1,0:T(8,128)} %flags.3, s32[3,4608]{1,0:T(4,128)} %cells.1, ...), custom_call_target="tpu_custom_call" | custom-call | tf_op jit(solution)/shard_map/sample/pallas_call | solution.py:585
  5.6 3.3 %collective-permute-start = (f32[192,128]{1,0:T(8,128)S(1)}, f32[192,128]{1,0:T(8,128)S(1)}, u32[]{:S(2)}, u32[]{:S(2)}) collective-permute-start(f32[192,128]{1,0:T(8,128)S(1)} %get-tuple-element.14.own), channel_id=1, source_target_pairs={{1,0},{0,1},{3,2},{2,3},{5,4},{4,5},{7,6},{6,7},{9,8},{8,9},{11,10... | collective-permute-start | bytes 294920 | tf_op jit(solution)/shard_map/ppermute | solution.py:555
  8.9 0.9 %collective-permute-done.beside = f32[192,128]{1,0:T(8,128)S(1)} collective-permute-done((f32[192,128]{1,0:T(8,128)S(1)}, f32[192,128]{1,0:T(8,128)S(1)}, u32[]{:S(2)}, u32[]{:S(2)}) %collective-permute-start) | collective-permute-done | bytes 98336 | tf_op jit(solution)/shard_map/ppermute | solution.py:555
  9.9 3.4 %collective-permute-done.1.beyond = f32[192,128]{1,0:T(8,128)S(1)} collective-permute-done((f32[192,128]{1,0:T(8,128)S(1)}, f32[192,128]{1,0:T(8,128)S(1)}, u32[]{:S(2)}, u32[]{:S(2)}) %collective-permute-start.1) | collective-permute-done | bytes 98336 | tf_op jit(solution)/shard_map/ppermute | solution.py:555
  13.3 4.8 %collective-permute-start.3 = (f32[136,128]{1,0:T(8,128)S(1)}, f32[136,128]{1,0:T(8,128)S(1)}, u32[]{:S(2)}, u32[]{:S(2)}) collective-permute-start(f32[136,128]{1,0:T(8,128)S(1)} %join.1), channel_id=1, source_target_pairs={{8,0},{16,8},{24,16},{32,24},{40,32},{48,40},{56,48},{64,56},{72,6... | collective-permute-start | bytes 208904 | tf_op jit(solution)/shard_map/ppermute | solution.py:545
  18.0 1.4 %collective-permute-done.3.east_pts = f32[136,128]{1,0:T(8,128)S(1)} collective-permute-done((f32[136,128]{1,0:T(8,128)S(1)}, f32[136,128]{1,0:T(8,128)S(1)}, u32[]{:S(2)}, u32[]{:S(2)}) %collective-permute-start.3) | collective-permute-done | bytes 69664 | tf_op jit(solution)/shard_map/ppermute | solution.py:545
  19.4 5.1 %collective-permute-done.2.west_pts = f32[136,128]{1,0:T(8,128)S(1)} collective-permute-done((f32[136,128]{1,0:T(8,128)S(1)}, f32[136,128]{1,0:T(8,128)S(1)}, u32[]{:S(2)}, u32[]{:S(2)}) %collective-permute-start.2) | collective-permute-done | bytes 69664 | tf_op jit(solution)/shard_map/ppermute | solution.py:545
  24.5 4.0 %collective-permute-start.6 = (f32[112,128]{1,0:T(8,128)S(1)}, f32[112,128]{1,0:T(8,128)S(1)}, u32[]{:S(2)}, u32[]{:S(2)}) collective-permute-start(f32[112,128]{1,0:T(8,128)S(1)} %compare_select_fusion.7.points_in), channel_id=1, source_target_pairs={{1,0},{0,1},{3,2},{2,3},{5,4},{4,5},{7,6},{6,7},{9,8},{8,9},{11,10... | collective-permute-start | bytes 172040 | tf_op jit(solution)/shard_map/ppermute | solution.py:555
  28.5 0.9 %collective-permute-done.6 = f32[112,128]{1,0:T(8,128)S(1)} collective-permute-done((f32[112,128]{1,0:T(8,128)S(1)}, f32[112,128]{1,0:T(8,128)S(1)}, u32[]{:S(2)}, u32[]{:S(2)}) %collective-permute-start.6) | collective-permute-done | bytes 57376 | tf_op jit(solution)/shard_map/ppermute | solution.py:555
  29.5 5.1 %collective-permute-done.7 = f32[112,128]{1,0:T(8,128)S(1)} collective-permute-done((f32[112,128]{1,0:T(8,128)S(1)}, f32[112,128]{1,0:T(8,128)S(1)}, u32[]{:S(2)}, u32[]{:S(2)}) %collective-permute-start.7) | collective-permute-done | bytes 57376 | tf_op jit(solution)/shard_map/ppermute | solution.py:555
  34.6 0.7 %collective-permute-start.8 = (f32[112,128]{1,0:T(8,128)S(1)}, f32[112,128]{1,0:T(8,128)S(1)}, u32[]{:S(2)}, u32[]{:S(2)}) collective-permute-start(f32[112,128]{1,0:T(8,128)S(1)} %compare_select_fusion.4), channel_id=1, source_target_pairs={{1,0},{0,1},{3,2},{2,3},{5,4},{4,5},{7,6},{6,7},{9,8},{8,9},{11,10... | collective-permute-start | bytes 172040 | tf_op jit(solution)/shard_map/ppermute | solution.py:555
  35.3 0.9 %collective-permute-done.8 = f32[112,128]{1,0:T(8,128)S(1)} collective-permute-done((f32[112,128]{1,0:T(8,128)S(1)}, f32[112,128]{1,0:T(8,128)S(1)}, u32[]{:S(2)}, u32[]{:S(2)}) %collective-permute-start.8) | collective-permute-done | bytes 57376 | tf_op jit(solution)/shard_map/ppermute | solution.py:555
  36.3 5.8 %collective-permute-done.9 = f32[112,128]{1,0:T(8,128)S(1)} collective-permute-done((f32[112,128]{1,0:T(8,128)S(1)}, f32[112,128]{1,0:T(8,128)S(1)}, u32[]{:S(2)}, u32[]{:S(2)}) %collective-permute-start.9) | collective-permute-done | bytes 57376 | tf_op jit(solution)/shard_map/ppermute | solution.py:555
  42.1 0.9 %collective-permute-start.10 = (f32[112,128]{1,0:T(8,128)S(1)}, f32[112,128]{1,0:T(8,128)S(1)}, u32[]{:S(2)}, u32[]{:S(2)}) collective-permute-start(f32[112,128]{1,0:T(8,128)S(1)} %compare_select_fusion.2), channel_id=1, source_target_pairs={{1,0},{0,1},{3,2},{2,3},{5,4},{4,5},{7,6},{6,7},{9,8},{8,9},{11,10... | collective-permute-start | bytes 172040 | tf_op jit(solution)/shard_map/ppermute | solution.py:555
  43.1 0.9 %collective-permute-done.10 = f32[112,128]{1,0:T(8,128)S(1)} collective-permute-done((f32[112,128]{1,0:T(8,128)S(1)}, f32[112,128]{1,0:T(8,128)S(1)}, u32[]{:S(2)}, u32[]{:S(2)}) %collective-permute-start.10) | collective-permute-done | bytes 57376 | tf_op jit(solution)/shard_map/ppermute | solution.py:555
  44.0 1.8 %collective-permute-start.4 = (f32[10,64,128]{2,1,0:T(8,128)S(1)}, f32[10,64,128]{2,1,0:T(8,128)S(1)}, u32[]{:S(2)}, u32[]{:S(2)}) collective-permute-start(f32[10,64,128]{2,1,0:T(8,128)S(1)} %get-tuple-element.16), channel_id=1, source_target_pairs={{248,0},{0,8},{8,16},{16,24},{24,32},{32,40},{40,48},{48,56},{56,6... | collective-permute-start | bytes 983048 | tf_op jit(solution)/shard_map/ppermute | solution.py:545
  45.8 3.1 %collective-permute-start.5 = (f32[10,64,128]{2,1,0:T(8,128)S(1)}, f32[10,64,128]{2,1,0:T(8,128)S(1)}, u32[]{:S(2)}, u32[]{:S(2)}) collective-permute-start(f32[10,64,128]{2,1,0:T(8,128)S(1)} %get-tuple-element.17), channel_id=1, source_target_pairs={{8,0},{16,8},{24,16},{32,24},{40,32},{48,40},{56,48},{64,56},{72,6... | collective-permute-start | bytes 983048 | tf_op jit(solution)/shard_map/ppermute | solution.py:545
  48.9 3.6 %collective-permute-done.11 = f32[112,128]{1,0:T(8,128)S(1)} collective-permute-done((f32[112,128]{1,0:T(8,128)S(1)}, f32[112,128]{1,0:T(8,128)S(1)}, u32[]{:S(2)}, u32[]{:S(2)}) %collective-permute-start.11) | collective-permute-done | bytes 57376 | tf_op jit(solution)/shard_map/ppermute | solution.py:555
  52.6 1.1 %prep.1 = (f32[5,8,256]{2,1,0:T(8,128)S(1)}, f32[128,128]{1,0:T(8,128)S(1)}, f32[8,4608]{1,0:T(8,128)S(1)}) custom-call(s32[3,4608]{1,0:T(4,128)S(1)} %copy-done.1), custom_call_target="tpu_custom_call" | custom-call | flops 40000000 | tf_op jit(solution)/shard_map/prep/pallas_call | solution.py:636
  53.7 0.9 %force.1 = f32[3,10,72,128]{3,2,1,0:T(8,128)S(1)} custom-call(f32[5,8,256]{2,1,0:T(8,128)S(1)} %get-tuple-element.11.spot_in, f32[128,128]{1,0:T(8,128)S(1)} %get-tuple-element.12.rank, f32[8,4608]{1,0:T(8,128)S(1)} %get-tuple-element.13.places, f32[112,128]{1,0:T(8,128)S(1)} %compare_select_fusion.7.points_in), custom_call_target="tpu_custom_call" | custom-call | flops 40000000 | tf_op jit(solution)/shard_map/force/pallas_call | solution.py:650
  54.6 3.0 %collective-permute-done.4.from_west = f32[10,64,128]{2,1,0:T(8,128)S(1)} collective-permute-done((f32[10,64,128]{2,1,0:T(8,128)S(1)}, f32[10,64,128]{2,1,0:T(8,128)S(1)}, u32[]{:S(2)}, u32[]{:S(2)}) %collective-permute-start.4) | collective-permute-done | bytes 327712 | tf_op jit(solution)/shard_map/ppermute | solution.py:545
  57.6 2.9 %shard_map.86.rest_0_ = f32[19,8,64,128]{3,2,1,0:T(8,128)} custom-call(f32[19,8,64,128]{3,2,1,0:T(8,128)S(1)} %get-tuple-element.10.pops, s32[8,64,128]{2,1,0:T(8,128)S(1)} %copy-done, f32[3,10,72,128]{3,2,1,0:T(8,128)S(1)} %force.1, f32[10,64,128]{2,1,0:T(8,128)S(1)} %collective-permute-done.4.from_west, ...), custom_call_target="tpu_custom_call" | custom-call | flops 60000000 | tf_op jit(solution)/shard_map/pallas_call | solution.py:666
  60.5 2.9 %shard_map.87 = f32[19,8,64,128]{3,2,1,0:T(8,128)} custom-call(f32[19,8,64,128]{3,2,1,0:T(8,128)S(1)} %get-tuple-element.10.pops, s32[8,64,128]{2,1,0:T(8,128)S(1)} %copy-done, f32[3,10,72,128]{3,2,1,0:T(8,128)S(1)} %force.1, f32[10,64,128]{2,1,0:T(8,128)S(1)} %collective-permute-done.4.from_west, ...), custom_call_target="tpu_custom_call", output_to_operand_aliasing={{}: (9, {})} | custom-call | flops 60000000 | tf_op jit(solution)/shard_map/pallas_call | solution.py:666
  63.4 0.7 %finish.1 = f32[3,4608]{1,0:T(4,128)} custom-call(f32[112,128]{1,0:T(8,128)S(1)} %compare_select_fusion.mine, f32[112,128]{1,0:T(8,128)S(1)} %collective-permute-done.12.other), custom_call_target="tpu_custom_call" | custom-call | tf_op jit(solution)/shard_map/finish/pallas_call | solution.py:689
  (20 shorter events, 0.3 us)
Async XLA Ops:
  0.6 57.0 %copy-start = (s32[8,64,128]{2,1,0:T(8,128)S(1)}, s32[8,64,128]{2,1,0:T(8,128)}, u32[]{:S(2)}) copy-start(s32[8,64,128]{2,1,0:T(8,128)} %flags.3) | copy-start | bytes 786436
  0.6 51.9 %copy-start.1 = (s32[3,4608]{1,0:T(4,128)S(1)}, s32[3,4608]{1,0:T(4,128)}, u32[]{:S(2)}) copy-start(s32[3,4608]{1,0:T(4,128)} %cells.1) | copy-start | bytes 165892
  5.6 4.2 %collective-permute-start = (f32[192,128]{1,0:T(8,128)S(1)}, f32[192,128]{1,0:T(8,128)S(1)}, u32[]{:S(2)}, u32[]{:S(2)}) collective-permute-start(f32[192,128]{1,0:T(8,128)S(1)} %get-tuple-element.14.own), channel_id=1, source_target_pairs={{1,0},{0,1},{3,2},{2,3},{5,4},{4,5},{7,6},{6,7},{9,8},{8,9},{11,10... | collective-permute-start | bytes 294920 | tf_op jit(solution)/shard_map/ppermute | solution.py:555
  8.9 4.3 %collective-permute-start.1 = (f32[192,128]{1,0:T(8,128)S(1)}, f32[192,128]{1,0:T(8,128)S(1)}, u32[]{:S(2)}, u32[]{:S(2)}) collective-permute-start(f32[192,128]{1,0:T(8,128)S(1)} %get-tuple-element.15), channel_id=1, source_target_pairs={{7,0},{2,1},{1,2},{4,3},{3,4},{6,5},{5,6},{0,7},{15,8},{10,9},{9,1... | collective-permute-start | bytes 294920 | tf_op jit(solution)/shard_map/ppermute | solution.py:555
  13.3 6.1 %collective-permute-start.3 = (f32[136,128]{1,0:T(8,128)S(1)}, f32[136,128]{1,0:T(8,128)S(1)}, u32[]{:S(2)}, u32[]{:S(2)}) collective-permute-start(f32[136,128]{1,0:T(8,128)S(1)} %join.1), channel_id=1, source_target_pairs={{8,0},{16,8},{24,16},{32,24},{40,32},{48,40},{56,48},{64,56},{72,6... | collective-permute-start | bytes 208904 | tf_op jit(solution)/shard_map/ppermute | solution.py:545
  18.0 6.5 %collective-permute-start.2 = (f32[136,128]{1,0:T(8,128)S(1)}, f32[136,128]{1,0:T(8,128)S(1)}, u32[]{:S(2)}, u32[]{:S(2)}) collective-permute-start(f32[136,128]{1,0:T(8,128)S(1)} %join.1), channel_id=1, source_target_pairs={{248,0},{0,8},{8,16},{16,24},{24,32},{32,40},{40,48},{48,56},{56,6... | collective-permute-start | bytes 208904 | tf_op jit(solution)/shard_map/ppermute | solution.py:545
  24.5 4.9 %collective-permute-start.6 = (f32[112,128]{1,0:T(8,128)S(1)}, f32[112,128]{1,0:T(8,128)S(1)}, u32[]{:S(2)}, u32[]{:S(2)}) collective-permute-start(f32[112,128]{1,0:T(8,128)S(1)} %compare_select_fusion.7.points_in), channel_id=1, source_target_pairs={{1,0},{0,1},{3,2},{2,3},{5,4},{4,5},{7,6},{6,7},{9,8},{8,9},{11,10... | collective-permute-start | bytes 172040 | tf_op jit(solution)/shard_map/ppermute | solution.py:555
  29.4 5.2 %collective-permute-start.7 = (f32[112,128]{1,0:T(8,128)S(1)}, f32[112,128]{1,0:T(8,128)S(1)}, u32[]{:S(2)}, u32[]{:S(2)}) collective-permute-start(f32[112,128]{1,0:T(8,128)S(1)} %compare_select_fusion.5), channel_id=1, source_target_pairs={{24,0},{233,1},{26,2},{235,3},{28,4},{237,5},{30,6},{239,7},{32,8}... | collective-permute-start | bytes 172040 | tf_op jit(solution)/shard_map/ppermute | solution.py:555
  34.6 1.6 %collective-permute-start.8 = (f32[112,128]{1,0:T(8,128)S(1)}, f32[112,128]{1,0:T(8,128)S(1)}, u32[]{:S(2)}, u32[]{:S(2)}) collective-permute-start(f32[112,128]{1,0:T(8,128)S(1)} %compare_select_fusion.4), channel_id=1, source_target_pairs={{1,0},{0,1},{3,2},{2,3},{5,4},{4,5},{7,6},{6,7},{9,8},{8,9},{11,10... | collective-permute-start | bytes 172040 | tf_op jit(solution)/shard_map/ppermute | solution.py:555
  36.2 5.9 %collective-permute-start.9 = (f32[112,128]{1,0:T(8,128)S(1)}, f32[112,128]{1,0:T(8,128)S(1)}, u32[]{:S(2)}, u32[]{:S(2)}) collective-permute-start(f32[112,128]{1,0:T(8,128)S(1)} %compare_select_fusion.3), channel_id=1, source_target_pairs={{56,0},{37,1},{58,2},{39,3},{60,4},{33,5},{62,6},{35,7},{64,8},{45... | collective-permute-start | bytes 172040 | tf_op jit(solution)/shard_map/ppermute | solution.py:555
  42.1 1.8 %collective-permute-start.10 = (f32[112,128]{1,0:T(8,128)S(1)}, f32[112,128]{1,0:T(8,128)S(1)}, u32[]{:S(2)}, u32[]{:S(2)}) collective-permute-start(f32[112,128]{1,0:T(8,128)S(1)} %compare_select_fusion.2), channel_id=1, source_target_pairs={{1,0},{0,1},{3,2},{2,3},{5,4},{4,5},{7,6},{6,7},{9,8},{8,9},{11,10... | collective-permute-start | bytes 172040 | tf_op jit(solution)/shard_map/ppermute | solution.py:555
  44.0 8.5 %collective-permute-start.11 = (f32[112,128]{1,0:T(8,128)S(1)}, f32[112,128]{1,0:T(8,128)S(1)}, u32[]{:S(2)}, u32[]{:S(2)}) collective-permute-start(f32[112,128]{1,0:T(8,128)S(1)} %compare_select_fusion.1), channel_id=1, source_target_pairs={{64,0},{165,1},{66,2},{167,3},{68,4},{161,5},{70,6},{163,7},{72,8}... | collective-permute-start | bytes 172040 | tf_op jit(solution)/shard_map/ppermute | solution.py:555
  44.0 13.6 %collective-permute-start.4 = (f32[10,64,128]{2,1,0:T(8,128)S(1)}, f32[10,64,128]{2,1,0:T(8,128)S(1)}, u32[]{:S(2)}, u32[]{:S(2)}) collective-permute-start(f32[10,64,128]{2,1,0:T(8,128)S(1)} %get-tuple-element.16), channel_id=1, source_target_pairs={{248,0},{0,8},{8,16},{16,24},{24,32},{32,40},{40,48},{48,56},{56,6... | collective-permute-start | bytes 983048 | tf_op jit(solution)/shard_map/ppermute | solution.py:545
  45.8 11.8 %collective-permute-start.5 = (f32[10,64,128]{2,1,0:T(8,128)S(1)}, f32[10,64,128]{2,1,0:T(8,128)S(1)}, u32[]{:S(2)}, u32[]{:S(2)}) collective-permute-start(f32[10,64,128]{2,1,0:T(8,128)S(1)} %get-tuple-element.17), channel_id=1, source_target_pairs={{8,0},{16,8},{24,16},{32,24},{40,32},{48,40},{56,48},{64,56},{72,6... | collective-permute-start | bytes 983048 | tf_op jit(solution)/shard_map/ppermute | solution.py:545
  52.4 11.0 %collective-permute-start.12 = (f32[112,128]{1,0:T(8,128)S(1)}, f32[112,128]{1,0:T(8,128)S(1)}, u32[]{:S(2)}, u32[]{:S(2)}) collective-permute-start(f32[112,128]{1,0:T(8,128)S(1)} %compare_select_fusion.mine), channel_id=1, source_target_pairs={{1,0},{0,1},{3,2},{2,3},{5,4},{4,5},{7,6},{6,7},{9,8},{8,9},{11,10... | collective-permute-start | bytes 172040 | tf_op jit(solution)/shard_map/ppermute | solution.py:555

commit v4 on v3

--- a/solution.py
+++ b/solution.py
@@ -124,11 +124,33 @@
 KEEP = 1.0 - 1.0 / RELAX
 
 
-def sample_kernel(
+def choose_points(rank, base, sel):
+    spots = lax.broadcasted_iota(jnp.int32, (CHUNK, LANES), 0).astype(F32)
+    for j in range(sel.shape[1] // LANES):
+        hit = rank[j : j + 1, :] - base == spots
+        sel[:, j * LANES : (j + 1) * LANES] = jnp.where(hit, 1.0, 0.0).astype(BF16)
+
+
+def number_points(wanted, m128, rank):
+    m128[...] = jnp.zeros_like(m128)
+    for j in range(wanted.shape[1] // LANES):
+        m128[j : j + 1, :] = wanted[:, j * LANES : (j + 1) * LANES]
+    mask = m128[...]
+    maskb = mask.astype(BF16)
+    rows = lax.broadcasted_iota(jnp.int32, (LANES, LANES), 0)
+    cols = lax.broadcasted_iota(jnp.int32, (LANES, LANES), 1)
+    before = jnp.where(rows < cols, 1.0, 0.0).astype(BF16)
+    above = jnp.where(rows > cols, 1.0, 0.0).astype(BF16)
+    inside = dot(maskb, before)
+    ahead = jnp.sum(dot(above, maskb), axis=1, keepdims=True)
+    rank[...] = jnp.where(mask > 0.0, inside + ahead, -1.0)
+    return jnp.sum(mask).astype(jnp.int32)
+
+
+def dense_kernel(
     gain_hbm, pops_hbm, flags_hbm, cells_hbm, turb_hbm, chord_hbm, blade_hbm,
-    sibling, across, east, west, pops,
-    vhm, vl, sel, fld, m128, r128, got_ref,
-    gain, flags, cells, turb, chord, blade, sems, in_sems,
+    sibling, across, east, west, pops, vhm, vl, fld, r128, got_ref,
+    sel, m128, gain, flags, cells, turb, chord, blade, sems, in_sems,
 ):
     small = [
         pltpu.make_async_copy(src, dst, in_sems.at[k])
@@ -148,7 +170,6 @@
     for x in range(CX):
         pltpu.make_async_copy(pops_hbm.at[:, x], pops.at[:, x], sems.at[x]).start()
     points = cells.shape[1]
-    tiles = points // LANES
     start_x, start_y = lax.axis_index("gx") * CX, lax.axis_index("gy") * CY
     even = lax.axis_index("gy") % 2 == 0
     for copy in small[:5]:
@@ -156,42 +177,25 @@
     px = cells[0:1, :] - start_x
     py = cells[1:2, :] - start_y
     own = (px >= 0) & (px < CX) & (py >= 0) & (py < CY)
-    own = jnp.where(own, 1.0, 0.0)
-    m128[...] = jnp.zeros_like(m128)
-    for j in range(tiles):
-        m128[j : j + 1, :] = own[:, j * LANES : (j + 1) * LANES]
-    mask = m128[...]
-    maskb = mask.astype(BF16)
-    rows = lax.broadcasted_iota(jnp.int32, (LANES, LANES), 0)
-    cols = lax.broadcasted_iota(jnp.int32, (LANES, LANES), 1)
-    before = jnp.where(rows < cols, 1.0, 0.0).astype(BF16)
-    above = jnp.where(rows > cols, 1.0, 0.0).astype(BF16)
-    inside = dot(maskb, before)
-    ahead = jnp.sum(dot(above, maskb), axis=1, keepdims=True)
-    r128[...] = jnp.where(mask > 0.0, inside + ahead, -1.0)
-    count = jnp.sum(mask).astype(jnp.int32)
-
-    fld[0:1, :] = px.astype(F32)
-    fld[1:2, :] = py.astype(F32)
-    fld[2:3, :] = cells[2:3, :].astype(F32)
-    fld[3:4, :] = turb[...].astype(F32)
-    ch = split3(chord[...])
-    bl = split3(blade[...])
-    for k in range(3):
-        fld[4 + k : 5 + k, :] = ch[k].astype(F32)
-        fld[7 + 3 * k : 10 + 3 * k, :] = bl[k].astype(F32)
-    spots = lax.broadcasted_iota(jnp.int32, (CHUNK, LANES), 0).astype(F32)
-
-    def choose(turn):
-        base = (turn * CHUNK).astype(F32) if not isinstance(turn, int) else 0.0
-        for j in range(tiles):
-            hit = r128[j : j + 1, :] - base == spots
-            sel[:, j * LANES : (j + 1) * LANES] = jnp.where(hit, 1.0, 0.0).astype(BF16)
-        got_ref[...] = dot(fld[...].astype(BF16), sel[...], NT)
+    count = number_points(jnp.where(own, 1.0, 0.0), m128, r128)
 
     @pl.when(count > 0)
     def _():
-        choose(0)
+        fld[0:1, :] = px.astype(F32)
+        fld[1:2, :] = py.astype(F32)
+        fld[2:3, :] = cells[2:3, :].astype(F32)
+        owner = turb[...]
+        gains = jnp.zeros((1, points), F32)
+        for t in range(gain.shape[0]):
+            gains = jnp.where(owner == t, gain[t], gains)
+        factor = split3(chord[...] * gains)
+        bl = split3(blade[...])
+        for k in range(3):
+            fld[3 + k : 4 + k, :] = factor[k].astype(F32)
+            fld[6 + 3 * k : 9 + 3 * k, :] = bl[k].astype(F32)
+        fld[15:16, :] = jnp.zeros((1, points), F32)
+        choose_points(r128, 0.0, sel)
+        got_ref[...] = dot(fld[...].astype(BF16), sel[...], NT)
 
     small[5].wait()
 
@@ -225,31 +229,37 @@
     up = pack(NORTH, [pops[i, :, CY - 1, :] for i in range(19)], flags[:, CY - 1, :])
     down = pack(SOUTH, [pops[i, :, 0, :] for i in range(19)], flags[:, 0, :])
     for k, (a, b) in enumerate(zip(up, down)):
-        sibling[112 + 8 * k : 120 + 8 * k, :] = jnp.where(even, a, b)
-        across[112 + 8 * k : 120 + 8 * k, :] = jnp.where(even, b, a)
-
+        sibling[8 * k : 8 * k + 8, :] = jnp.where(even, a, b)
+        across[8 * k : 8 * k + 8, :] = jnp.where(even, b, a)
+
+
+def sample_kernel(rows_sibling, rows_across, vhm, vl, fld, r128, got_in, sibling, across, sel, got_ref):
+    tiles = fld.shape[1] // LANES
+    count = jnp.max(r128[...]).astype(jnp.int32) + 1
     levels = lax.broadcasted_iota(jnp.int32, (LANES, CHUNK), 0).astype(F32)
     cell_ids = lax.broadcasted_iota(jnp.int32, (CX * CY, CHUNK), 0).astype(F32)
 
     def chunk(turn, carry):
+        @pl.when(turn == 0)
+        def _():
+            got_ref[...] = got_in[...]
+
         @pl.when(turn > 0)
         def _():
-            choose(turn)
+            choose_points(r128, (turn * CHUNK).astype(F32), sel)
+            got_ref[...] = dot(fld[...].astype(BF16), sel[...], NT)
 
         got = got_ref[...]
         cell = got[0:1] * CY + got[1:2]
         onez = jnp.where(levels == got[2:3], 1.0, 0.0).astype(BF16)
         twice = jnp.concatenate([onez, onez], axis=0)
-        factor = jnp.zeros((1, CHUNK), F32)
-        for t in range(gain.shape[0]):
-            factor = jnp.where(got[3:4] == t, gain[t], factor)
-        factor = factor * (got[4:5] + got[5:6] + got[6:7])
+        factor = got[3:4] + got[4:5] + got[5:6]
         rel = []
         for c in range(3):
             at = slice(c * CX * CY, (c + 1) * CX * CY)
             lines = dot(vhm[at, :], twice) + dot(vl[at, :], onez)
             sampled = jnp.sum(jnp.where(cell_ids == cell, lines, 0.0), axis=0, keepdims=True)
-            speed = got[7 + c : 8 + c] + got[10 + c : 11 + c] + got[13 + c : 14 + c]
+            speed = got[6 + c : 7 + c] + got[9 + c : 10 + c] + got[12 + c : 13 + c]
             rel.append(sampled - speed)
         size = jnp.sqrt(rel[0] * rel[0] + rel[1] * rel[1] + rel[2] * rel[2] + 0.0001)
         size = -(factor * size)
@@ -270,6 +280,8 @@
     sibling[0:112, :] = jnp.zeros((112, LANES), F32)
     lax.fori_loop(0, (count + CHUNK - 1) // CHUNK, chunk, 0)
     across[0:112, :] = sibling[0:112, :]
+    sibling[112:192, :] = rows_sibling[...]
+    across[112:192, :] = rows_across[...]
 
 
 def known(a, b):
@@ -304,16 +316,8 @@
 READY = 4
 
 
-def choose_points(rank, base, sel):
-    spots = lax.broadcasted_iota(jnp.int32, (CHUNK, LANES), 0).astype(F32)
-    for j in range(sel.shape[1] // LANES):
-        hit = rank[j : j + 1, :] - base == spots
-        sel[:, j * LANES : (j + 1) * LANES] = jnp.where(hit, 1.0, 0.0).astype(BF16)
-
-
 def prep_kernel(cells, spot, rank, places, sel, m128, *, total_x, total_y):
     points = cells.shape[1]
-    tiles = points // LANES
 
     def wrapped(v, total):
         v = jnp.where(v < -(total // 2), v + total, v)
@@ -323,20 +327,7 @@
     py = wrapped(cells[1:2, :] - lax.axis_index("gy") * CY, total_y)
     reach = SMEAR + 1
     near = (px >= -reach) & (px < CX + reach) & (py >= -reach) & (py < CY + reach)
-    near = jnp.where(near, 1.0, 0.0)
-    m128[...] = jnp.zeros_like(m128)
-    for j in range(tiles):
-        m128[j : j + 1, :] = near[:, j * LANES : (j + 1) * LANES]
-    mask = m128[...]
-    maskb = mask.astype(BF16)
-    rows = lax.broadcasted_iota(jnp.int32, (LANES, LANES), 0)
-    cols = lax.broadcasted_iota(jnp.int32, (LANES, LANES), 1)
-    before = jnp.where(rows < cols, 1.0, 0.0).astype(BF16)
-    above = jnp.where(rows > cols, 1.0, 0.0).astype(BF16)
-    inside = dot(maskb, before)
-    ahead = jnp.sum(dot(above, maskb), axis=1, keepdims=True)
-    rank[...] = jnp.where(mask > 0.0, inside + ahead, -1.0)
-    count = jnp.sum(mask).astype(jnp.int32)
+    count = number_points(jnp.where(near, 1.0, 0.0), m128, rank)
     places[0:1, :] = px.astype(F32)
     places[1:2, :] = py.astype(F32)
     places[2:3, :] = cells[2:3, :].astype(F32)
@@ -576,28 +567,25 @@
     sds = jax.ShapeDtypeStruct
     params = pltpu.CompilerParams(vmem_limit_bytes=24 * 1024 * 1024)
     light = pltpu.CompilerParams(vmem_limit_bytes=4 * 1024 * 1024)
-    compact = [
-        pltpu.VMEM((CHUNK, points), BF16),
-        pltpu.VMEM((16, points), F32),
-        pltpu.VMEM((LANES, LANES), F32),
-        pltpu.VMEM((LANES, LANES), F32),
-    ]
-    sibling, across, east, west, held_pops = pl.pallas_call(
-        sample_kernel,
+    rows_sibling, rows_across, east, west, held_pops, vhm, vl, fld, rank, got = pl.pallas_call(
+        dense_kernel,
         out_shape=(
-            sds((192, LANES), F32),
-            sds((192, LANES), F32),
+            sds((80, LANES), F32),
+            sds((80, LANES), F32),
             sds((10, CY, LANES), F32),
             sds((10, CY, LANES), F32),
             sds(populations.shape, F32),
+            sds((3 * CX * CY, 2 * LANES), BF16),
+            sds((3 * CX * CY, LANES), BF16),
+            sds((16, points), F32),
+            sds((LANES, LANES), F32),
+            sds((16, CHUNK), F32),
         ),
         in_specs=[HBM] * 7,
-        out_specs=(VMEM,) * 5,
+        out_specs=(VMEM,) * 10,
         scratch_shapes=[
-            pltpu.VMEM((3 * CX * CY, 2 * LANES), BF16),
-            pltpu.VMEM((3 * CX * CY, LANES), BF16),
-            *compact,
-            pltpu.VMEM((16, CHUNK), F32),
+            pltpu.VMEM((CHUNK, points), BF16),
+            pltpu.VMEM((LANES, LANES), F32),
             pltpu.SMEM(turbine_gain.shape, F32),
             pltpu.VMEM(solid_flags.shape, jnp.int32),
             pltpu.VMEM((3, points), jnp.int32),
@@ -608,7 +596,7 @@
             pltpu.SemaphoreType.DMA((6,)),
         ],
         compiler_params=params,
-        name="sample",
+        name="dense",
     )(
         *[
             pltpu.with_memory_space_constraint(arg, pltpu.HBM)
@@ -618,10 +606,20 @@
             )
         ]
     )
+    from_west = from_behind(east, "gx", 1)
+    from_east = from_behind(west, "gx", -1)
+    sibling, across = pl.pallas_call(
+        sample_kernel,
+        out_shape=(sds((192, LANES), F32), sds((192, LANES), F32)),
+        in_specs=[VMEM] * 7,
+        out_specs=(VMEM, VMEM),
+        scratch_shapes=[pltpu.VMEM((CHUNK, points), BF16), pltpu.VMEM((16, CHUNK), F32)],
+        compiler_params=params,
+        cost_estimate=cost(FORCE_FLOPS),
+        name="sample",
+    )(rows_sibling, rows_across, vhm, vl, fld, rank, got)
     beside = swapped(sibling)
     beyond = exchanged(across, lambda x, y: (x, y + 1 if y % 2 else y - 1))
-    from_west = from_behind(east, "gx", 1)
-    from_east = from_behind(west, "gx", -1)
     joined = pl.pallas_call(
         join_kernel,
         out_shape=sds((136, LANES), F32),

time: 64.2 us -> 64.4 us (level)
    pallas_call x0 -> x1, Pallas kernels: none -> 4.29 us  [local(): pl.pallas_call(dense_kernel, out_shape=(sds((80, LANES), F32), sds((80, L...]
    pallas_call x1, Pallas kernels: 4.97 us -> 0.88 us  [local(): pl.pallas_call(sample_kernel, out_shape=(sds((192, LANES), F32), sds((192...]
where the time goes in v4:
time: 64.4 us; the launch traced here: 64.3 us
  waiting for transfers between devices  31 us (48%)
  starting transfers between devices  18.8 us (29%)
  Pallas kernels  13.7 us (21%)
  between operations  0.77 us (1%)
    ppermute x9, waiting for transfers between devices, exchanged(): return lax.ppermute(block, ('gx', 'gy'), pairs)  21.5 us
    ppermute x4, starting transfers between devices, from_behind(): lax.ppermute(block, axis, [((i - distance) % count, i) for i in range(cou...  9.57 us
    ppermute x4, waiting for transfers between devices, from_behind(): lax.ppermute(block, axis, [((i - distance) % count, i) for i in range(cou...  9.5 us
    ppermute x9, starting transfers between devices, exchanged(): return lax.ppermute(block, ('gx', 'gy'), pairs)  9.23 us
    pallas_call x2, Pallas kernels, local(): pl.pallas_call(functools.partial(step_kernel, low=low, high=high), out_sh...  5.77 us
    pallas_call x1, Pallas kernels, local(): pl.pallas_call(dense_kernel, out_shape=(sds((80, LANES), F32), sds((80, L...  4.29 us
  transfers between devices with their start and end apart: 13, of which 11 were waited for; matrix products, arithmetic and copies ran while one was open for 0% of the time, Pallas kernels for 12%

profile of v4, /device:TPU:1, one launch (start us, length us, event | category | flops | bytes accessed | tf_op | source)
XLA Modules:
  0.0 64.3 jit_solution(13098653105904524210)
XLA Ops:
  0.7 4.3 %dense.1 = (f32[80,128]{1,0:T(8,128)S(1)}, f32[80,128]{1,0:T(8,128)S(1)}, f32[10,64,128]{2,1,0:T(8,128)S(1)}, f32[10,64,128]{2,1,0:T(8,128)S(1)}, f32[19,8,64,12...) custom-call(f32[24]{0:T(128)} %gain_hbm.1, ...), custom_call_target="tpu_custom_call" | custom-call | tf_op jit(solution)/shard_map/dense/pallas_call | solution.py:570
  5.0 0.9 %sample.1 = (f32[192,128]{1,0:T(8,128)S(1)}, f32[192,128]{1,0:T(8,128)S(1)}) custom-call(f32[80,128]{1,0:T(8,128)S(1)} %get-tuple-element.21.rows_sibling, f32[80,128]{1,0:T(8,128)S(1)} %get-tuple-element.22.rows_across, bf16[1536,256]{1,0:T(8,128)(2,1)S(1)} %get-tuple-element.23.vhm, bf16[1536,128]{1,0:T(8,128)(2,1)S(1)} %get-tuple-element.24.vl, ...), custom_call_target="tpu_custom_call" | custom-call | flops 40000000 | tf_op jit(solution)/shard_map/sample/pallas_call | solution.py:611
  5.8 3.3 %collective-permute-start = (f32[192,128]{1,0:T(8,128)S(1)}, f32[192,128]{1,0:T(8,128)S(1)}, u32[]{:S(2)}, u32[]{:S(2)}) collective-permute-start(f32[192,128]{1,0:T(8,128)S(1)} %get-tuple-element.28.own), channel_id=1, source_target_pairs={{1,0},{0,1},{3,2},{2,3},{5,4},{4,5},{7,6},{6,7},{9,8},{8,9},{11,10... | collective-permute-start | bytes 294920 | tf_op jit(solution)/shard_map/ppermute | solution.py:546
  9.1 0.9 %collective-permute-done.beside = f32[192,128]{1,0:T(8,128)S(1)} collective-permute-done((f32[192,128]{1,0:T(8,128)S(1)}, f32[192,128]{1,0:T(8,128)S(1)}, u32[]{:S(2)}, u32[]{:S(2)}) %collective-permute-start) | collective-permute-done | bytes 98336 | tf_op jit(solution)/shard_map/ppermute | solution.py:546
  10.1 3.4 %collective-permute-done.1.beyond = f32[192,128]{1,0:T(8,128)S(1)} collective-permute-done((f32[192,128]{1,0:T(8,128)S(1)}, f32[192,128]{1,0:T(8,128)S(1)}, u32[]{:S(2)}, u32[]{:S(2)}) %collective-permute-start.1) | collective-permute-done | bytes 98336 | tf_op jit(solution)/shard_map/ppermute | solution.py:546
  13.5 4.7 %collective-permute-start.3 = (f32[136,128]{1,0:T(8,128)S(1)}, f32[136,128]{1,0:T(8,128)S(1)}, u32[]{:S(2)}, u32[]{:S(2)}) collective-permute-start(f32[136,128]{1,0:T(8,128)S(1)} %join.1), channel_id=1, source_target_pairs={{8,0},{16,8},{24,16},{32,24},{40,32},{48,40},{56,48},{64,56},{72,6... | collective-permute-start | bytes 208904 | tf_op jit(solution)/shard_map/ppermute | solution.py:536
  18.2 1.4 %collective-permute-done.3.east_pts = f32[136,128]{1,0:T(8,128)S(1)} collective-permute-done((f32[136,128]{1,0:T(8,128)S(1)}, f32[136,128]{1,0:T(8,128)S(1)}, u32[]{:S(2)}, u32[]{:S(2)}) %collective-permute-start.3) | collective-permute-done | bytes 69664 | tf_op jit(solution)/shard_map/ppermute | solution.py:536
  19.6 5.1 %collective-permute-done.2.west_pts = f32[136,128]{1,0:T(8,128)S(1)} collective-permute-done((f32[136,128]{1,0:T(8,128)S(1)}, f32[136,128]{1,0:T(8,128)S(1)}, u32[]{:S(2)}, u32[]{:S(2)}) %collective-permute-start.2) | collective-permute-done | bytes 69664 | tf_op jit(solution)/shard_map/ppermute | solution.py:536
  24.7 4.0 %collective-permute-start.6 = (f32[112,128]{1,0:T(8,128)S(1)}, f32[112,128]{1,0:T(8,128)S(1)}, u32[]{:S(2)}, u32[]{:S(2)}) collective-permute-start(f32[112,128]{1,0:T(8,128)S(1)} %compare_select_fusion.7.points_in), channel_id=1, source_target_pairs={{1,0},{0,1},{3,2},{2,3},{5,4},{4,5},{7,6},{6,7},{9,8},{8,9},{11,10... | collective-permute-start | bytes 172040 | tf_op jit(solution)/shard_map/ppermute | solution.py:546
  28.7 0.9 %collective-permute-done.6 = f32[112,128]{1,0:T(8,128)S(1)} collective-permute-done((f32[112,128]{1,0:T(8,128)S(1)}, f32[112,128]{1,0:T(8,128)S(1)}, u32[]{:S(2)}, u32[]{:S(2)}) %collective-permute-start.6) | collective-permute-done | bytes 57376 | tf_op jit(solution)/shard_map/ppermute | solution.py:546
  29.7 5.1 %collective-permute-done.7 = f32[112,128]{1,0:T(8,128)S(1)} collective-permute-done((f32[112,128]{1,0:T(8,128)S(1)}, f32[112,128]{1,0:T(8,128)S(1)}, u32[]{:S(2)}, u32[]{:S(2)}) %collective-permute-start.7) | collective-permute-done | bytes 57376 | tf_op jit(solution)/shard_map/ppermute | solution.py:546
  34.8 0.7 %collective-permute-start.8 = (f32[112,128]{1,0:T(8,128)S(1)}, f32[112,128]{1,0:T(8,128)S(1)}, u32[]{:S(2)}, u32[]{:S(2)}) collective-permute-start(f32[112,128]{1,0:T(8,128)S(1)} %compare_select_fusion.4), channel_id=1, source_target_pairs={{1,0},{0,1},{3,2},{2,3},{5,4},{4,5},{7,6},{6,7},{9,8},{8,9},{11,10... | collective-permute-start | bytes 172040 | tf_op jit(solution)/shard_map/ppermute | solution.py:546
  35.6 0.9 %collective-permute-done.8 = f32[112,128]{1,0:T(8,128)S(1)} collective-permute-done((f32[112,128]{1,0:T(8,128)S(1)}, f32[112,128]{1,0:T(8,128)S(1)}, u32[]{:S(2)}, u32[]{:S(2)}) %collective-permute-start.8) | collective-permute-done | bytes 57376 | tf_op jit(solution)/shard_map/ppermute | solution.py:546
  36.5 5.8 %collective-permute-done.9 = f32[112,128]{1,0:T(8,128)S(1)} collective-permute-done((f32[112,128]{1,0:T(8,128)S(1)}, f32[112,128]{1,0:T(8,128)S(1)}, u32[]{:S(2)}, u32[]{:S(2)}) %collective-permute-start.9) | collective-permute-done | bytes 57376 | tf_op jit(solution)/shard_map/ppermute | solution.py:546
  42.3 0.9 %collective-permute-start.10 = (f32[112,128]{1,0:T(8,128)S(1)}, f32[112,128]{1,0:T(8,128)S(1)}, u32[]{:S(2)}, u32[]{:S(2)}) collective-permute-start(f32[112,128]{1,0:T(8,128)S(1)} %compare_select_fusion.2), channel_id=1, source_target_pairs={{1,0},{0,1},{3,2},{2,3},{5,4},{4,5},{7,6},{6,7},{9,8},{8,9},{11,10... | collective-permute-start | bytes 172040 | tf_op jit(solution)/shard_map/ppermute | solution.py:546
  43.3 0.9 %collective-permute-done.10 = f32[112,128]{1,0:T(8,128)S(1)} collective-permute-done((f32[112,128]{1,0:T(8,128)S(1)}, f32[112,128]{1,0:T(8,128)S(1)}, u32[]{:S(2)}, u32[]{:S(2)}) %collective-permute-start.10) | collective-permute-done | bytes 57376 | tf_op jit(solution)/shard_map/ppermute | solution.py:546
  44.2 1.7 %collective-permute-start.4 = (f32[10,64,128]{2,1,0:T(8,128)S(1)}, f32[10,64,128]{2,1,0:T(8,128)S(1)}, u32[]{:S(2)}, u32[]{:S(2)}) collective-permute-start(f32[10,64,128]{2,1,0:T(8,128)S(1)} %get-tuple-element.30), channel_id=1, source_target_pairs={{248,0},{0,8},{8,16},{16,24},{24,32},{32,40},{40,48},{48,56},{56,6... | collective-permute-start | bytes 983048 | tf_op jit(solution)/shard_map/ppermute | solution.py:536
  45.9 3.2 %collective-permute-start.5 = (f32[10,64,128]{2,1,0:T(8,128)S(1)}, f32[10,64,128]{2,1,0:T(8,128)S(1)}, u32[]{:S(2)}, u32[]{:S(2)}) collective-permute-start(f32[10,64,128]{2,1,0:T(8,128)S(1)} %get-tuple-element.31), channel_id=1, source_target_pairs={{8,0},{16,8},{24,16},{32,24},{40,32},{48,40},{56,48},{64,56},{72,6... | collective-permute-start | bytes 983048 | tf_op jit(solution)/shard_map/ppermute | solution.py:536
  49.1 3.6 %collective-permute-done.11 = f32[112,128]{1,0:T(8,128)S(1)} collective-permute-done((f32[112,128]{1,0:T(8,128)S(1)}, f32[112,128]{1,0:T(8,128)S(1)}, u32[]{:S(2)}, u32[]{:S(2)}) %collective-permute-start.11) | collective-permute-done | bytes 57376 | tf_op jit(solution)/shard_map/ppermute | solution.py:546
  52.8 1.1 %prep.1 = (f32[5,8,256]{2,1,0:T(8,128)S(1)}, f32[128,128]{1,0:T(8,128)S(1)}, f32[8,4608]{1,0:T(8,128)S(1)}) custom-call(s32[3,4608]{1,0:T(4,128)S(1)} %copy-done.1), custom_call_target="tpu_custom_call" | custom-call | flops 40000000 | tf_op jit(solution)/shard_map/prep/pallas_call | solution.py:634
  53.9 0.9 %force.1 = f32[3,10,72,128]{3,2,1,0:T(8,128)S(1)} custom-call(f32[5,8,256]{2,1,0:T(8,128)S(1)} %get-tuple-element.18.spot_in, f32[128,128]{1,0:T(8,128)S(1)} %get-tuple-element.19.rank, f32[8,4608]{1,0:T(8,128)S(1)} %get-tuple-element.20.places, f32[112,128]{1,0:T(8,128)S(1)} %compare_select_fusion.7.points_in), custom_call_target="tpu_custom_call" | custom-call | flops 40000000 | tf_op jit(solution)/shard_map/force/pallas_call | solution.py:648
  54.8 3.0 %collective-permute-done.4.from_west = f32[10,64,128]{2,1,0:T(8,128)S(1)} collective-permute-done((f32[10,64,128]{2,1,0:T(8,128)S(1)}, f32[10,64,128]{2,1,0:T(8,128)S(1)}, u32[]{:S(2)}, u32[]{:S(2)}) %collective-permute-start.4) | collective-permute-done | bytes 327712 | tf_op jit(solution)/shard_map/ppermute | solution.py:536
  57.8 2.9 %shard_map.86.rest_0_ = f32[19,8,64,128]{3,2,1,0:T(8,128)} custom-call(f32[19,8,64,128]{3,2,1,0:T(8,128)S(1)} %get-tuple-element.17.pops, s32[8,64,128]{2,1,0:T(8,128)S(1)} %copy-done, f32[3,10,72,128]{3,2,1,0:T(8,128)S(1)} %force.1, f32[10,64,128]{2,1,0:T(8,128)S(1)} %collective-permute-done.4.from_west, ...), custom_call_target="tpu_custom_call" | custom-call | flops 60000000 | tf_op jit(solution)/shard_map/pallas_call | solution.py:664
  60.7 2.9 %shard_map.87 = f32[19,8,64,128]{3,2,1,0:T(8,128)} custom-call(f32[19,8,64,128]{3,2,1,0:T(8,128)S(1)} %get-tuple-element.17.pops, s32[8,64,128]{2,1,0:T(8,128)S(1)} %copy-done, f32[3,10,72,128]{3,2,1,0:T(8,128)S(1)} %force.1, f32[10,64,128]{2,1,0:T(8,128)S(1)} %collective-permute-done.4.from_west, ...), custom_call_target="tpu_custom_call", output_to_operand_aliasing={{}: (9, {})} | custom-call | flops 60000000 | tf_op jit(solution)/shard_map/pallas_call | solution.py:664
  (21 shorter events, 1.0 us)
Async XLA Ops:
  0.6 57.2 %copy-start = (s32[8,64,128]{2,1,0:T(8,128)S(1)}, s32[8,64,128]{2,1,0:T(8,128)}, u32[]{:S(2)}) copy-start(s32[8,64,128]{2,1,0:T(8,128)} %flags.3) | copy-start | bytes 786436
  0.6 52.1 %copy-start.1 = (s32[3,4608]{1,0:T(4,128)S(1)}, s32[3,4608]{1,0:T(4,128)}, u32[]{:S(2)}) copy-start(s32[3,4608]{1,0:T(4,128)} %cells.1) | copy-start | bytes 165892
  5.8 4.2 %collective-permute-start = (f32[192,128]{1,0:T(8,128)S(1)}, f32[192,128]{1,0:T(8,128)S(1)}, u32[]{:S(2)}, u32[]{:S(2)}) collective-permute-start(f32[192,128]{1,0:T(8,128)S(1)} %get-tuple-element.28.own), channel_id=1, source_target_pairs={{1,0},{0,1},{3,2},{2,3},{5,4},{4,5},{7,6},{6,7},{9,8},{8,9},{11,10... | collective-permute-start | bytes 294920 | tf_op jit(solution)/shard_map/ppermute | solution.py:546
  9.1 4.3 %collective-permute-start.1 = (f32[192,128]{1,0:T(8,128)S(1)}, f32[192,128]{1,0:T(8,128)S(1)}, u32[]{:S(2)}, u32[]{:S(2)}) collective-permute-start(f32[192,128]{1,0:T(8,128)S(1)} %get-tuple-element.29), channel_id=1, source_target_pairs={{7,0},{2,1},{1,2},{4,3},{3,4},{6,5},{5,6},{0,7},{15,8},{10,9},{9,1... | collective-permute-start | bytes 294920 | tf_op jit(solution)/shard_map/ppermute | solution.py:546
  13.5 6.1 %collective-permute-start.3 = (f32[136,128]{1,0:T(8,128)S(1)}, f32[136,128]{1,0:T(8,128)S(1)}, u32[]{:S(2)}, u32[]{:S(2)}) collective-permute-start(f32[136,128]{1,0:T(8,128)S(1)} %join.1), channel_id=1, source_target_pairs={{8,0},{16,8},{24,16},{32,24},{40,32},{48,40},{56,48},{64,56},{72,6... | collective-permute-start | bytes 208904 | tf_op jit(solution)/shard_map/ppermute | solution.py:536
  18.2 6.5 %collective-permute-start.2 = (f32[136,128]{1,0:T(8,128)S(1)}, f32[136,128]{1,0:T(8,128)S(1)}, u32[]{:S(2)}, u32[]{:S(2)}) collective-permute-start(f32[136,128]{1,0:T(8,128)S(1)} %join.1), channel_id=1, source_target_pairs={{248,0},{0,8},{8,16},{16,24},{24,32},{32,40},{40,48},{48,56},{56,6... | collective-permute-start | bytes 208904 | tf_op jit(solution)/shard_map/ppermute | solution.py:536
  24.7 4.9 %collective-permute-start.6 = (f32[112,128]{1,0:T(8,128)S(1)}, f32[112,128]{1,0:T(8,128)S(1)}, u32[]{:S(2)}, u32[]{:S(2)}) collective-permute-start(f32[112,128]{1,0:T(8,128)S(1)} %compare_select_fusion.7.points_in), channel_id=1, source_target_pairs={{1,0},{0,1},{3,2},{2,3},{5,4},{4,5},{7,6},{6,7},{9,8},{8,9},{11,10... | collective-permute-start | bytes 172040 | tf_op jit(solution)/shard_map/ppermute | solution.py:546
  29.6 5.2 %collective-permute-start.7 = (f32[112,128]{1,0:T(8,128)S(1)}, f32[112,128]{1,0:T(8,128)S(1)}, u32[]{:S(2)}, u32[]{:S(2)}) collective-permute-start(f32[112,128]{1,0:T(8,128)S(1)} %compare_select_fusion.5), channel_id=1, source_target_pairs={{24,0},{233,1},{26,2},{235,3},{28,4},{237,5},{30,6},{239,7},{32,8}... | collective-permute-start | bytes 172040 | tf_op jit(solution)/shard_map/ppermute | solution.py:546
  34.8 1.6 %collective-permute-start.8 = (f32[112,128]{1,0:T(8,128)S(1)}, f32[112,128]{1,0:T(8,128)S(1)}, u32[]{:S(2)}, u32[]{:S(2)}) collective-permute-start(f32[112,128]{1,0:T(8,128)S(1)} %compare_select_fusion.4), channel_id=1, source_target_pairs={{1,0},{0,1},{3,2},{2,3},{5,4},{4,5},{7,6},{6,7},{9,8},{8,9},{11,10... | collective-permute-start | bytes 172040 | tf_op jit(solution)/shard_map/ppermute | solution.py:546
  36.5 5.9 %collective-permute-start.9 = (f32[112,128]{1,0:T(8,128)S(1)}, f32[112,128]{1,0:T(8,128)S(1)}, u32[]{:S(2)}, u32[]{:S(2)}) collective-permute-start(f32[112,128]{1,0:T(8,128)S(1)} %compare_select_fusion.3), channel_id=1, source_target_pairs={{56,0},{37,1},{58,2},{39,3},{60,4},{33,5},{62,6},{35,7},{64,8},{45... | collective-permute-start | bytes 172040 | tf_op jit(solution)/shard_map/ppermute | solution.py:546
  42.3 1.8 %collective-permute-start.10 = (f32[112,128]{1,0:T(8,128)S(1)}, f32[112,128]{1,0:T(8,128)S(1)}, u32[]{:S(2)}, u32[]{:S(2)}) collective-permute-start(f32[112,128]{1,0:T(8,128)S(1)} %compare_select_fusion.2), channel_id=1, source_target_pairs={{1,0},{0,1},{3,2},{2,3},{5,4},{4,5},{7,6},{6,7},{9,8},{8,9},{11,10... | collective-permute-start | bytes 172040 | tf_op jit(solution)/shard_map/ppermute | solution.py:546
  44.2 8.5 %collective-permute-start.11 = (f32[112,128]{1,0:T(8,128)S(1)}, f32[112,128]{1,0:T(8,128)S(1)}, u32[]{:S(2)}, u32[]{:S(2)}) collective-permute-start(f32[112,128]{1,0:T(8,128)S(1)} %compare_select_fusion.1), channel_id=1, source_target_pairs={{64,0},{165,1},{66,2},{167,3},{68,4},{161,5},{70,6},{163,7},{72,8}... | collective-permute-start | bytes 172040 | tf_op jit(solution)/shard_map/ppermute | solution.py:546
  44.2 13.6 %collective-permute-start.4 = (f32[10,64,128]{2,1,0:T(8,128)S(1)}, f32[10,64,128]{2,1,0:T(8,128)S(1)}, u32[]{:S(2)}, u32[]{:S(2)}) collective-permute-start(f32[10,64,128]{2,1,0:T(8,128)S(1)} %get-tuple-element.30), channel_id=1, source_target_pairs={{248,0},{0,8},{8,16},{16,24},{24,32},{32,40},{40,48},{48,56},{56,6... | collective-permute-start | bytes 983048 | tf_op jit(solution)/shard_map/ppermute | solution.py:536
  45.9 11.9 %collective-permute-start.5 = (f32[10,64,128]{2,1,0:T(8,128)S(1)}, f32[10,64,128]{2,1,0:T(8,128)S(1)}, u32[]{:S(2)}, u32[]{:S(2)}) collective-permute-start(f32[10,64,128]{2,1,0:T(8,128)S(1)} %get-tuple-element.31), channel_id=1, source_target_pairs={{8,0},{16,8},{24,16},{32,24},{40,32},{48,40},{56,48},{64,56},{72,6... | collective-permute-start | bytes 983048 | tf_op jit(solution)/shard_map/ppermute | solution.py:536
  52.7 11.0 %collective-permute-start.12 = (f32[112,128]{1,0:T(8,128)S(1)}, f32[112,128]{1,0:T(8,128)S(1)}, u32[]{:S(2)}, u32[]{:S(2)}) collective-permute-start(f32[112,128]{1,0:T(8,128)S(1)} %compare_select_fusion.mine), channel_id=1, source_target_pairs={{1,0},{0,1},{3,2},{2,3},{5,4},{4,5},{7,6},{6,7},{9,8},{8,9},{11,10... | collective-permute-start | bytes 172040 | tf_op jit(solution)/shard_map/ppermute | solution.py:546

commit v5 on v3

--- a/solution.py
+++ b/solution.py
@@ -632,6 +632,7 @@
     )(sibling, beside, beyond)
     west_pts = from_behind(joined, "gx", 1)
     east_pts = from_behind(joined, "gx", -1)
+    other_half = exchanged(joined, lambda x, y: (x, y + 4))
     near = known(joined[:112], known(west_pts[:112], east_pts[:112]))
     prepared = pl.pallas_call(
         functools.partial(prep_kernel, total_x=total_x, total_y=total_y),
@@ -676,15 +677,18 @@
             compiler_params=params,
             cost_estimate=cost(STEP_FLOPS),
         )(*step_args, *extra)
-    got = swapped(near)
-    have = known(near, got)
-    got = fetched(have, (3, 0), (-3, 0))
+    have = known(near, other_half[:112])
+    got = swapped(have)
+    have = known(have, got)
+    got = fetched(have, (4, 0), (-4, 0))
     have = known(have, got)
     have = known(have, swapped(have))
-    got = fetched(have, (7, 0), (4, 4))
+    got = fetched(have, (12, 0), (-12, 0))
     have = known(have, got)
     have = known(have, swapped(have))
-    got = fetched(have, (8, 0), (20, 4))
+    got = exchanged(
+        have, lambda x, y: (x // 4 * 4 + (x + 2) % 4, y) if y % 2 else (x, y + 4)
+    )
     have = known(have, got)
     point_force = pl.pallas_call(
         finish_kernel,

time: 64.2 us -> 63.5 us (0.989)
  waiting for transfers between devices: 31 us -> 27.2 us
  starting transfers between devices: 18.8 us -> 21.4 us
    ppermute x4, starting transfers between devices: 9.62 us -> 13.6 us  [from_behind(): lax.ppermute(block, axis, [((i - distance) % count, i) for i in range(cou...]
    ppermute x9 -> x10, waiting for transfers between devices: 21.5 us -> 18.9 us  [exchanged(): return lax.ppermute(block, ('gx', 'gy'), pairs)]
    ppermute x9 -> x10, starting transfers between devices: 9.17 us -> 7.8 us  [exchanged(): return lax.ppermute(block, ('gx', 'gy'), pairs)]
    ppermute x4, waiting for transfers between devices: 9.51 us -> 8.33 us  [from_behind(): lax.ppermute(block, axis, [((i - distance) % count, i) for i in range(cou...]
  transfers between devices with their start and end apart: 13 -> 14, of which waited for: 11 -> 11; matrix products, arithmetic and copies ran while one was open for 0% -> 0% of each run, Pallas kernels for 12% -> 13%
where the time goes in v5:
time: 63.5 us; the launch traced here: 63 us
  waiting for transfers between devices  27.2 us (43%)
  starting transfers between devices  21.4 us (34%)
  Pallas kernels  13.6 us (21%)
  between operations  0.76 us (1%)
    ppermute x10, waiting for transfers between devices, exchanged(): return lax.ppermute(block, ('gx', 'gy'), pairs)  18.9 us
    ppermute x4, starting transfers between devices, from_behind(): lax.ppermute(block, axis, [((i - distance) % count, i) for i in range(cou...  13.6 us
    ppermute x4, waiting for transfers between devices, from_behind(): lax.ppermute(block, axis, [((i - distance) % count, i) for i in range(cou...  8.33 us
    ppermute x10, starting transfers between devices, exchanged(): return lax.ppermute(block, ('gx', 'gy'), pairs)  7.8 us
    pallas_call x2, Pallas kernels, local(): pl.pallas_call(functools.partial(step_kernel, low=low, high=high), out_sh...  5.77 us
    pallas_call x1, Pallas kernels, local(): pl.pallas_call(sample_kernel, out_shape=(sds((192, LANES), F32), sds((192...  4.97 us
  transfers between devices with their start and end apart: 14, of which 11 were waited for; matrix products, arithmetic and copies ran while one was open for 0% of the time, Pallas kernels for 13%

profile of v5, /device:TPU:1, one launch (start us, length us, event | category | flops | bytes accessed | tf_op | source)
XLA Modules:
  0.0 63.0 jit_solution(9106853566974695667)
XLA Ops:
  0.7 5.0 %sample.1 = (f32[192,128]{1,0:T(8,128)S(1)}, f32[192,128]{1,0:T(8,128)S(1)}, f32[10,64,128]{2,1,0:T(8,128)S(1)}, f32[10,64,128]{2,1,0:T(8,128)S(1)}, f32[19,8,64,128]{3,2,1,0:T(8,128)S(1)}) custom-call(f32[24]{0:T(128)} %gain_hbm.1, f32[19,8,64,128]{3,2,1,0:T(8,128)} %pops_hbm.1, s32[8,64,128]{2,1,0:T(8,128)} %flags.3, s32[3,4608]{1,0:T(4,128)} %cells.1, ...), custom_call_target="tpu_custom_call" | custom-call | tf_op jit(solution)/shard_map/sample/pallas_call | solution.py:585
  5.6 3.3 %collective-permute-start = (f32[192,128]{1,0:T(8,128)S(1)}, f32[192,128]{1,0:T(8,128)S(1)}, u32[]{:S(2)}, u32[]{:S(2)}) collective-permute-start(f32[192,128]{1,0:T(8,128)S(1)} %get-tuple-element.14.own), channel_id=1, source_target_pairs={{1,0},{0,1},{3,2},{2,3},{5,4},{4,5},{7,6},{6,7},{9,8},{8,9},{11,10... | collective-permute-start | bytes 294920 | tf_op jit(solution)/shard_map/ppermute | solution.py:555
  8.9 0.9 %collective-permute-done.beside = f32[192,128]{1,0:T(8,128)S(1)} collective-permute-done((f32[192,128]{1,0:T(8,128)S(1)}, f32[192,128]{1,0:T(8,128)S(1)}, u32[]{:S(2)}, u32[]{:S(2)}) %collective-permute-start) | collective-permute-done | bytes 98336 | tf_op jit(solution)/shard_map/ppermute | solution.py:555
  9.9 3.4 %collective-permute-done.1.beyond = f32[192,128]{1,0:T(8,128)S(1)} collective-permute-done((f32[192,128]{1,0:T(8,128)S(1)}, f32[192,128]{1,0:T(8,128)S(1)}, u32[]{:S(2)}, u32[]{:S(2)}) %collective-permute-start.1) | collective-permute-done | bytes 98336 | tf_op jit(solution)/shard_map/ppermute | solution.py:555
  13.4 8.8 %collective-permute-start.3 = (f32[136,128]{1,0:T(8,128)S(1)}, f32[136,128]{1,0:T(8,128)S(1)}, u32[]{:S(2)}, u32[]{:S(2)}) collective-permute-start(f32[136,128]{1,0:T(8,128)S(1)} %join.1), channel_id=1, source_target_pairs={{8,0},{16,8},{24,16},{32,24},{40,32},{48,40},{56,48},{64,56},{72,6... | collective-permute-start | bytes 208904 | tf_op jit(solution)/shard_map/ppermute | solution.py:545
  22.1 1.4 %collective-permute-done.3.east_pts = f32[136,128]{1,0:T(8,128)S(1)} collective-permute-done((f32[136,128]{1,0:T(8,128)S(1)}, f32[136,128]{1,0:T(8,128)S(1)}, u32[]{:S(2)}, u32[]{:S(2)}) %collective-permute-start.3) | collective-permute-done | bytes 69664 | tf_op jit(solution)/shard_map/ppermute | solution.py:545
  23.5 5.1 %collective-permute-done.2.west_pts = f32[136,128]{1,0:T(8,128)S(1)} collective-permute-done((f32[136,128]{1,0:T(8,128)S(1)}, f32[136,128]{1,0:T(8,128)S(1)}, u32[]{:S(2)}, u32[]{:S(2)}) %collective-permute-start.2) | collective-permute-done | bytes 69664 | tf_op jit(solution)/shard_map/ppermute | solution.py:545
  28.6 1.9 %collective-permute-start.7 = (f32[112,128]{1,0:T(8,128)S(1)}, f32[112,128]{1,0:T(8,128)S(1)}, u32[]{:S(2)}, u32[]{:S(2)}) collective-permute-start(f32[112,128]{1,0:T(8,128)S(1)} %get-tuple-element.18), channel_id=1, source_target_pairs={{1,0},{0,1},{3,2},{2,3},{5,4},{4,5},{7,6},{6,7},{9,8},{8,9},{11,10... | collective-permute-start | bytes 172040 | tf_op jit(solution)/shard_map/ppermute | solution.py:555
  30.5 0.9 %collective-permute-done.7 = f32[112,128]{1,0:T(8,128)S(1)} collective-permute-done((f32[112,128]{1,0:T(8,128)S(1)}, f32[112,128]{1,0:T(8,128)S(1)}, u32[]{:S(2)}, u32[]{:S(2)}) %collective-permute-start.7) | collective-permute-done | bytes 57376 | tf_op jit(solution)/shard_map/ppermute | solution.py:555
  31.5 4.2 %collective-permute-done.8 = f32[112,128]{1,0:T(8,128)S(1)} collective-permute-done((f32[112,128]{1,0:T(8,128)S(1)}, f32[112,128]{1,0:T(8,128)S(1)}, u32[]{:S(2)}, u32[]{:S(2)}) %collective-permute-start.8) | collective-permute-done | bytes 57376 | tf_op jit(solution)/shard_map/ppermute | solution.py:555
  35.7 0.4 collective-permute-start.9
  36.1 0.9 %collective-permute-done.9 = f32[112,128]{1,0:T(8,128)S(1)} collective-permute-done((f32[112,128]{1,0:T(8,128)S(1)}, f32[112,128]{1,0:T(8,128)S(1)}, u32[]{:S(2)}, u32[]{:S(2)}) %collective-permute-start.9) | collective-permute-done | bytes 57376 | tf_op jit(solution)/shard_map/ppermute | solution.py:555
  37.2 6.9 %collective-permute-done.10 = f32[112,128]{1,0:T(8,128)S(1)} collective-permute-done((f32[112,128]{1,0:T(8,128)S(1)}, f32[112,128]{1,0:T(8,128)S(1)}, u32[]{:S(2)}, u32[]{:S(2)}) %collective-permute-start.10) | collective-permute-done | bytes 57376 | tf_op jit(solution)/shard_map/ppermute | solution.py:555
  44.0 0.2 collective-permute-start.11
  44.3 1.1 %collective-permute-done.11 = f32[112,128]{1,0:T(8,128)S(1)} collective-permute-done((f32[112,128]{1,0:T(8,128)S(1)}, f32[112,128]{1,0:T(8,128)S(1)}, u32[]{:S(2)}, u32[]{:S(2)}) %collective-permute-start.11) | collective-permute-done | bytes 57376 | tf_op jit(solution)/shard_map/ppermute | solution.py:555
  45.6 4.8 %collective-permute-start.5 = (f32[10,64,128]{2,1,0:T(8,128)S(1)}, f32[10,64,128]{2,1,0:T(8,128)S(1)}, u32[]{:S(2)}, u32[]{:S(2)}) collective-permute-start(f32[10,64,128]{2,1,0:T(8,128)S(1)} %get-tuple-element.17), channel_id=1, source_target_pairs={{8,0},{16,8},{24,16},{32,24},{40,32},{48,40},{56,48},{64,56},{72,6... | collective-permute-start | bytes 983048 | tf_op jit(solution)/shard_map/ppermute | solution.py:545
  50.4 0.6 collective-permute-done.12
  50.9 1.7 %collective-permute-start.13 = (f32[112,128]{1,0:T(8,128)S(1)}, f32[112,128]{1,0:T(8,128)S(1)}, u32[]{:S(2)}, u32[]{:S(2)}) collective-permute-start(f32[112,128]{1,0:T(8,128)S(1)} %compare_select_fusion.mine), channel_id=1, source_target_pairs={{1,0},{0,1},{3,2},{2,3},{5,4},{4,5},{7,6},{6,7},{9,8},{8,9},{11,10... | collective-permute-start | bytes 172040 | tf_op jit(solution)/shard_map/ppermute | solution.py:555
  52.6 1.2 %prep.1 = (f32[5,8,256]{2,1,0:T(8,128)S(1)}, f32[128,128]{1,0:T(8,128)S(1)}, f32[8,4608]{1,0:T(8,128)S(1)}) custom-call(s32[3,4608]{1,0:T(4,128)S(1)} %copy-done.1), custom_call_target="tpu_custom_call" | custom-call | flops 40000000 | tf_op jit(solution)/shard_map/prep/pallas_call | solution.py:637
  53.8 0.9 %force.1 = f32[3,10,72,128]{3,2,1,0:T(8,128)S(1)} custom-call(f32[5,8,256]{2,1,0:T(8,128)S(1)} %get-tuple-element.11.spot_in, f32[128,128]{1,0:T(8,128)S(1)} %get-tuple-element.12.rank, f32[8,4608]{1,0:T(8,128)S(1)} %get-tuple-element.13.places, f32[112,128]{1,0:T(8,128)S(1)} %get-tuple-element.19.points_in), custom_call_target="tpu_custom_call" | custom-call | flops 40000000 | tf_op jit(solution)/shard_map/force/pallas_call | solution.py:651
  54.7 1.9 %collective-permute-done.4.from_west = f32[10,64,128]{2,1,0:T(8,128)S(1)} collective-permute-done((f32[10,64,128]{2,1,0:T(8,128)S(1)}, f32[10,64,128]{2,1,0:T(8,128)S(1)}, u32[]{:S(2)}, u32[]{:S(2)}) %collective-permute-start.4) | collective-permute-done | bytes 327712 | tf_op jit(solution)/shard_map/ppermute | solution.py:545
  56.6 2.9 %shard_map.86.rest_0_ = f32[19,8,64,128]{3,2,1,0:T(8,128)} custom-call(f32[19,8,64,128]{3,2,1,0:T(8,128)S(1)} %get-tuple-element.10.pops, s32[8,64,128]{2,1,0:T(8,128)S(1)} %copy-done, f32[3,10,72,128]{3,2,1,0:T(8,128)S(1)} %force.1, f32[10,64,128]{2,1,0:T(8,128)S(1)} %collective-permute-done.4.from_west, ...), custom_call_target="tpu_custom_call" | custom-call | flops 60000000 | tf_op jit(solution)/shard_map/pallas_call | solution.py:667
  59.5 2.9 %shard_map.87 = f32[19,8,64,128]{3,2,1,0:T(8,128)} custom-call(f32[19,8,64,128]{3,2,1,0:T(8,128)S(1)} %get-tuple-element.10.pops, s32[8,64,128]{2,1,0:T(8,128)S(1)} %copy-done, f32[3,10,72,128]{3,2,1,0:T(8,128)S(1)} %force.1, f32[10,64,128]{2,1,0:T(8,128)S(1)} %collective-permute-done.4.from_west, ...), custom_call_target="tpu_custom_call", output_to_operand_aliasing={{}: (9, {})} | custom-call | flops 60000000 | tf_op jit(solution)/shard_map/pallas_call | solution.py:667
  62.4 0.7 %finish.1 = f32[3,4608]{1,0:T(4,128)} custom-call(f32[112,128]{1,0:T(8,128)S(1)} %compare_select_fusion.mine, f32[112,128]{1,0:T(8,128)S(1)} %collective-permute-done.13.other), custom_call_target="tpu_custom_call" | custom-call | tf_op jit(solution)/shard_map/finish/pallas_call | solution.py:693
  (22 shorter events, 0.5 us)
Async XLA Ops:
  0.6 56.0 %copy-start = (s32[8,64,128]{2,1,0:T(8,128)S(1)}, s32[8,64,128]{2,1,0:T(8,128)}, u32[]{:S(2)}) copy-start(s32[8,64,128]{2,1,0:T(8,128)} %flags.3) | copy-start | bytes 786436
  0.6 52.0 %copy-start.1 = (s32[3,4608]{1,0:T(4,128)S(1)}, s32[3,4608]{1,0:T(4,128)}, u32[]{:S(2)}) copy-start(s32[3,4608]{1,0:T(4,128)} %cells.1) | copy-start | bytes 165892
  5.6 4.2 %collective-permute-start = (f32[192,128]{1,0:T(8,128)S(1)}, f32[192,128]{1,0:T(8,128)S(1)}, u32[]{:S(2)}, u32[]{:S(2)}) collective-permute-start(f32[192,128]{1,0:T(8,128)S(1)} %get-tuple-element.14.own), channel_id=1, source_target_pairs={{1,0},{0,1},{3,2},{2,3},{5,4},{4,5},{7,6},{6,7},{9,8},{8,9},{11,10... | collective-permute-start | bytes 294920 | tf_op jit(solution)/shard_map/ppermute | solution.py:555
  8.9 4.3 %collective-permute-start.1 = (f32[192,128]{1,0:T(8,128)S(1)}, f32[192,128]{1,0:T(8,128)S(1)}, u32[]{:S(2)}, u32[]{:S(2)}) collective-permute-start(f32[192,128]{1,0:T(8,128)S(1)} %get-tuple-element.15), channel_id=1, source_target_pairs={{7,0},{2,1},{1,2},{4,3},{3,4},{6,5},{5,6},{0,7},{15,8},{10,9},{9,1... | collective-permute-start | bytes 294920 | tf_op jit(solution)/shard_map/ppermute | solution.py:555
  13.3 8.9 %collective-permute-start.6 = (f32[136,128]{1,0:T(8,128)S(1)}, f32[136,128]{1,0:T(8,128)S(1)}, u32[]{:S(2)}, u32[]{:S(2)}) collective-permute-start(f32[136,128]{1,0:T(8,128)S(1)} %join.1), channel_id=1, source_target_pairs={{4,0},{5,1},{6,2},{7,3},{0,4},{1,5},{2,6},{3,7},{12,8},{13,9},{14,... | collective-permute-start | bytes 208904 | tf_op jit(solution)/shard_map/ppermute | solution.py:555
  13.4 10.1 %collective-permute-start.3 = (f32[136,128]{1,0:T(8,128)S(1)}, f32[136,128]{1,0:T(8,128)S(1)}, u32[]{:S(2)}, u32[]{:S(2)}) collective-permute-start(f32[136,128]{1,0:T(8,128)S(1)} %join.1), channel_id=1, source_target_pairs={{8,0},{16,8},{24,16},{32,24},{40,32},{48,40},{56,48},{64,56},{72,6... | collective-permute-start | bytes 208904 | tf_op jit(solution)/shard_map/ppermute | solution.py:545
  22.1 6.5 %collective-permute-start.2 = (f32[136,128]{1,0:T(8,128)S(1)}, f32[136,128]{1,0:T(8,128)S(1)}, u32[]{:S(2)}, u32[]{:S(2)}) collective-permute-start(f32[136,128]{1,0:T(8,128)S(1)} %join.1), channel_id=1, source_target_pairs={{248,0},{0,8},{8,16},{16,24},{24,32},{32,40},{40,48},{48,56},{56,6... | collective-permute-start | bytes 208904 | tf_op jit(solution)/shard_map/ppermute | solution.py:545
  28.6 2.8 %collective-permute-start.7 = (f32[112,128]{1,0:T(8,128)S(1)}, f32[112,128]{1,0:T(8,128)S(1)}, u32[]{:S(2)}, u32[]{:S(2)}) collective-permute-start(f32[112,128]{1,0:T(8,128)S(1)} %get-tuple-element.18), channel_id=1, source_target_pairs={{1,0},{0,1},{3,2},{2,3},{5,4},{4,5},{7,6},{6,7},{9,8},{8,9},{11,10... | collective-permute-start | bytes 172040 | tf_op jit(solution)/shard_map/ppermute | solution.py:555
  31.4 4.3 %collective-permute-start.8 = (f32[112,128]{1,0:T(8,128)S(1)}, f32[112,128]{1,0:T(8,128)S(1)}, u32[]{:S(2)}, u32[]{:S(2)}) collective-permute-start(f32[112,128]{1,0:T(8,128)S(1)} %compare_select_fusion.5), channel_id=1, source_target_pairs={{32,0},{225,1},{34,2},{227,3},{36,4},{229,5},{38,6},{231,7},{40,8}... | collective-permute-start | bytes 172040 | tf_op jit(solution)/shard_map/ppermute | solution.py:555
  35.7 1.3 %collective-permute-start.9 = (f32[112,128]{1,0:T(8,128)S(1)}, f32[112,128]{1,0:T(8,128)S(1)}, u32[]{:S(2)}, u32[]{:S(2)}) collective-permute-start(f32[112,128]{1,0:T(8,128)S(1)} %compare_select_fusion.4), channel_id=1, source_target_pairs={{1,0},{0,1},{3,2},{2,3},{5,4},{4,5},{7,6},{6,7},{9,8},{8,9},{11,10... | collective-permute-start | bytes 172040 | tf_op jit(solution)/shard_map/ppermute | solution.py:555
  37.1 7.0 %collective-permute-start.10 = (f32[112,128]{1,0:T(8,128)S(1)}, f32[112,128]{1,0:T(8,128)S(1)}, u32[]{:S(2)}, u32[]{:S(2)}) collective-permute-start(f32[112,128]{1,0:T(8,128)S(1)} %compare_select_fusion.3), channel_id=1, source_target_pairs={{96,0},{161,1},{98,2},{163,3},{100,4},{165,5},{102,6},{167,7},{104... | collective-permute-start | bytes 172040 | tf_op jit(solution)/shard_map/ppermute | solution.py:555
  44.0 1.3 %collective-permute-start.11 = (f32[112,128]{1,0:T(8,128)S(1)}, f32[112,128]{1,0:T(8,128)S(1)}, u32[]{:S(2)}, u32[]{:S(2)}) collective-permute-start(f32[112,128]{1,0:T(8,128)S(1)} %compare_select_fusion.2), channel_id=1, source_target_pairs={{1,0},{0,1},{3,2},{2,3},{5,4},{4,5},{7,6},{6,7},{9,8},{8,9},{11,10... | collective-permute-start | bytes 172040 | tf_op jit(solution)/shard_map/ppermute | solution.py:555
  45.4 5.5 %collective-permute-start.12 = (f32[112,128]{1,0:T(8,128)S(1)}, f32[112,128]{1,0:T(8,128)S(1)}, u32[]{:S(2)}, u32[]{:S(2)}) collective-permute-start(f32[112,128]{1,0:T(8,128)S(1)} %compare_select_fusion.1), channel_id=1, source_target_pairs={{4,0},{17,1},{6,2},{19,3},{0,4},{21,5},{2,6},{23,7},{12,8},{25,9},... | collective-permute-start | bytes 172040 | tf_op jit(solution)/shard_map/ppermute | solution.py:555
  45.5 11.1 %collective-permute-start.4 = (f32[10,64,128]{2,1,0:T(8,128)S(1)}, f32[10,64,128]{2,1,0:T(8,128)S(1)}, u32[]{:S(2)}, u32[]{:S(2)}) collective-permute-start(f32[10,64,128]{2,1,0:T(8,128)S(1)} %get-tuple-element.16), channel_id=1, source_target_pairs={{248,0},{0,8},{8,16},{16,24},{24,32},{32,40},{40,48},{48,56},{56,6... | collective-permute-start | bytes 983048 | tf_op jit(solution)/shard_map/ppermute | solution.py:545
  45.6 11.0 %collective-permute-start.5 = (f32[10,64,128]{2,1,0:T(8,128)S(1)}, f32[10,64,128]{2,1,0:T(8,128)S(1)}, u32[]{:S(2)}, u32[]{:S(2)}) collective-permute-start(f32[10,64,128]{2,1,0:T(8,128)S(1)} %get-tuple-element.17), channel_id=1, source_target_pairs={{8,0},{16,8},{24,16},{32,24},{40,32},{48,40},{56,48},{64,56},{72,6... | collective-permute-start | bytes 983048 | tf_op jit(solution)/shard_map/ppermute | solution.py:545
  50.9 11.5 %collective-permute-start.13 = (f32[112,128]{1,0:T(8,128)S(1)}, f32[112,128]{1,0:T(8,128)S(1)}, u32[]{:S(2)}, u32[]{:S(2)}) collective-permute-start(f32[112,128]{1,0:T(8,128)S(1)} %compare_select_fusion.mine), channel_id=1, source_target_pairs={{1,0},{0,1},{3,2},{2,3},{5,4},{4,5},{7,6},{6,7},{9,8},{8,9},{11,10... | collective-permute-start | bytes 172040 | tf_op jit(solution)/shard_map/ppermute | solution.py:555

commit v6 on v5

--- a/solution.py
+++ b/solution.py
@@ -126,7 +126,7 @@
 
 def sample_kernel(
     gain_hbm, pops_hbm, flags_hbm, cells_hbm, turb_hbm, chord_hbm, blade_hbm,
-    sibling, across, east, west, pops,
+    sibling, across, paired, unpaired, pops,
     vhm, vl, sel, fld, m128, r128, got_ref,
     gain, flags, cells, turb, chord, blade, sems, in_sems,
 ):
@@ -216,12 +216,14 @@
         held = [jnp.where(solid, g[OPP[i]], g[i]) for i in ids]
         return held + [rho, *mom, flag.astype(F32)]
 
-    for ids, x, out in ((EAST, CX - 1, east), (WEST, 0, west)):
-        for yb in range(CY // 8):
-            at = slice(yb * 8, yb * 8 + 8)
-            parts = pack(ids, [pops[i, x, at, :] for i in range(19)], flags[x, at, :])
-            for k, part in enumerate(parts):
-                out[k, at, :] = part
+    even_x = lax.axis_index("gx") % 2 == 0
+    for yb in range(CY // 8):
+        at = slice(yb * 8, yb * 8 + 8)
+        ahead = pack(EAST, [pops[i, CX - 1, at, :] for i in range(19)], flags[CX - 1, at, :])
+        back = pack(WEST, [pops[i, 0, at, :] for i in range(19)], flags[0, at, :])
+        for k, (a, b) in enumerate(zip(ahead, back)):
+            paired[k, at, :] = jnp.where(even_x, a, b)
+            unpaired[k, at, :] = jnp.where(even_x, b, a)
     up = pack(NORTH, [pops[i, :, CY - 1, :] for i in range(19)], flags[:, CY - 1, :])
     down = pack(SOUTH, [pops[i, :, 0, :] for i in range(19)], flags[:, 0, :])
     for k, (a, b) in enumerate(zip(up, down)):
@@ -426,7 +428,7 @@
 
 
 def step_kernel(
-    pops, flags, force, from_west, from_east, beside, beyond, west_pts, east_pts, *rest, low, high
+    pops, flags, force, paired, unpaired, beside, beyond, pair_pts, other_pts, *rest, low, high
 ):
     out_hbm, out, out_sems = rest[-3:]
     lane = lax.broadcasted_iota(jnp.int32, (8, LANES), 1)
@@ -449,7 +451,12 @@
     def force_at(x, yb):
         return [force[c, x + 1, yb * 8 + 1 : yb * 8 + 9, :] for c in range(3)]
 
-    for ids, x, src in ((EAST, low - 1, from_west), (WEST, high, from_east)):
+    even_x = lax.axis_index("gx") % 2 == 0
+
+    def from_side(west, pair, other):
+        return jnp.where(even_x, other, pair) if west else jnp.where(even_x, pair, other)
+
+    for ids, x in ((EAST, low - 1), (WEST, high)):
         for yb in range(CY // 8):
             at = slice(yb * 8, yb * 8 + 8)
             if 0 <= x < CX:
@@ -458,9 +465,10 @@
                 solid = flags[x, at, :] != 0
                 held = [jnp.where(solid, g[OPP[i]], g[i]) for i in ids]
             else:
-                rho, mom = src[5, at, :], [src[6 + c, at, :] for c in range(3)]
-                solid = src[9, at, :] != 0.0
-                held = [src[k, at, :] for k in range(5)]
+                part = [from_side(x < 0, paired[k, at, :], unpaired[k, at, :]) for k in range(10)]
+                rho, mom = part[5], part[6:9]
+                solid = part[9] != 0.0
+                held = part[:5]
             hit = Collision(rho, mom, force_at(x, yb))
             for val, i in zip(held, ids):
                 put(i, x, yb * 8, jnp.where(solid, val, KEEP * val + hit.one(i)))
@@ -487,17 +495,15 @@
                 else:
                     keep = (not_first if cz == 1 else not_last)[0:1]
                     pltpu.store(dst, val[x : x + 1], mask=keep)
-    for src, at, i, x, y in (
-        (west_pts, 112, 7, -1, -1),
-        (west_pts, 118, 9, -1, CY),
-        (east_pts, 124, 10, CX, -1),
-        (east_pts, 130, 8, CX, CY),
-    ):
+    for at, i, x, y in ((112, 7, -1, -1), (118, 9, -1, CY), (124, 10, CX, -1), (130, 8, CX, CY)):
         if not inside(x + DIRS[i][0]):
             continue
-        held, rho = src[at : at + 1, :], src[at + 1 : at + 2, :]
-        mom = [src[at + 2 + c : at + 3 + c, :] for c in range(3)]
-        solid = src[at + 5 : at + 6, :] != 0.0
+        part = [
+            from_side(x < 0, pair_pts[at + k : at + k + 1, :], other_pts[at + k : at + k + 1, :])
+            for k in range(6)
+        ]
+        held, rho, mom = part[0], part[1], part[2:5]
+        solid = part[5] != 0.0
         frc = [force[c, x + 1, y + 1 : y + 2, :] for c in range(3)]
         hit = Collision(rho, mom, frc)
         put(i, x, y, jnp.where(solid, held, KEEP * held + hit.one(i)))
@@ -540,11 +546,6 @@
         send(x).wait()
 
 
-def from_behind(block, axis, distance):
-    count = lax.axis_size(axis)
-    return lax.ppermute(block, axis, [((i - distance) % count, i) for i in range(count)])
-
-
 def exchanged(block, source):
     count_x, count_y = lax.axis_size("gx"), lax.axis_size("gy")
     pairs = []
@@ -559,10 +560,11 @@
     return exchanged(block, lambda x, y: (x, y ^ 1))
 
 
-def fetched(block, first, second):
-    return exchanged(
-        block, lambda x, y: (x + (second if y % 2 else first)[0], y + (second if y % 2 else first)[1])
-    )
+def along_z(block, distance):
+    def source(x, y):
+        return x + 4 * distance * (1 if (x // 4 + y) % 2 == 0 else -1), y
+
+    return exchanged(block, source)
 
 
 def cost(flops):
@@ -582,7 +584,7 @@
         pltpu.VMEM((LANES, LANES), F32),
         pltpu.VMEM((LANES, LANES), F32),
     ]
-    sibling, across, east, west, held_pops = pl.pallas_call(
+    sibling, across, paired, unpaired, held_pops = pl.pallas_call(
         sample_kernel,
         out_shape=(
             sds((192, LANES), F32),
@@ -620,8 +622,8 @@
     )
     beside = swapped(sibling)
     beyond = exchanged(across, lambda x, y: (x, y + 1 if y % 2 else y - 1))
-    from_west = from_behind(east, "gx", 1)
-    from_east = from_behind(west, "gx", -1)
+    paired = exchanged(paired, lambda x, y: (x ^ 1, y))
+    unpaired = exchanged(unpaired, lambda x, y: (x + 1 if x % 2 else x - 1, y))
     joined = pl.pallas_call(
         join_kernel,
         out_shape=sds((136, LANES), F32),
@@ -630,10 +632,10 @@
         compiler_params=light,
         name="join",
     )(sibling, beside, beyond)
-    west_pts = from_behind(joined, "gx", 1)
-    east_pts = from_behind(joined, "gx", -1)
+    pair_pts = exchanged(joined, lambda x, y: (x ^ 1, y))
+    other_pts = exchanged(joined, lambda x, y: (x + 1 if x % 2 else x - 1, y))
     other_half = exchanged(joined, lambda x, y: (x, y + 4))
-    near = known(joined[:112], known(west_pts[:112], east_pts[:112]))
+    near = known(joined[:112], known(pair_pts[:112], other_pts[:112]))
     prepared = pl.pallas_call(
         functools.partial(prep_kernel, total_x=total_x, total_y=total_y),
         out_shape=(
@@ -659,7 +661,7 @@
         name="force",
     )(*prepared, near)
     step_args = (
-        held_pops, solid_flags, force, from_west, from_east, beside, beyond, west_pts, east_pts,
+        held_pops, solid_flags, force, paired, unpaired, beside, beyond, pair_pts, other_pts,
     )
     read = None
     for low, high in ((0, CX // 2), (CX // 2, CX)):
@@ -680,10 +682,10 @@
     have = known(near, other_half[:112])
     got = swapped(have)
     have = known(have, got)
-    got = fetched(have, (4, 0), (-4, 0))
+    got = along_z(have, 1)
     have = known(have, got)
     have = known(have, swapped(have))
-    got = fetched(have, (12, 0), (-12, 0))
+    got = along_z(have, 3)
     have = known(have, got)
     have = known(have, swapped(have))
     got = exchanged(

time: 63.5 us -> 61.4 us (0.967)
  waiting for transfers between devices: 27.2 us -> 25.8 us
    ppermute x4 -> x0, starting transfers between devices: 13.6 us -> none  [from_behind(): lax.ppermute(block, axis, [((i - distance) % count, i) for i in range(cou...]
    ppermute x10 -> x14, starting transfers between devices: 7.8 us -> 21.1 us  [exchanged(): return lax.ppermute(block, ('gx', 'gy'), pairs)]
    ppermute x4 -> x0, waiting for transfers between devices: 8.33 us -> none  [from_behind(): lax.ppermute(block, axis, [((i - distance) % count, i) for i in range(cou...]
    ppermute x10 -> x14, waiting for transfers between devices: 18.9 us -> 25.8 us  [exchanged(): return lax.ppermute(block, ('gx', 'gy'), pairs)]
  transfers between devices with their start and end apart: 14 -> 14, of which waited for: 11 -> 12; matrix products, arithmetic and copies ran while one was open for 0% -> 0% of each run, Pallas kernels for 13% -> 13%
where the time goes in v6:
time: 61.4 us; the launch traced here: 61.3 us
  waiting for transfers between devices  25.8 us (42%)
  starting transfers between devices  21.1 us (34%)
  Pallas kernels  13.6 us (22%)
  between operations  0.74 us (1%)
    ppermute x14, waiting for transfers between devices, exchanged(): return lax.ppermute(block, ('gx', 'gy'), pairs)  25.8 us
    ppermute x14, starting transfers between devices, exchanged(): return lax.ppermute(block, ('gx', 'gy'), pairs)  21.1 us
    pallas_call x2, Pallas kernels, local(): pl.pallas_call(functools.partial(step_kernel, low=low, high=high), out_sh...  5.79 us
    pallas_call x1, Pallas kernels, local(): pl.pallas_call(sample_kernel, out_shape=(sds((192, LANES), F32), sds((192...  5 us
  transfers between devices with their start and end apart: 14, of which 12 were waited for; matrix products, arithmetic and copies ran while one was open for 0% of the time, Pallas kernels for 13%

profile of v6, /device:TPU:1, one launch (start us, length us, event | category | flops | bytes accessed | tf_op | source)
XLA Modules:
  0.0 61.3 jit_solution(13054408643651347202)
XLA Ops:
  0.7 5.0 %sample.1 = (f32[192,128]{1,0:T(8,128)S(1)}, f32[192,128]{1,0:T(8,128)S(1)}, f32[10,64,128]{2,1,0:T(8,128)S(1)}, f32[10,64,128]{2,1,0:T(8,128)S(1)}, f32[19,8,64,128]{3,2,1,0:T(8,128)S(1)}) custom-call(f32[24]{0:T(128)} %gain_hbm.1, f32[19,8,64,128]{3,2,1,0:T(8,128)} %pops_hbm.1, s32[8,64,128]{2,1,0:T(8,128)} %flags.3, s32[3,4608]{1,0:T(4,128)} %cells.1, ...), custom_call_target="tpu_custom_call" | custom-call | tf_op jit(solution)/shard_map/sample/pallas_call | solution.py:587
  5.7 3.3 %collective-permute-start = (f32[192,128]{1,0:T(8,128)S(1)}, f32[192,128]{1,0:T(8,128)S(1)}, u32[]{:S(2)}, u32[]{:S(2)}) collective-permute-start(f32[192,128]{1,0:T(8,128)S(1)} %get-tuple-element.14.own), channel_id=1, source_target_pairs={{1,0},{0,1},{3,2},{2,3},{5,4},{4,5},{7,6},{6,7},{9,8},{8,9},{11,10... | collective-permute-start | bytes 294920 | tf_op jit(solution)/shard_map/ppermute | solution.py:556
  9.0 0.9 %collective-permute-done.beside = f32[192,128]{1,0:T(8,128)S(1)} collective-permute-done((f32[192,128]{1,0:T(8,128)S(1)}, f32[192,128]{1,0:T(8,128)S(1)}, u32[]{:S(2)}, u32[]{:S(2)}) %collective-permute-start) | collective-permute-done | bytes 98336 | tf_op jit(solution)/shard_map/ppermute | solution.py:556
  9.9 3.4 %collective-permute-done.1.beyond = f32[192,128]{1,0:T(8,128)S(1)} collective-permute-done((f32[192,128]{1,0:T(8,128)S(1)}, f32[192,128]{1,0:T(8,128)S(1)}, u32[]{:S(2)}, u32[]{:S(2)}) %collective-permute-start.1) | collective-permute-done | bytes 98336 | tf_op jit(solution)/shard_map/ppermute | solution.py:556
  13.4 8.8 %collective-permute-start.3 = (f32[136,128]{1,0:T(8,128)S(1)}, f32[136,128]{1,0:T(8,128)S(1)}, u32[]{:S(2)}, u32[]{:S(2)}) collective-permute-start(f32[136,128]{1,0:T(8,128)S(1)} %join.1), channel_id=1, source_target_pairs={{248,0},{249,1},{250,2},{251,3},{252,4},{253,5},{254,6},{255,7},{1... | collective-permute-start | bytes 208904 | tf_op jit(solution)/shard_map/ppermute | solution.py:556
  22.2 2.2 %collective-permute-done.3.other_pts = f32[136,128]{1,0:T(8,128)S(1)} collective-permute-done((f32[136,128]{1,0:T(8,128)S(1)}, f32[136,128]{1,0:T(8,128)S(1)}, u32[]{:S(2)}, u32[]{:S(2)}) %collective-permute-start.3) | collective-permute-done | bytes 69664 | tf_op jit(solution)/shard_map/ppermute | solution.py:556
  24.3 1.0 %collective-permute-done.2.pair_pts = f32[136,128]{1,0:T(8,128)S(1)} collective-permute-done((f32[136,128]{1,0:T(8,128)S(1)}, f32[136,128]{1,0:T(8,128)S(1)}, u32[]{:S(2)}, u32[]{:S(2)}) %collective-permute-start.2) | collective-permute-done | bytes 69664 | tf_op jit(solution)/shard_map/ppermute | solution.py:556
  25.4 1.9 %collective-permute-start.7 = (f32[112,128]{1,0:T(8,128)S(1)}, f32[112,128]{1,0:T(8,128)S(1)}, u32[]{:S(2)}, u32[]{:S(2)}) collective-permute-start(f32[112,128]{1,0:T(8,128)S(1)} %get-tuple-element.18), channel_id=1, source_target_pairs={{1,0},{0,1},{3,2},{2,3},{5,4},{4,5},{7,6},{6,7},{9,8},{8,9},{11,10... | collective-permute-start | bytes 172040 | tf_op jit(solution)/shard_map/ppermute | solution.py:556
  27.2 0.9 %collective-permute-done.7 = f32[112,128]{1,0:T(8,128)S(1)} collective-permute-done((f32[112,128]{1,0:T(8,128)S(1)}, f32[112,128]{1,0:T(8,128)S(1)}, u32[]{:S(2)}, u32[]{:S(2)}) %collective-permute-start.7) | collective-permute-done | bytes 57376 | tf_op jit(solution)/shard_map/ppermute | solution.py:556
  28.2 4.2 %collective-permute-done.8 = f32[112,128]{1,0:T(8,128)S(1)} collective-permute-done((f32[112,128]{1,0:T(8,128)S(1)}, f32[112,128]{1,0:T(8,128)S(1)}, u32[]{:S(2)}, u32[]{:S(2)}) %collective-permute-start.8) | collective-permute-done | bytes 57376 | tf_op jit(solution)/shard_map/ppermute | solution.py:556
  32.9 0.9 %collective-permute-done.9 = f32[112,128]{1,0:T(8,128)S(1)} collective-permute-done((f32[112,128]{1,0:T(8,128)S(1)}, f32[112,128]{1,0:T(8,128)S(1)}, u32[]{:S(2)}, u32[]{:S(2)}) %collective-permute-start.9) | collective-permute-done | bytes 57376 | tf_op jit(solution)/shard_map/ppermute | solution.py:556
  34.1 5.8 %collective-permute-done.10 = f32[112,128]{1,0:T(8,128)S(1)} collective-permute-done((f32[112,128]{1,0:T(8,128)S(1)}, f32[112,128]{1,0:T(8,128)S(1)}, u32[]{:S(2)}, u32[]{:S(2)}) %collective-permute-start.10) | collective-permute-done | bytes 57376 | tf_op jit(solution)/shard_map/ppermute | solution.py:556
  39.9 0.8 %collective-permute-start.11 = (f32[112,128]{1,0:T(8,128)S(1)}, f32[112,128]{1,0:T(8,128)S(1)}, u32[]{:S(2)}, u32[]{:S(2)}) collective-permute-start(f32[112,128]{1,0:T(8,128)S(1)} %compare_select_fusion.2), channel_id=1, source_target_pairs={{1,0},{0,1},{3,2},{2,3},{5,4},{4,5},{7,6},{6,7},{9,8},{8,9},{11,10... | collective-permute-start | bytes 172040 | tf_op jit(solution)/shard_map/ppermute | solution.py:556
  40.7 0.9 %collective-permute-done.11 = f32[112,128]{1,0:T(8,128)S(1)} collective-permute-done((f32[112,128]{1,0:T(8,128)S(1)}, f32[112,128]{1,0:T(8,128)S(1)}, u32[]{:S(2)}, u32[]{:S(2)}) %collective-permute-start.11) | collective-permute-done | bytes 57376 | tf_op jit(solution)/shard_map/ppermute | solution.py:556
  41.6 1.3 %collective-permute-start.4 = (f32[10,64,128]{2,1,0:T(8,128)S(1)}, f32[10,64,128]{2,1,0:T(8,128)S(1)}, u32[]{:S(2)}, u32[]{:S(2)}) collective-permute-start(f32[10,64,128]{2,1,0:T(8,128)S(1)} %get-tuple-element.16), channel_id=1, source_target_pairs={{8,0},{9,1},{10,2},{11,3},{12,4},{13,5},{14,6},{15,7},{0,8},{1,9},... | collective-permute-start | bytes 983048 | tf_op jit(solution)/shard_map/ppermute | solution.py:556
  42.9 2.6 %collective-permute-start.5 = (f32[10,64,128]{2,1,0:T(8,128)S(1)}, f32[10,64,128]{2,1,0:T(8,128)S(1)}, u32[]{:S(2)}, u32[]{:S(2)}) collective-permute-start(f32[10,64,128]{2,1,0:T(8,128)S(1)} %get-tuple-element.17), channel_id=1, source_target_pairs={{248,0},{249,1},{250,2},{251,3},{252,4},{253,5},{254,6},{255,7},{1... | collective-permute-start | bytes 983048 | tf_op jit(solution)/shard_map/ppermute | solution.py:556
  45.5 0.7 %collective-permute-done.12 = f32[112,128]{1,0:T(8,128)S(1)} collective-permute-done((f32[112,128]{1,0:T(8,128)S(1)}, f32[112,128]{1,0:T(8,128)S(1)}, u32[]{:S(2)}, u32[]{:S(2)}) %collective-permute-start.12) | collective-permute-done | bytes 57376 | tf_op jit(solution)/shard_map/ppermute | solution.py:556
  46.2 1.6 %collective-permute-start.13 = (f32[112,128]{1,0:T(8,128)S(1)}, f32[112,128]{1,0:T(8,128)S(1)}, u32[]{:S(2)}, u32[]{:S(2)}) collective-permute-start(f32[112,128]{1,0:T(8,128)S(1)} %compare_select_fusion.mine), channel_id=1, source_target_pairs={{1,0},{0,1},{3,2},{2,3},{5,4},{4,5},{7,6},{6,7},{9,8},{8,9},{11,10... | collective-permute-start | bytes 172040 | tf_op jit(solution)/shard_map/ppermute | solution.py:556
  47.8 1.0 %prep.1 = (f32[5,8,256]{2,1,0:T(8,128)S(1)}, f32[128,128]{1,0:T(8,128)S(1)}, f32[8,4608]{1,0:T(8,128)S(1)}) custom-call(s32[3,4608]{1,0:T(4,128)S(1)} %copy-done.1), custom_call_target="tpu_custom_call" | custom-call | flops 40000000 | tf_op jit(solution)/shard_map/prep/pallas_call | solution.py:639
  48.8 1.1 %force.1 = f32[3,10,72,128]{3,2,1,0:T(8,128)S(1)} custom-call(f32[5,8,256]{2,1,0:T(8,128)S(1)} %get-tuple-element.11.spot_in, f32[128,128]{1,0:T(8,128)S(1)} %get-tuple-element.12.rank, f32[8,4608]{1,0:T(8,128)S(1)} %get-tuple-element.13.places, f32[112,128]{1,0:T(8,128)S(1)} %get-tuple-element.19.points_in), custom_call_target="tpu_custom_call" | custom-call | flops 40000000 | tf_op jit(solution)/shard_map/force/pallas_call | solution.py:653
  50.1 4.8 %collective-permute-done.5.unpaired = f32[10,64,128]{2,1,0:T(8,128)S(1)} collective-permute-done((f32[10,64,128]{2,1,0:T(8,128)S(1)}, f32[10,64,128]{2,1,0:T(8,128)S(1)}, u32[]{:S(2)}, u32[]{:S(2)}) %collective-permute-start.5) | collective-permute-done | bytes 327712 | tf_op jit(solution)/shard_map/ppermute | solution.py:556
  54.8 2.9 %shard_map.86.rest_0_ = f32[19,8,64,128]{3,2,1,0:T(8,128)} custom-call(f32[19,8,64,128]{3,2,1,0:T(8,128)S(1)} %get-tuple-element.10.pops, s32[8,64,128]{2,1,0:T(8,128)S(1)} %copy-done, f32[3,10,72,128]{3,2,1,0:T(8,128)S(1)} %force.1, f32[10,64,128]{2,1,0:T(8,128)S(1)} %collective-permute-done.4.paired, f32[10,64,128]{2,1,0:T(8,128)S(1)} %collective-permute-done.5.unpaired, ...), custom_call_target="tpu_custom_call" | custom-call | flops 60000000 | tf_op jit(solution)/shard_map/pallas_call | solution.py:669
  57.7 2.9 %shard_map.87 = f32[19,8,64,128]{3,2,1,0:T(8,128)} custom-call(f32[19,8,64,128]{3,2,1,0:T(8,128)S(1)} %get-tuple-element.10.pops, s32[8,64,128]{2,1,0:T(8,128)S(1)} %copy-done, f32[3,10,72,128]{3,2,1,0:T(8,128)S(1)} %force.1, f32[10,64,128]{2,1,0:T(8,128)S(1)} %collective-permute-done.4.paired, ...), custom_call_target="tpu_custom_call", output_to_operand_aliasing={{}: (9, {})} | custom-call | flops 60000000 | tf_op jit(solution)/shard_map/pallas_call | solution.py:669
  60.7 0.7 %finish.1 = f32[3,4608]{1,0:T(4,128)} custom-call(f32[112,128]{1,0:T(8,128)S(1)} %compare_select_fusion.mine, f32[112,128]{1,0:T(8,128)S(1)} %collective-permute-done.13.other), custom_call_target="tpu_custom_call" | custom-call | tf_op jit(solution)/shard_map/finish/pallas_call | solution.py:695
  (22 shorter events, 1.1 us)
Async XLA Ops:
  0.6 54.2 %copy-start = (s32[8,64,128]{2,1,0:T(8,128)S(1)}, s32[8,64,128]{2,1,0:T(8,128)}, u32[]{:S(2)}) copy-start(s32[8,64,128]{2,1,0:T(8,128)} %flags.3) | copy-start | bytes 786436
  0.6 47.2 %copy-start.1 = (s32[3,4608]{1,0:T(4,128)S(1)}, s32[3,4608]{1,0:T(4,128)}, u32[]{:S(2)}) copy-start(s32[3,4608]{1,0:T(4,128)} %cells.1) | copy-start | bytes 165892
  5.7 4.2 %collective-permute-start = (f32[192,128]{1,0:T(8,128)S(1)}, f32[192,128]{1,0:T(8,128)S(1)}, u32[]{:S(2)}, u32[]{:S(2)}) collective-permute-start(f32[192,128]{1,0:T(8,128)S(1)} %get-tuple-element.14.own), channel_id=1, source_target_pairs={{1,0},{0,1},{3,2},{2,3},{5,4},{4,5},{7,6},{6,7},{9,8},{8,9},{11,10... | collective-permute-start | bytes 294920 | tf_op jit(solution)/shard_map/ppermute | solution.py:556
  9.0 4.3 %collective-permute-start.1 = (f32[192,128]{1,0:T(8,128)S(1)}, f32[192,128]{1,0:T(8,128)S(1)}, u32[]{:S(2)}, u32[]{:S(2)}) collective-permute-start(f32[192,128]{1,0:T(8,128)S(1)} %get-tuple-element.15), channel_id=1, source_target_pairs={{7,0},{2,1},{1,2},{4,3},{3,4},{6,5},{5,6},{0,7},{15,8},{10,9},{9,1... | collective-permute-start | bytes 294920 | tf_op jit(solution)/shard_map/ppermute | solution.py:556
  13.3 8.9 %collective-permute-start.6 = (f32[136,128]{1,0:T(8,128)S(1)}, f32[136,128]{1,0:T(8,128)S(1)}, u32[]{:S(2)}, u32[]{:S(2)}) collective-permute-start(f32[136,128]{1,0:T(8,128)S(1)} %join.1), channel_id=1, source_target_pairs={{4,0},{5,1},{6,2},{7,3},{0,4},{1,5},{2,6},{3,7},{12,8},{13,9},{14,... | collective-permute-start | bytes 208904 | tf_op jit(solution)/shard_map/ppermute | solution.py:556
  13.4 10.9 %collective-permute-start.3 = (f32[136,128]{1,0:T(8,128)S(1)}, f32[136,128]{1,0:T(8,128)S(1)}, u32[]{:S(2)}, u32[]{:S(2)}) collective-permute-start(f32[136,128]{1,0:T(8,128)S(1)} %join.1), channel_id=1, source_target_pairs={{248,0},{249,1},{250,2},{251,3},{252,4},{253,5},{254,6},{255,7},{1... | collective-permute-start | bytes 208904 | tf_op jit(solution)/shard_map/ppermute | solution.py:556
  22.2 3.2 %collective-permute-start.2 = (f32[136,128]{1,0:T(8,128)S(1)}, f32[136,128]{1,0:T(8,128)S(1)}, u32[]{:S(2)}, u32[]{:S(2)}) collective-permute-start(f32[136,128]{1,0:T(8,128)S(1)} %join.1), channel_id=1, source_target_pairs={{8,0},{9,1},{10,2},{11,3},{12,4},{13,5},{14,6},{15,7},{0,8},{1,9},... | collective-permute-start | bytes 208904 | tf_op jit(solution)/shard_map/ppermute | solution.py:556
  25.4 2.8 %collective-permute-start.7 = (f32[112,128]{1,0:T(8,128)S(1)}, f32[112,128]{1,0:T(8,128)S(1)}, u32[]{:S(2)}, u32[]{:S(2)}) collective-permute-start(f32[112,128]{1,0:T(8,128)S(1)} %get-tuple-element.18), channel_id=1, source_target_pairs={{1,0},{0,1},{3,2},{2,3},{5,4},{4,5},{7,6},{6,7},{9,8},{8,9},{11,10... | collective-permute-start | bytes 172040 | tf_op jit(solution)/shard_map/ppermute | solution.py:556
  28.1 4.3 %collective-permute-start.8 = (f32[112,128]{1,0:T(8,128)S(1)}, f32[112,128]{1,0:T(8,128)S(1)}, u32[]{:S(2)}, u32[]{:S(2)}) collective-permute-start(f32[112,128]{1,0:T(8,128)S(1)} %compare_select_fusion.5), channel_id=1, source_target_pairs={{32,0},{225,1},{34,2},{227,3},{36,4},{229,5},{38,6},{231,7},{40,8}... | collective-permute-start | bytes 172040 | tf_op jit(solution)/shard_map/ppermute | solution.py:556
  32.4 1.3 %collective-permute-start.9 = (f32[112,128]{1,0:T(8,128)S(1)}, f32[112,128]{1,0:T(8,128)S(1)}, u32[]{:S(2)}, u32[]{:S(2)}) collective-permute-start(f32[112,128]{1,0:T(8,128)S(1)} %compare_select_fusion.4), channel_id=1, source_target_pairs={{1,0},{0,1},{3,2},{2,3},{5,4},{4,5},{7,6},{6,7},{9,8},{8,9},{11,10... | collective-permute-start | bytes 172040 | tf_op jit(solution)/shard_map/ppermute | solution.py:556
  33.8 6.1 %collective-permute-start.10 = (f32[112,128]{1,0:T(8,128)S(1)}, f32[112,128]{1,0:T(8,128)S(1)}, u32[]{:S(2)}, u32[]{:S(2)}) collective-permute-start(f32[112,128]{1,0:T(8,128)S(1)} %compare_select_fusion.3), channel_id=1, source_target_pairs={{96,0},{161,1},{98,2},{163,3},{100,4},{165,5},{102,6},{167,7},{104... | collective-permute-start | bytes 172040 | tf_op jit(solution)/shard_map/ppermute | solution.py:556
  39.9 1.7 %collective-permute-start.11 = (f32[112,128]{1,0:T(8,128)S(1)}, f32[112,128]{1,0:T(8,128)S(1)}, u32[]{:S(2)}, u32[]{:S(2)}) collective-permute-start(f32[112,128]{1,0:T(8,128)S(1)} %compare_select_fusion.2), channel_id=1, source_target_pairs={{1,0},{0,1},{3,2},{2,3},{5,4},{4,5},{7,6},{6,7},{9,8},{8,9},{11,10... | collective-permute-start | bytes 172040 | tf_op jit(solution)/shard_map/ppermute | solution.py:556
  41.6 4.6 %collective-permute-start.12 = (f32[112,128]{1,0:T(8,128)S(1)}, f32[112,128]{1,0:T(8,128)S(1)}, u32[]{:S(2)}, u32[]{:S(2)}) collective-permute-start(f32[112,128]{1,0:T(8,128)S(1)} %compare_select_fusion.1), channel_id=1, source_target_pairs={{4,0},{17,1},{6,2},{19,3},{0,4},{21,5},{2,6},{23,7},{12,8},{25,9},... | collective-permute-start | bytes 172040 | tf_op jit(solution)/shard_map/ppermute | solution.py:556
  41.6 8.4 %collective-permute-start.4 = (f32[10,64,128]{2,1,0:T(8,128)S(1)}, f32[10,64,128]{2,1,0:T(8,128)S(1)}, u32[]{:S(2)}, u32[]{:S(2)}) collective-permute-start(f32[10,64,128]{2,1,0:T(8,128)S(1)} %get-tuple-element.16), channel_id=1, source_target_pairs={{8,0},{9,1},{10,2},{11,3},{12,4},{13,5},{14,6},{15,7},{0,8},{1,9},... | collective-permute-start | bytes 983048 | tf_op jit(solution)/shard_map/ppermute | solution.py:556
  42.9 11.9 %collective-permute-start.5 = (f32[10,64,128]{2,1,0:T(8,128)S(1)}, f32[10,64,128]{2,1,0:T(8,128)S(1)}, u32[]{:S(2)}, u32[]{:S(2)}) collective-permute-start(f32[10,64,128]{2,1,0:T(8,128)S(1)} %get-tuple-element.17), channel_id=1, source_target_pairs={{248,0},{249,1},{250,2},{251,3},{252,4},{253,5},{254,6},{255,7},{1... | collective-permute-start | bytes 983048 | tf_op jit(solution)/shard_map/ppermute | solution.py:556
  46.2 14.5 %collective-permute-start.13 = (f32[112,128]{1,0:T(8,128)S(1)}, f32[112,128]{1,0:T(8,128)S(1)}, u32[]{:S(2)}, u32[]{:S(2)}) collective-permute-start(f32[112,128]{1,0:T(8,128)S(1)} %compare_select_fusion.mine), channel_id=1, source_target_pairs={{1,0},{0,1},{3,2},{2,3},{5,4},{4,5},{7,6},{6,7},{9,8},{8,9},{11,10... | collective-permute-start | bytes 172040 | tf_op jit(solution)/shard_map/ppermute | solution.py:556

commit v7 on v6

--- a/solution.py
+++ b/solution.py
@@ -660,12 +660,12 @@
         cost_estimate=cost(FORCE_FLOPS),
         name="force",
     )(*prepared, near)
-    step_args = (
-        held_pops, solid_flags, force, paired, unpaired, beside, beyond, pair_pts, other_pts,
-    )
+    step_args = (held_pops, solid_flags, force)
+    rest_args = (beside, beyond, pair_pts, other_pts)
     read = None
-    for low, high in ((0, CX // 2), (CX // 2, CX)):
+    for low, high in ((1, CX // 2 + 1), (CX // 2 + 1, CX), (0, 1)):
         extra = () if read is None else (read,)
+        halos = (paired, unpaired) if low == 0 or high == CX else (pair_pts, other_pts)
         read = pl.pallas_call(
             functools.partial(step_kernel, low=low, high=high),
             out_shape=sds(populations.shape, F32),
@@ -678,13 +678,14 @@
             input_output_aliases={9: 0} if extra else {},
             compiler_params=params,
             cost_estimate=cost(STEP_FLOPS),
-        )(*step_args, *extra)
+        )(*step_args, *halos, *rest_args, *extra)
     have = known(near, other_half[:112])
     got = swapped(have)
     have = known(have, got)
     got = along_z(have, 1)
     have = known(have, got)
-    have = known(have, swapped(have))
+    got = swapped(have)
+    have = known(have, got)
     got = along_z(have, 3)
     have = known(have, got)
     have = known(have, swapped(have))
@@ -692,6 +693,7 @@
         have, lambda x, y: (x // 4 * 4 + (x + 2) % 4, y) if y % 2 else (x, y + 4)
     )
     have = known(have, got)
+    last = swapped(have)
     point_force = pl.pallas_call(
         finish_kernel,
         out_shape=sds((3, points), F32),
@@ -699,7 +701,7 @@
         out_specs=VMEM,
         compiler_params=light,
         name="finish",
-    )(have, swapped(have))
+    )(have, last)
     return read, point_force
 
 

time: 61.4 us -> 59.8 us (0.974)
  waiting for transfers between devices: 25.8 us -> 22.8 us
  Pallas kernels: 13.6 us -> 15 us
    ppermute x14, waiting for transfers between devices: 25.8 us -> 22.8 us  [exchanged(): return lax.ppermute(block, ('gx', 'gy'), pairs)]
    pallas_call x2 -> x3, Pallas kernels: 5.79 us -> 7.14 us  [local(): pl.pallas_call(functools.partial(step_kernel, low=low, high=high), out_sh...]
  transfers between devices with their start and end apart: 14 -> 14, of which waited for: 12 -> 11; matrix products, arithmetic and copies ran while one was open for 0% -> 0% of each run, Pallas kernels for 13% -> 16%
where the time goes in v7:
time: 59.8 us; the launch traced here: 59.7 us
  waiting for transfers between devices  22.8 us (38%)
  starting transfers between devices  21.1 us (35%)
  Pallas kernels  15 us (25%)
  between operations  0.76 us (1%)
    ppermute x14, waiting for transfers between devices, exchanged(): return lax.ppermute(block, ('gx', 'gy'), pairs)  22.8 us
    ppermute x14, starting transfers between devices, exchanged(): return lax.ppermute(block, ('gx', 'gy'), pairs)  21.1 us
    pallas_call x3, Pallas kernels, local(): pl.pallas_call(functools.partial(step_kernel, low=low, high=high), out_sh...  7.14 us
    pallas_call x1, Pallas kernels, local(): pl.pallas_call(sample_kernel, out_shape=(sds((192, LANES), F32), sds((192...  5 us
  transfers between devices with their start and end apart: 14, of which 11 were waited for; matrix products, arithmetic and copies ran while one was open for 0% of the time, Pallas kernels for 16%

profile of v7, /device:TPU:1, one launch (start us, length us, event | category | flops | bytes accessed | tf_op | source)
XLA Modules:
  0.0 59.7 jit_solution(7162440871720571641)
XLA Ops:
  0.7 5.0 %sample.1 = (f32[192,128]{1,0:T(8,128)S(1)}, f32[192,128]{1,0:T(8,128)S(1)}, f32[10,64,128]{2,1,0:T(8,128)S(1)}, f32[10,64,128]{2,1,0:T(8,128)S(1)}, f32[19,8,64,128]{3,2,1,0:T(8,128)S(1)}) custom-call(f32[24]{0:T(128)} %gain_hbm.1, f32[19,8,64,128]{3,2,1,0:T(8,128)} %pops_hbm.1, s32[8,64,128]{2,1,0:T(8,128)} %flags.5, s32[3,4608]{1,0:T(4,128)} %cells.1, ...), custom_call_target="tpu_custom_call" | custom-call | tf_op jit(solution)/shard_map/sample/pallas_call | solution.py:587
  5.7 3.3 %collective-permute-start = (f32[192,128]{1,0:T(8,128)S(1)}, f32[192,128]{1,0:T(8,128)S(1)}, u32[]{:S(2)}, u32[]{:S(2)}) collective-permute-start(f32[192,128]{1,0:T(8,128)S(1)} %get-tuple-element.14.own), channel_id=1, source_target_pairs={{1,0},{0,1},{3,2},{2,3},{5,4},{4,5},{7,6},{6,7},{9,8},{8,9},{11,10... | collective-permute-start | bytes 294920 | tf_op jit(solution)/shard_map/ppermute | solution.py:556
  9.0 0.9 %collective-permute-done.beside = f32[192,128]{1,0:T(8,128)S(1)} collective-permute-done((f32[192,128]{1,0:T(8,128)S(1)}, f32[192,128]{1,0:T(8,128)S(1)}, u32[]{:S(2)}, u32[]{:S(2)}) %collective-permute-start) | collective-permute-done | bytes 98336 | tf_op jit(solution)/shard_map/ppermute | solution.py:556
  9.9 3.4 %collective-permute-done.1.beyond = f32[192,128]{1,0:T(8,128)S(1)} collective-permute-done((f32[192,128]{1,0:T(8,128)S(1)}, f32[192,128]{1,0:T(8,128)S(1)}, u32[]{:S(2)}, u32[]{:S(2)}) %collective-permute-start.1) | collective-permute-done | bytes 98336 | tf_op jit(solution)/shard_map/ppermute | solution.py:556
  13.4 8.8 %collective-permute-start.3 = (f32[136,128]{1,0:T(8,128)S(1)}, f32[136,128]{1,0:T(8,128)S(1)}, u32[]{:S(2)}, u32[]{:S(2)}) collective-permute-start(f32[136,128]{1,0:T(8,128)S(1)} %join.1), channel_id=1, source_target_pairs={{248,0},{249,1},{250,2},{251,3},{252,4},{253,5},{254,6},{255,7},{1... | collective-permute-start | bytes 208904 | tf_op jit(solution)/shard_map/ppermute | solution.py:556
  22.2 2.2 %collective-permute-done.3.unpaired.other_pts = f32[136,128]{1,0:T(8,128)S(1)} collective-permute-done((f32[136,128]{1,0:T(8,128)S(1)}, f32[136,128]{1,0:T(8,128)S(1)}, u32[]{:S(2)}, u32[]{:S(2)}) %collective-permute-start.3) | collective-permute-done | bytes 69664 | tf_op jit(solution)/shard_map/ppermute | solution.py:556
  24.4 1.0 %collective-permute-done.2.paired.pair_pts = f32[136,128]{1,0:T(8,128)S(1)} collective-permute-done((f32[136,128]{1,0:T(8,128)S(1)}, f32[136,128]{1,0:T(8,128)S(1)}, u32[]{:S(2)}, u32[]{:S(2)}) %collective-permute-start.2) | collective-permute-done | bytes 69664 | tf_op jit(solution)/shard_map/ppermute | solution.py:556
  25.4 1.9 %collective-permute-start.7 = (f32[112,128]{1,0:T(8,128)S(1)}, f32[112,128]{1,0:T(8,128)S(1)}, u32[]{:S(2)}, u32[]{:S(2)}) collective-permute-start(f32[112,128]{1,0:T(8,128)S(1)} %get-tuple-element.18), channel_id=1, source_target_pairs={{1,0},{0,1},{3,2},{2,3},{5,4},{4,5},{7,6},{6,7},{9,8},{8,9},{11,10... | collective-permute-start | bytes 172040 | tf_op jit(solution)/shard_map/ppermute | solution.py:556
  27.3 0.9 %collective-permute-done.7 = f32[112,128]{1,0:T(8,128)S(1)} collective-permute-done((f32[112,128]{1,0:T(8,128)S(1)}, f32[112,128]{1,0:T(8,128)S(1)}, u32[]{:S(2)}, u32[]{:S(2)}) %collective-permute-start.7) | collective-permute-done | bytes 57376 | tf_op jit(solution)/shard_map/ppermute | solution.py:556
  28.2 4.2 %collective-permute-done.8 = f32[112,128]{1,0:T(8,128)S(1)} collective-permute-done((f32[112,128]{1,0:T(8,128)S(1)}, f32[112,128]{1,0:T(8,128)S(1)}, u32[]{:S(2)}, u32[]{:S(2)}) %collective-permute-start.8) | collective-permute-done | bytes 57376 | tf_op jit(solution)/shard_map/ppermute | solution.py:556
  32.9 0.9 %collective-permute-done.9 = f32[112,128]{1,0:T(8,128)S(1)} collective-permute-done((f32[112,128]{1,0:T(8,128)S(1)}, f32[112,128]{1,0:T(8,128)S(1)}, u32[]{:S(2)}, u32[]{:S(2)}) %collective-permute-start.9) | collective-permute-done | bytes 57376 | tf_op jit(solution)/shard_map/ppermute | solution.py:556
  34.1 5.8 %collective-permute-done.10 = f32[112,128]{1,0:T(8,128)S(1)} collective-permute-done((f32[112,128]{1,0:T(8,128)S(1)}, f32[112,128]{1,0:T(8,128)S(1)}, u32[]{:S(2)}, u32[]{:S(2)}) %collective-permute-start.10) | collective-permute-done | bytes 57376 | tf_op jit(solution)/shard_map/ppermute | solution.py:556
  39.9 0.8 %collective-permute-start.11 = (f32[112,128]{1,0:T(8,128)S(1)}, f32[112,128]{1,0:T(8,128)S(1)}, u32[]{:S(2)}, u32[]{:S(2)}) collective-permute-start(f32[112,128]{1,0:T(8,128)S(1)} %compare_select_fusion.2), channel_id=1, source_target_pairs={{1,0},{0,1},{3,2},{2,3},{5,4},{4,5},{7,6},{6,7},{9,8},{8,9},{11,10... | collective-permute-start | bytes 172040 | tf_op jit(solution)/shard_map/ppermute | solution.py:556
  40.7 0.9 %collective-permute-done.11 = f32[112,128]{1,0:T(8,128)S(1)} collective-permute-done((f32[112,128]{1,0:T(8,128)S(1)}, f32[112,128]{1,0:T(8,128)S(1)}, u32[]{:S(2)}, u32[]{:S(2)}) %collective-permute-start.11) | collective-permute-done | bytes 57376 | tf_op jit(solution)/shard_map/ppermute | solution.py:556
  41.6 1.3 %collective-permute-start.4 = (f32[10,64,128]{2,1,0:T(8,128)S(1)}, f32[10,64,128]{2,1,0:T(8,128)S(1)}, u32[]{:S(2)}, u32[]{:S(2)}) collective-permute-start(f32[10,64,128]{2,1,0:T(8,128)S(1)} %get-tuple-element.16), channel_id=1, source_target_pairs={{8,0},{9,1},{10,2},{11,3},{12,4},{13,5},{14,6},{15,7},{0,8},{1,9},... | collective-permute-start | bytes 983048 | tf_op jit(solution)/shard_map/ppermute | solution.py:556
  42.9 2.6 %collective-permute-start.5 = (f32[10,64,128]{2,1,0:T(8,128)S(1)}, f32[10,64,128]{2,1,0:T(8,128)S(1)}, u32[]{:S(2)}, u32[]{:S(2)}) collective-permute-start(f32[10,64,128]{2,1,0:T(8,128)S(1)} %get-tuple-element.17), channel_id=1, source_target_pairs={{248,0},{249,1},{250,2},{251,3},{252,4},{253,5},{254,6},{255,7},{1... | collective-permute-start | bytes 983048 | tf_op jit(solution)/shard_map/ppermute | solution.py:556
  45.5 0.7 %collective-permute-done.12 = f32[112,128]{1,0:T(8,128)S(1)} collective-permute-done((f32[112,128]{1,0:T(8,128)S(1)}, f32[112,128]{1,0:T(8,128)S(1)}, u32[]{:S(2)}, u32[]{:S(2)}) %collective-permute-start.12) | collective-permute-done | bytes 57376 | tf_op jit(solution)/shard_map/ppermute | solution.py:556
  46.2 1.6 %collective-permute-start.13 = (f32[112,128]{1,0:T(8,128)S(1)}, f32[112,128]{1,0:T(8,128)S(1)}, u32[]{:S(2)}, u32[]{:S(2)}) collective-permute-start(f32[112,128]{1,0:T(8,128)S(1)} %compare_select_fusion.mine), channel_id=1, source_target_pairs={{1,0},{0,1},{3,2},{2,3},{5,4},{4,5},{7,6},{6,7},{9,8},{8,9},{11,10... | collective-permute-start | bytes 172040 | tf_op jit(solution)/shard_map/ppermute | solution.py:556
  47.8 1.0 %prep.1 = (f32[5,8,256]{2,1,0:T(8,128)S(1)}, f32[128,128]{1,0:T(8,128)S(1)}, f32[8,4608]{1,0:T(8,128)S(1)}) custom-call(s32[3,4608]{1,0:T(4,128)S(1)} %copy-done.1), custom_call_target="tpu_custom_call" | custom-call | flops 40000000 | tf_op jit(solution)/shard_map/prep/pallas_call | solution.py:639
  48.9 1.1 %force.1 = f32[3,10,72,128]{3,2,1,0:T(8,128)S(1)} custom-call(f32[5,8,256]{2,1,0:T(8,128)S(1)} %get-tuple-element.11.spot_in, f32[128,128]{1,0:T(8,128)S(1)} %get-tuple-element.12.rank, f32[8,4608]{1,0:T(8,128)S(1)} %get-tuple-element.13.places, f32[112,128]{1,0:T(8,128)S(1)} %get-tuple-element.19.points_in), custom_call_target="tpu_custom_call" | custom-call | flops 40000000 | tf_op jit(solution)/shard_map/force/pallas_call | solution.py:653
  50.0 3.0 %shard_map.86.rest_0_ = f32[19,8,64,128]{3,2,1,0:T(8,128)} custom-call(f32[19,8,64,128]{3,2,1,0:T(8,128)S(1)} %get-tuple-element.10.pops, s32[8,64,128]{2,1,0:T(8,128)S(1)} %copy-done, f32[3,10,72,128]{3,2,1,0:T(8,128)S(1)} %force.1, f32[136,128]{1,0:T(8,128)S(1)} %collective-permute-done.2.paired.pair_pts, ...), custom_call_target="tpu_custom_call" | custom-call | flops 60000000 | tf_op jit(solution)/shard_map/pallas_call | solution.py:669
  53.0 1.9 %collective-permute-done.5.unpaired = f32[10,64,128]{2,1,0:T(8,128)S(1)} collective-permute-done((f32[10,64,128]{2,1,0:T(8,128)S(1)}, f32[10,64,128]{2,1,0:T(8,128)S(1)}, u32[]{:S(2)}, u32[]{:S(2)}) %collective-permute-start.5) | collective-permute-done | bytes 327712 | tf_op jit(solution)/shard_map/ppermute | solution.py:556
  54.8 2.6 %shard_map.87.rest_0_ = f32[19,8,64,128]{3,2,1,0:T(8,128)} custom-call(f32[19,8,64,128]{3,2,1,0:T(8,128)S(1)} %get-tuple-element.10.pops, s32[8,64,128]{2,1,0:T(8,128)S(1)} %copy-done, f32[3,10,72,128]{3,2,1,0:T(8,128)S(1)} %force.1, f32[10,64,128]{2,1,0:T(8,128)S(1)} %collective-permute-done.4.paired, ...), custom_call_target="tpu_custom_call", output_to_operand_aliasing={{}: (9, {})} | custom-call | flops 60000000 | tf_op jit(solution)/shard_map/pallas_call | solution.py:669
  57.4 1.6 %shard_map.88 = f32[19,8,64,128]{3,2,1,0:T(8,128)} custom-call(f32[19,8,64,128]{3,2,1,0:T(8,128)S(1)} %get-tuple-element.10.pops, s32[8,64,128]{2,1,0:T(8,128)S(1)} %copy-done, f32[3,10,72,128]{3,2,1,0:T(8,128)S(1)} %force.1, f32[10,64,128]{2,1,0:T(8,128)S(1)} %collective-permute-done.4.paired, ...), custom_call_target="tpu_custom_call", output_to_operand_aliasing={{}: (9, {})} | custom-call | flops 60000000 | tf_op jit(solution)/shard_map/pallas_call | solution.py:669
  (23 shorter events, 1.7 us)
Async XLA Ops:
  0.6 49.3 %copy-start = (s32[8,64,128]{2,1,0:T(8,128)S(1)}, s32[8,64,128]{2,1,0:T(8,128)}, u32[]{:S(2)}) copy-start(s32[8,64,128]{2,1,0:T(8,128)} %flags.5) | copy-start | bytes 786436
  0.6 47.2 %copy-start.1 = (s32[3,4608]{1,0:T(4,128)S(1)}, s32[3,4608]{1,0:T(4,128)}, u32[]{:S(2)}) copy-start(s32[3,4608]{1,0:T(4,128)} %cells.1) | copy-start | bytes 165892
  5.7 4.2 %collective-permute-start = (f32[192,128]{1,0:T(8,128)S(1)}, f32[192,128]{1,0:T(8,128)S(1)}, u32[]{:S(2)}, u32[]{:S(2)}) collective-permute-start(f32[192,128]{1,0:T(8,128)S(1)} %get-tuple-element.14.own), channel_id=1, source_target_pairs={{1,0},{0,1},{3,2},{2,3},{5,4},{4,5},{7,6},{6,7},{9,8},{8,9},{11,10... | collective-permute-start | bytes 294920 | tf_op jit(solution)/shard_map/ppermute | solution.py:556
  9.0 4.3 %collective-permute-start.1 = (f32[192,128]{1,0:T(8,128)S(1)}, f32[192,128]{1,0:T(8,128)S(1)}, u32[]{:S(2)}, u32[]{:S(2)}) collective-permute-start(f32[192,128]{1,0:T(8,128)S(1)} %get-tuple-element.15), channel_id=1, source_target_pairs={{7,0},{2,1},{1,2},{4,3},{3,4},{6,5},{5,6},{0,7},{15,8},{10,9},{9,1... | collective-permute-start | bytes 294920 | tf_op jit(solution)/shard_map/ppermute | solution.py:556
  13.3 8.9 %collective-permute-start.6 = (f32[136,128]{1,0:T(8,128)S(1)}, f32[136,128]{1,0:T(8,128)S(1)}, u32[]{:S(2)}, u32[]{:S(2)}) collective-permute-start(f32[136,128]{1,0:T(8,128)S(1)} %join.1), channel_id=1, source_target_pairs={{4,0},{5,1},{6,2},{7,3},{0,4},{1,5},{2,6},{3,7},{12,8},{13,9},{14,... | collective-permute-start | bytes 208904 | tf_op jit(solution)/shard_map/ppermute | solution.py:556
  13.4 10.9 %collective-permute-start.3 = (f32[136,128]{1,0:T(8,128)S(1)}, f32[136,128]{1,0:T(8,128)S(1)}, u32[]{:S(2)}, u32[]{:S(2)}) collective-permute-start(f32[136,128]{1,0:T(8,128)S(1)} %join.1), channel_id=1, source_target_pairs={{248,0},{249,1},{250,2},{251,3},{252,4},{253,5},{254,6},{255,7},{1... | collective-permute-start | bytes 208904 | tf_op jit(solution)/shard_map/ppermute | solution.py:556
  22.2 3.2 %collective-permute-start.2 = (f32[136,128]{1,0:T(8,128)S(1)}, f32[136,128]{1,0:T(8,128)S(1)}, u32[]{:S(2)}, u32[]{:S(2)}) collective-permute-start(f32[136,128]{1,0:T(8,128)S(1)} %join.1), channel_id=1, source_target_pairs={{8,0},{9,1},{10,2},{11,3},{12,4},{13,5},{14,6},{15,7},{0,8},{1,9},... | collective-permute-start | bytes 208904 | tf_op jit(solution)/shard_map/ppermute | solution.py:556
  25.4 2.8 %collective-permute-start.7 = (f32[112,128]{1,0:T(8,128)S(1)}, f32[112,128]{1,0:T(8,128)S(1)}, u32[]{:S(2)}, u32[]{:S(2)}) collective-permute-start(f32[112,128]{1,0:T(8,128)S(1)} %get-tuple-element.18), channel_id=1, source_target_pairs={{1,0},{0,1},{3,2},{2,3},{5,4},{4,5},{7,6},{6,7},{9,8},{8,9},{11,10... | collective-permute-start | bytes 172040 | tf_op jit(solution)/shard_map/ppermute | solution.py:556
  28.2 4.3 %collective-permute-start.8 = (f32[112,128]{1,0:T(8,128)S(1)}, f32[112,128]{1,0:T(8,128)S(1)}, u32[]{:S(2)}, u32[]{:S(2)}) collective-permute-start(f32[112,128]{1,0:T(8,128)S(1)} %compare_select_fusion.5), channel_id=1, source_target_pairs={{32,0},{225,1},{34,2},{227,3},{36,4},{229,5},{38,6},{231,7},{40,8}... | collective-permute-start | bytes 172040 | tf_op jit(solution)/shard_map/ppermute | solution.py:556
  32.4 1.3 %collective-permute-start.9 = (f32[112,128]{1,0:T(8,128)S(1)}, f32[112,128]{1,0:T(8,128)S(1)}, u32[]{:S(2)}, u32[]{:S(2)}) collective-permute-start(f32[112,128]{1,0:T(8,128)S(1)} %compare_select_fusion.4), channel_id=1, source_target_pairs={{1,0},{0,1},{3,2},{2,3},{5,4},{4,5},{7,6},{6,7},{9,8},{8,9},{11,10... | collective-permute-start | bytes 172040 | tf_op jit(solution)/shard_map/ppermute | solution.py:556
  33.8 6.1 %collective-permute-start.10 = (f32[112,128]{1,0:T(8,128)S(1)}, f32[112,128]{1,0:T(8,128)S(1)}, u32[]{:S(2)}, u32[]{:S(2)}) collective-permute-start(f32[112,128]{1,0:T(8,128)S(1)} %compare_select_fusion.3), channel_id=1, source_target_pairs={{96,0},{161,1},{98,2},{163,3},{100,4},{165,5},{102,6},{167,7},{104... | collective-permute-start | bytes 172040 | tf_op jit(solution)/shard_map/ppermute | solution.py:556
  39.9 1.7 %collective-permute-start.11 = (f32[112,128]{1,0:T(8,128)S(1)}, f32[112,128]{1,0:T(8,128)S(1)}, u32[]{:S(2)}, u32[]{:S(2)}) collective-permute-start(f32[112,128]{1,0:T(8,128)S(1)} %compare_select_fusion.2), channel_id=1, source_target_pairs={{1,0},{0,1},{3,2},{2,3},{5,4},{4,5},{7,6},{6,7},{9,8},{8,9},{11,10... | collective-permute-start | bytes 172040 | tf_op jit(solution)/shard_map/ppermute | solution.py:556
  41.6 4.6 %collective-permute-start.12 = (f32[112,128]{1,0:T(8,128)S(1)}, f32[112,128]{1,0:T(8,128)S(1)}, u32[]{:S(2)}, u32[]{:S(2)}) collective-permute-start(f32[112,128]{1,0:T(8,128)S(1)} %compare_select_fusion.1), channel_id=1, source_target_pairs={{4,0},{17,1},{6,2},{19,3},{0,4},{21,5},{2,6},{23,7},{12,8},{25,9},... | collective-permute-start | bytes 172040 | tf_op jit(solution)/shard_map/ppermute | solution.py:556
  41.6 11.3 %collective-permute-start.4 = (f32[10,64,128]{2,1,0:T(8,128)S(1)}, f32[10,64,128]{2,1,0:T(8,128)S(1)}, u32[]{:S(2)}, u32[]{:S(2)}) collective-permute-start(f32[10,64,128]{2,1,0:T(8,128)S(1)} %get-tuple-element.16), channel_id=1, source_target_pairs={{8,0},{9,1},{10,2},{11,3},{12,4},{13,5},{14,6},{15,7},{0,8},{1,9},... | collective-permute-start | bytes 983048 | tf_op jit(solution)/shard_map/ppermute | solution.py:556
  42.9 11.9 %collective-permute-start.5 = (f32[10,64,128]{2,1,0:T(8,128)S(1)}, f32[10,64,128]{2,1,0:T(8,128)S(1)}, u32[]{:S(2)}, u32[]{:S(2)}) collective-permute-start(f32[10,64,128]{2,1,0:T(8,128)S(1)} %get-tuple-element.17), channel_id=1, source_target_pairs={{248,0},{249,1},{250,2},{251,3},{252,4},{253,5},{254,6},{255,7},{1... | collective-permute-start | bytes 983048 | tf_op jit(solution)/shard_map/ppermute | solution.py:556
  46.2 12.8 %collective-permute-start.13 = (f32[112,128]{1,0:T(8,128)S(1)}, f32[112,128]{1,0:T(8,128)S(1)}, u32[]{:S(2)}, u32[]{:S(2)}) collective-permute-start(f32[112,128]{1,0:T(8,128)S(1)} %compare_select_fusion.mine), channel_id=1, source_target_pairs={{1,0},{0,1},{3,2},{2,3},{5,4},{4,5},{7,6},{6,7},{9,8},{8,9},{11,10... | collective-permute-start | bytes 172040 | tf_op jit(solution)/shard_map/ppermute | solution.py:556
